TPU v7x, 512 devices: a whole 4x8x8 slice. The times are simulated.
512 devices in a mesh: hx: 4 (over y_hi), hy: 4 (over x), tok: 32 (over y_lo, z, core).
Axes of the slice: x: 4, y: 8 (y_hi: 4, y_lo: 2; y = y_hi * 2 + y_lo), z: 8, core: 2. Of those that a mesh axis runs over, the one named last changes fastest.
Arguments:
- stream_in: bfloat16 [8192, 4608], P('tok', ('hx', 'hy')), may hold values from -6 to 6
- before_gain: bfloat16 [4608], P(('hx', 'hy')), may hold values from 0.25 to 1.75
- after_gain: bfloat16 [4608], P(('hx', 'hy')), may hold values from 0.25 to 1.75
- feed_gain: bfloat16 [4608], P(('hx', 'hy')), may hold values from 0.25 to 1.75
- query_weight: bfloat16 [4608, 4096], P('tok', ('hx', 'hy')), may hold values from -1 to 1
- key_weight: bfloat16 [4608, 2048], P('tok', ('hx', 'hy')), may hold values from -64 to 64
- value_weight: bfloat16 [4608, 2048], P('tok', ('hx', 'hy')), may hold values from -0.09375 to 0.09375
- output_weight: bfloat16 [4096, 4608], P(('hx', 'hy'), 'tok'), may hold values from -0.09375 to 0.09375
- documents: int32 [8192], P('tok'), may hold values from 0 to 127, never falling along the last dimension, each value on 1 to 128 neighbouring positions
Outputs:
- residual: bfloat16 [8192, 4608], P('tok', ('hx', 'hy'))
- feed_input: bfloat16 [8192, 4608], P('tok', ('hx', 'hy'))
Inputs may be any that keep to these rules, and one draw needn't show every extreme that they name: `documents`: ids never fall along the tokens; a document holds at most 128 tokens and may run across a sequence's end.
All inputs are finite; a program needn't handle non-finite values.
Results may differ from a plain program's by a relative error of at most 0.014.
The roundings to bfloat16 on the way count: a program that leaves them out, or rounds other values in their place, can miss the bound.
Values may be sent and summed in bfloat16 or wider, within the bound.
No kernel may reach another device: no remote copies, remote signals or barrier semaphores. Data moves between devices by JAX's collectives and lax.ppermute only.
A program may use at most 64 MiB of HBM per device.

v0:
```python
import jax
import jax.numpy as jnp
from jax import lax
from jax.experimental import pallas as pl
from jax.experimental.pallas import tpu as pltpu
from jax.sharding import Mesh, PartitionSpec as P


D = 4608
QH = 32
HEAD = 128
LENGTH = 256
epsilon = 1e-06
neg_big = -1e30
BF, F32 = jnp.bfloat16, jnp.float32


def ring(n, s):
    return [(i, (i + s) % n) for i in range(n)]


def both_cores(x):
    return jnp.stack([x, lax.ppermute(x, "c", ring(2, 1))])


def z_pieces(own):
    def send(x, s):
        up_down = [((z, c), ((z + (s if c == 0 else -s)) % 8, c)) for z in range(8) for c in range(2)]
        return lax.ppermute(x, ("z", "c"), [(2 * a + b, 2 * d + e) for (a, b), (d, e) in up_down])

    one, two = send(own, 1), send(own, 2)
    three, four = send(two, 1), send(two[0], 2)
    near = [lax.ppermute(p, "c", ring(2, 1)) for p in (one, two)]
    far = [lax.ppermute(p, "c", ring(2, 1)) for p in (three, four)]
    return [own, one, two, three, four, *near, *far]


def exchanged(x, axis):
    return lax.all_to_all(x, axis, split_axis=0, concat_axis=0, tiled=True)


def norm_kernel(x, normed, first):
    per = 288
    acc = jnp.zeros((16, 256), F32)
    for p in range(16):
        for b in range(per // 16):
            w = x[p, b * 16 : (b + 1) * 16].astype(F32)
            acc = acc + w * w
    sq = jnp.sum(acc, axis=0, keepdims=True)
    first[...] = jnp.broadcast_to(sq, (8, 256))
    scale = lax.rsqrt(sq / D + epsilon)
    scale_col = jnp.transpose(jnp.broadcast_to(scale, (128, 256)), (1, 0))
    rows = []
    for p in range(16):
        rows += [x[p, per : per + 1].astype(F32), x[p, per + 1 : per + 2, :32].astype(F32)]
    gain = jnp.concatenate(rows, axis=1)
    for b in range(D // 128):
        cols = slice(b * 128, (b + 1) * 128)
        p, at = divmod(b * 128, per)
        if at + 128 <= per:
            block = x[p, at : at + 128]
        else:
            block = jnp.concatenate([x[p, at:per], x[p + 1, : at + 128 - per]], axis=0)
        turned = jnp.transpose(block.astype(F32), (1, 0))
        normed[:, cols] = (turned * scale_col * gain[:, cols]).astype(BF)


STEPS = ((0, 0), (1, 0), (2, 0), (3, 0), (4, 0), (1, 1), (2, 1), (3, 1), (4, 1))


def blocks(pos):
    yl, z, c = pos[0], pos[1], pos[2]
    for k, (far, swapped) in enumerate(STEPS):
        holder = (c + swapped) % 2
        dz = jnp.where(holder == 0, 8 - far, far)
        for i in (0, 1) if far < 4 else (0,):
            for r in range(2):
                t = ((yl + r) % 2) * 8 + (z + dz) % 8
                yield k, (i if far < 4 else None), r, t, (holder + i) % 2


def attend_kernel(pos, normed, cos, sin, mask, *refs):
    pieces, (out, w, o, sems) = refs[:9], refs[9:]
    for k, i, r, t, core in blocks(pos):
        w[t, core] = pieces[k][r] if i is None else pieces[k][i, r]
    acc = jnp.dot(normed[...], w[...].reshape(D, 512), preferred_element_type=F32)
    cv, sv = cos[...], sin[...]

    def rotate(u):
        a, b = u[:, :64], u[:, 64:]
        return jnp.concatenate([a * cv - b * sv, b * cv + a * sv], axis=1)

    keys = rotate(acc[:, 256:384]).astype(BF)
    values = acc[:, 384:512].astype(BF)
    allowed = mask[...] > 0.0
    for h in range(2):
        q = (rotate(acc[:, h * 128 : (h + 1) * 128]) * (D / QH) ** (-0.5)).astype(BF)
        scores = lax.dot_general(
            q, keys, (((1,), (1,)), ((), ())), preferred_element_type=F32
        )
        best = jnp.max(jnp.where(allowed, scores, neg_big), axis=1, keepdims=True)
        weights = jnp.where(allowed, jnp.exp(scores - best), 0.0)
        total = jnp.sum(weights, axis=1, keepdims=True)
        summed = jnp.dot(weights.astype(BF), values, preferred_element_type=F32)
        o[:, h * 128 : (h + 1) * 128] = (summed / total).astype(BF)
    moves = [pltpu.make_async_copy(o, out.at[i], sems.at[i]) for i in range(16)]
    for m in moves:
        m.start()
    for m in moves:
        m.wait()


def output_kernel(pos, x, gain, att, *refs):
    pieces, (mixed, sums, rows, att_v, *held, w_sems, sems) = refs[:9], refs[9:]
    w_moves = [pltpu.make_async_copy(p, h, w_sems.at[k]) for k, (p, h) in enumerate(zip(pieces, held))]
    moves = [pltpu.make_async_copy(att.at[g], att_v.at[g], sems.at[g]) for g in range(16)]
    for m in w_moves + moves:
        m.start()
    for m in w_moves + moves:
        m.wait()
    for k, i, r, t, core in blocks(pos):
        rows[t, core] = held[k][r] if i is None else held[k][i, r]
    total = jnp.zeros((288, 256), F32)
    for g in range(16):
        term = lax.dot_general(
            rows[g].reshape(288, 256), att_v[g], (((1,), (1,)), ((), ())), preferred_element_type=F32
        )
        total = total + term.astype(BF).astype(F32)
    mixed[...] = total
    branch = total * gain[...]
    wide = x[...].astype(F32)
    parts = [jnp.sum(u, axis=0, keepdims=True) for u in (total * total, wide * branch, branch * branch)]
    stacked = jnp.concatenate(parts + [jnp.zeros((5, 256), F32)], axis=0)
    for i in range(16):
        sums[i] = stacked


ANY = pl.BlockSpec(memory_space=pl.ANY)
VMEM = pl.BlockSpec(memory_space=pltpu.VMEM)
SMEM = pl.BlockSpec(memory_space=pltpu.SMEM)


def params(mib):
    return pltpu.CompilerParams(vmem_limit_bytes=mib << 20)


def per_device(
    stream_in,
    before_gain,
    after_gain,
    feed_gain,
    query_weight,
    key_weight,
    value_weight,
    output_weight,
    documents,
):
    hid = ("hx", "hy")
    pos = jnp.stack([lax.axis_index(a) for a in ("yl", "z", "c")]).astype(jnp.int32)
    rows = LENGTH

    w = jnp.concatenate([query_weight, key_weight, value_weight], axis=1)
    w_pair = lax.ppermute(w, "yl", ring(2, 1))
    w_pieces = z_pieces(both_cores(jnp.stack([w, w_pair])))

    x_t = stream_in.T
    gain_rows = jnp.pad(before_gain, (0, 8 * 256 - 288)).reshape(8, 256)
    packed = jnp.concatenate([x_t, gain_rows], axis=0)
    stream = exchanged(jnp.broadcast_to(packed, (16, *packed.shape)), hid)
    normed, first = pl.pallas_call(
        norm_kernel,
        out_shape=(
            jax.ShapeDtypeStruct((rows, D), BF),
            jax.ShapeDtypeStruct((8, rows), F32),
        ),
        in_specs=[VMEM],
        out_specs=(VMEM, VMEM),
        compiler_params=params(16),
        name="norm_stream",
    )(stream)

    def turned(flip):
        turn = [
            ((a * 16 + b) * 2 + k, (b * 16 + (a ^ flip)) * 2 + k)
            for a in range(16)
            for b in range(16)
            for k in range(2)
        ]
        return lax.ppermute(output_weight.T, ("hx", "hy", "yl", "z", "c"), turn)

    wo = jnp.stack([turned(0), turned(8)])
    wo_pieces = z_pieces(both_cores(wo))

    half_width = HEAD // 2
    frequency = 10000.0 ** (-jnp.arange(half_width, dtype=F32) / half_width)
    angles = (jnp.arange(rows, dtype=jnp.int32) % LENGTH).astype(F32)[:, None] * frequency[None, :]
    index = jnp.arange(rows)
    mask = (
        (index[None, :] <= index[:, None]) & (documents[None, :] == documents[:, None])
    ).astype(F32)
    attended = pl.pallas_call(
        attend_kernel,
        out_shape=jax.ShapeDtypeStruct((16, rows, 256), BF),
        in_specs=[SMEM] + [VMEM] * 13,
        out_specs=ANY,
        scratch_shapes=[
            pltpu.VMEM((16, 2, 144, 512), BF),
            pltpu.VMEM((rows, 256), BF),
            pltpu.SemaphoreType.DMA((16,)),
        ],
        compiler_params=params(24),
        name="attend",
    )(pos, normed, jnp.cos(angles), jnp.sin(angles), mask, *w_pieces)

    gathered = exchanged(attended, hid)
    after_col = after_gain.astype(F32)[:, None]
    feed_col = feed_gain.astype(F32)[:, None]
    mixed, sums = pl.pallas_call(
        output_kernel,
        out_shape=(
            jax.ShapeDtypeStruct((288, rows), F32),
            jax.ShapeDtypeStruct((16, 8, rows), F32),
        ),
        in_specs=[SMEM, VMEM, VMEM] + [ANY] * 10,
        out_specs=(VMEM, VMEM),
        scratch_shapes=[
            pltpu.VMEM((16, 2, 144, 256), BF),
            pltpu.VMEM((16, rows, 256), BF),
            *[pltpu.VMEM(p.shape, BF) for p in wo_pieces],
            pltpu.SemaphoreType.DMA((9,)),
            pltpu.SemaphoreType.DMA((16,)),
        ],
        compiler_params=params(56),
        name="project_out",
    )(pos, x_t, after_col, gathered, *wo_pieces)

    sums = exchanged(sums, hid).sum(axis=0)
    after_sq, cross_sum, branch_sq = sums[0:1], sums[1:2], sums[2:3]
    first_sq = first[0:1]
    after_scale = lax.rsqrt(after_sq / D + epsilon)
    wide = x_t.astype(F32)
    residual = (wide + mixed * after_scale * after_col).astype(BF)
    feed_sq = first_sq + 2.0 * after_scale * cross_sum + after_scale * after_scale * branch_sq
    feed_scale = lax.rsqrt(feed_sq / D + epsilon)
    feed_input = (residual.astype(F32) * feed_scale * feed_col).astype(BF)
    return (residual.T, feed_input.T)


def solution(mesh):
    fine = Mesh(mesh.devices.reshape(4, 4, 2, 8, 2), ("hx", "hy", "yl", "z", "c"))
    hid, tok = ("hx", "hy"), ("yl", "z", "c")
    in_specs = (
        P(tok, hid),
        P(hid),
        P(hid),
        P(hid),
        P(tok, hid),
        P(tok, hid),
        P(tok, hid),
        P(hid, tok),
        P(tok),
    )
    out_specs = (P(tok, hid), P(tok, hid))

    return jax.shard_map(per_device, mesh=fine, in_specs=in_specs, out_specs=out_specs, check_vma=False)
```

profile of v0, /device:TPU:8, one launch (start us, length us, event | category | flops | bytes accessed | tf_op | source)
XLA Modules:
  0.0 256.6 jit_solution(17523391129926587689)
XLA Ops:
  3.9 8.9 %all-to-all-start = ((bf16[16,296,256]{2,1,0:T(8,128)(2,1)}), bf16[16,296,256]{2,1,0:T(8,128)(2,1)S(1)}, u32[]{:S(2)}, u32[]{:S(2)}) async-start(bf16[16,296,256]{2,1,0:T(8,128)(2,1)} %broadcast_in_dim.5), calls=%async_computation | async-start | bytes 4849664 | tf_op jit(solution)/shard_map/all_to_all | solution.py:39
  12.9 3.3 %collective-permute-start = (bf16[144,512]{1,0:T(8,128)(2,1)S(1)}, bf16[144,512]{1,0:T(8,128)(2,1)S(1)}, u32[]{:S(2)}, u32[]{:S(2)}) collective-permute-start(bf16[144,512]{1,0:T(8,128)(2,1)S(1)} %constant_dynamic-update-slice_fusion), channel_id=1, source_target_pairs={{0,16},{16,0},{1,17},{17,1},{2,18},{18,2},{3,19},{19,3},{4,20},{20... | collective-permute-start | bytes 442376 | tf_op jit(solution)/shard_map/ppermute | solution.py:163
  16.1 53.4 %collective-permute-done = bf16[144,512]{1,0:T(8,128)(2,1)S(1)} collective-permute-done((bf16[144,512]{1,0:T(8,128)(2,1)S(1)}, bf16[144,512]{1,0:T(8,128)(2,1)S(1)}, u32[]{:S(2)}, u32[]{:S(2)}) %collective-permute-start) | collective-permute-done | bytes 147488 | tf_op jit(solution)/shard_map/ppermute | solution.py:163
  73.1 6.1 %collective-permute-start.3 = (bf16[2,2,144,512]{3,2,1,0:T(8,128)(2,1)S(1)}, bf16[2,2,144,512]{3,2,1,0:T(8,128)(2,1)}, u32[]{:S(2)}, u32[]{:S(2)}) collective-permute-start(bf16[2,2,144,512]{3,2,1,0:T(8,128)(2,1)S(1)} %pad_maximum_fusion.refs_0_), channel_id=1, source_target_pairs={{0,4},{1,13},{2,6},{3,15},{4,8},{5,1},{6,10},{7,3},{8,12},{9,5},{1... | collective-permute-start | bytes 1769480 | tf_op jit(solution)/shard_map/ppermute | solution.py:29
  79.2 4.3 %collective-permute-start.2 = (bf16[2,2,144,512]{3,2,1,0:T(8,128)(2,1)S(1)}, bf16[2,2,144,512]{3,2,1,0:T(8,128)(2,1)}, u32[]{:S(2)}, u32[]{:S(2)}) collective-permute-start(bf16[2,2,144,512]{3,2,1,0:T(8,128)(2,1)S(1)} %pad_maximum_fusion.refs_0_), channel_id=1, source_target_pairs={{0,2},{1,15},{2,4},{3,1},{4,6},{5,3},{6,8},{7,5},{8,10},{9,7},{10,... | collective-permute-start | bytes 1769480 | tf_op jit(solution)/shard_map/ppermute | solution.py:29
  83.5 8.7 %collective-permute-done.3.refs_2_ = bf16[2,2,144,512]{3,2,1,0:T(8,128)(2,1)} collective-permute-done((bf16[2,2,144,512]{3,2,1,0:T(8,128)(2,1)S(1)}, bf16[2,2,144,512]{3,2,1,0:T(8,128)(2,1)}, u32[]{:S(2)}, u32[]{:S(2)}) %collective-permute-start.3) | collective-permute-done | bytes 589856 | tf_op jit(solution)/shard_map/ppermute | solution.py:29
  92.1 9.6 %collective-permute-start.4 = (bf16[2,2,144,512]{3,2,1,0:T(8,128)(2,1)}, bf16[2,2,144,512]{3,2,1,0:T(8,128)(2,1)}, u32[]{:S(2)}, u32[]{:S(2)}) collective-permute-start(bf16[2,2,144,512]{3,2,1,0:T(8,128)(2,1)} %collective-permute-done.3.refs_2_), channel_id=1, source_target_pairs={{0,2},{1,15},{2,4},{3,1},{4,6},{5,3},{6,8},{7,5},{8,10},{9,7},{10,... | collective-permute-start | bytes 1769480 | tf_op jit(solution)/shard_map/ppermute | solution.py:29
  105.4 3.3 %collective-permute-start.7 = (bf16[2,2,144,512]{3,2,1,0:T(8,128)(2,1)}, bf16[2,2,144,512]{3,2,1,0:T(8,128)(2,1)}, u32[]{:S(2)}, u32[]{:S(2)}) collective-permute-start(bf16[2,2,144,512]{3,2,1,0:T(8,128)(2,1)} %collective-permute-done.3.refs_2_), channel_id=1, source_target_pairs={{0,1},{1,0},{2,3},{3,2},{4,5},{5,4},{6,7},{7,6},{8,9},{9,8},{10,11... | collective-permute-start | bytes 1769480 | tf_op jit(solution)/shard_map/ppermute | solution.py:33
  108.7 1.9 collective-permute-start.6
  111.0 2.1 collective-permute-start.8
  114.7 3.2 %collective-permute-start.9 = (bf16[2,144,512]{2,1,0:T(8,128)(2,1)}, bf16[2,144,512]{2,1,0:T(8,128)(2,1)}, u32[]{:S(2)}, u32[]{:S(2)}) collective-permute-start(bf16[2,144,512]{2,1,0:T(8,128)(2,1)} %collective-permute-done.5.refs_4_), channel_id=1, source_target_pairs={{0,1},{1,0},{2,3},{3,2},{4,5},{5,4},{6,7},{7,6},{8,9},{9,8},{10,11... | collective-permute-start | bytes 884744 | tf_op jit(solution)/shard_map/ppermute | solution.py:34
  119.5 5.9 %attend.1 = bf16[16,256,256]{2,1,0:T(8,128)(2,1)} custom-call(s32[3]{0:T(128)S(1)} %pad_add_fusion.pos, bf16[256,4608]{1,0:T(8,128)(2,1)S(1)} %get-tuple-element.6.normed, f32[256,64]{1,0:T(8,128)S(1)} %get-tuple-element.19.cos, f32[256,64]{1,0:T(8,128)S(1)} %get-tuple-element.18.sin, f32[256,256]{1,0:T(8,128)S(1)} %fusion.1.mask, ...), custom_call_target="tpu_custom_call" | custom-call | tf_op jit(solution)/shard_map/attend/pallas_call | solution.py:201
  125.4 9.1 %all-to-all-start.1 = ((bf16[16,256,256]{2,1,0:T(8,128)(2,1)}), bf16[16,256,256]{2,1,0:T(8,128)(2,1)S(1)}, u32[]{:S(2)}, u32[]{:S(2)}) async-start(bf16[16,256,256]{2,1,0:T(8,128)(2,1)} %attend.1), calls=%async_computation.1 | async-start | bytes 4194304 | tf_op jit(solution)/shard_map/all_to_all | solution.py:39
  134.5 7.6 %collective-permute-start.10 = (bf16[144,256]{1,0:T(8,128)(2,1)S(1)}, bf16[144,256]{1,0:T(8,128)(2,1)S(1)}, u32[]{:S(2)}, u32[]{:S(2)}) collective-permute-start(bf16[144,256]{1,0:T(8,128)(2,1)S(1)} %bitcast.37), channel_id=1, source_target_pairs={{0,0},{1,1},{2,32},{3,33},{4,64},{5,65},{6,96},{7,97},{8,128},{9,1... | collective-permute-start | bytes 221192 | tf_op jit(solution)/shard_map/ppermute | solution.py:189
  144.1 44.2 %collective-permute-done.10 = bf16[144,256]{1,0:T(8,128)(2,1)S(1)} collective-permute-done((bf16[144,256]{1,0:T(8,128)(2,1)S(1)}, bf16[144,256]{1,0:T(8,128)(2,1)S(1)}, u32[]{:S(2)}, u32[]{:S(2)}) %collective-permute-start.10) | collective-permute-done | bytes 73760 | tf_op jit(solution)/shard_map/ppermute | solution.py:189
  191.6 7.1 %collective-permute-start.14 = (bf16[2,2,144,256]{3,2,1,0:T(8,128)(2,1)S(1)}, bf16[2,2,144,256]{3,2,1,0:T(8,128)(2,1)S(1)}, u32[]{:S(2)}, u32[]{:S(2)}) collective-permute-start(bf16[2,2,144,256]{3,2,1,0:T(8,128)(2,1)S(1)} %pad_maximum_fusion.2.refs_0_), channel_id=1, source_target_pairs={{0,4},{1,13},{2,6},{3,15},{4,8},{5,1},{6,10},{7,3},{8,12},{9,5},{1... | collective-permute-start | bytes 884744 | tf_op jit(solution)/shard_map/ppermute | solution.py:29
  198.7 3.1 %collective-permute-start.13 = (bf16[2,2,144,256]{3,2,1,0:T(8,128)(2,1)S(1)}, bf16[2,2,144,256]{3,2,1,0:T(8,128)(2,1)S(1)}, u32[]{:S(2)}, u32[]{:S(2)}) collective-permute-start(bf16[2,2,144,256]{3,2,1,0:T(8,128)(2,1)S(1)} %pad_maximum_fusion.2.refs_0_), channel_id=1, source_target_pairs={{0,2},{1,15},{2,4},{3,1},{4,6},{5,3},{6,8},{7,5},{8,10},{9,7},{10,... | collective-permute-start | bytes 884744 | tf_op jit(solution)/shard_map/ppermute | solution.py:29
  201.8 7.6 %collective-permute-done.14.refs_2_ = bf16[2,2,144,256]{3,2,1,0:T(8,128)(2,1)S(1)} collective-permute-done((bf16[2,2,144,256]{3,2,1,0:T(8,128)(2,1)S(1)}, bf16[2,2,144,256]{3,2,1,0:T(8,128)(2,1)S(1)}, u32[]{:S(2)}, u32[]{:S(2)}) %collective-permute-start.14) | collective-permute-done | bytes 294944 | tf_op jit(solution)/shard_map/ppermute | solution.py:29
  211.3 3.9 %collective-permute-start.16 = (bf16[2,144,256]{2,1,0:T(8,128)(2,1)S(1)}, bf16[2,144,256]{2,1,0:T(8,128)(2,1)S(1)}, u32[]{:S(2)}, u32[]{:S(2)}) collective-permute-start(bf16[2,144,256]{2,1,0:T(8,128)(2,1)S(1)} %slice_bitcast_fusion.1), channel_id=1, source_target_pairs={{0,4},{1,13},{2,6},{3,15},{4,8},{5,1},{6,10},{7,3},{8,12},{9,5},{1... | collective-permute-start | bytes 442376 | tf_op jit(solution)/shard_map/ppermute | solution.py:29
  215.2 2.8 %collective-permute-start.18 = (bf16[2,2,144,256]{3,2,1,0:T(8,128)(2,1)S(1)}, bf16[2,2,144,256]{3,2,1,0:T(8,128)(2,1)S(1)}, u32[]{:S(2)}, u32[]{:S(2)}) collective-permute-start(bf16[2,2,144,256]{3,2,1,0:T(8,128)(2,1)S(1)} %collective-permute-done.14.refs_2_), channel_id=1, source_target_pairs={{0,1},{1,0},{2,3},{3,2},{4,5},{5,4},{6,7},{7,6},{8,9},{9,8},{10,11... | collective-permute-start | bytes 884744 | tf_op jit(solution)/shard_map/ppermute | solution.py:33
  220.0 2.4 collective-permute-start.19
  228.8 5.3 %project_out.1 = (f32[288,256]{1,0:T(8,128)}, f32[16,8,256]{2,1,0:T(8,128)}) custom-call(s32[3]{0:T(128)} %copy-done, bf16[288,256]{1,0:T(8,128)(2,1)} %bitcast.27, f32[288,1]{1,0:T(8,128)} %broadcast_in_dim.6.gain, bf16[16,256,256]{2,1,0:T(8,128)(2,1)} %copy-done.1, bf16[2,2,144,256]{3,2,1,0:T(8,128)(2,1)} %copy-done.3, bf16[2,2,144,256]{3,2,1,0:T(8,128)(2,1)} %copy-done.5, ...), custom_call_target="tpu_custom_call" | custom-call | tf_op jit(solution)/shard_map/project_out/pallas_call | solution.py:218
  234.1 10.0 %all-to-all-start.2 = ((f32[16,8,256]{2,1,0:T(8,128)}), f32[16,8,256]{2,1,0:T(8,128)S(1)}, u32[]{:S(2)}, u32[]{:S(2)}) async-start(f32[16,8,256]{2,1,0:T(8,128)} %get-tuple-element.8), calls=%async_computation.2 | async-start | bytes 262144 | tf_op jit(solution)/shard_map/all_to_all | solution.py:39
  244.2 10.6 %all-to-all-done.2 = f32[16,8,256]{2,1,0:T(8,128)S(1)} async-done(((f32[16,8,256]{2,1,0:T(8,128)}), f32[16,8,256]{2,1,0:T(8,128)S(1)}, u32[]{:S(2)}, u32[]{:S(2)}) %all-to-all-start.2) | async-done | bytes 131104 | tf_op jit(solution)/shard_map/all_to_all | solution.py:39
  (87 shorter events, 31.3 us)
Async XLA Ops:
  3.9 114.3 %all-to-all-start = ((bf16[16,296,256]{2,1,0:T(8,128)(2,1)}), bf16[16,296,256]{2,1,0:T(8,128)(2,1)S(1)}, u32[]{:S(2)}, u32[]{:S(2)}) async-start(bf16[16,296,256]{2,1,0:T(8,128)(2,1)} %broadcast_in_dim.5), calls=%async_computation | async-start | bytes 4849664 | tf_op jit(solution)/shard_map/all_to_all | solution.py:39
  12.9 56.6 %collective-permute-start = (bf16[144,512]{1,0:T(8,128)(2,1)S(1)}, bf16[144,512]{1,0:T(8,128)(2,1)S(1)}, u32[]{:S(2)}, u32[]{:S(2)}) collective-permute-start(bf16[144,512]{1,0:T(8,128)(2,1)S(1)} %constant_dynamic-update-slice_fusion), channel_id=1, source_target_pairs={{0,16},{16,0},{1,17},{17,1},{2,18},{18,2},{3,19},{19,3},{4,20},{20... | collective-permute-start | bytes 442376 | tf_op jit(solution)/shard_map/ppermute | solution.py:163
  69.5 3.5 %collective-permute-start.1 = (bf16[2,144,512]{2,1,0:T(8,128)(2,1)S(1)}, bf16[2,144,512]{2,1,0:T(8,128)(2,1)S(1)}, u32[]{:S(2)}, u32[]{:S(2)}) collective-permute-start(bf16[2,144,512]{2,1,0:T(8,128)(2,1)S(1)} %get-tuple-element.13), channel_id=1, source_target_pairs={{0,1},{1,0},{2,3},{3,2},{4,5},{5,4},{6,7},{7,6},{8,9},{9,8},{10,11... | collective-permute-start | bytes 884744 | tf_op jit(solution)/shard_map/ppermute | solution.py:23
  73.1 19.0 %collective-permute-start.3 = (bf16[2,2,144,512]{3,2,1,0:T(8,128)(2,1)S(1)}, bf16[2,2,144,512]{3,2,1,0:T(8,128)(2,1)}, u32[]{:S(2)}, u32[]{:S(2)}) collective-permute-start(bf16[2,2,144,512]{3,2,1,0:T(8,128)(2,1)S(1)} %pad_maximum_fusion.refs_0_), channel_id=1, source_target_pairs={{0,4},{1,13},{2,6},{3,15},{4,8},{5,1},{6,10},{7,3},{8,12},{9,5},{1... | collective-permute-start | bytes 1769480 | tf_op jit(solution)/shard_map/ppermute | solution.py:29
  79.2 29.5 %collective-permute-start.2 = (bf16[2,2,144,512]{3,2,1,0:T(8,128)(2,1)S(1)}, bf16[2,2,144,512]{3,2,1,0:T(8,128)(2,1)}, u32[]{:S(2)}, u32[]{:S(2)}) collective-permute-start(bf16[2,2,144,512]{3,2,1,0:T(8,128)(2,1)S(1)} %pad_maximum_fusion.refs_0_), channel_id=1, source_target_pairs={{0,2},{1,15},{2,4},{3,1},{4,6},{5,3},{6,8},{7,5},{8,10},{9,7},{10,... | collective-permute-start | bytes 1769480 | tf_op jit(solution)/shard_map/ppermute | solution.py:29
  92.1 18.9 %collective-permute-start.4 = (bf16[2,2,144,512]{3,2,1,0:T(8,128)(2,1)}, bf16[2,2,144,512]{3,2,1,0:T(8,128)(2,1)}, u32[]{:S(2)}, u32[]{:S(2)}) collective-permute-start(bf16[2,2,144,512]{3,2,1,0:T(8,128)(2,1)} %collective-permute-done.3.refs_2_), channel_id=1, source_target_pairs={{0,2},{1,15},{2,4},{3,1},{4,6},{5,3},{6,8},{7,5},{8,10},{9,7},{10,... | collective-permute-start | bytes 1769480 | tf_op jit(solution)/shard_map/ppermute | solution.py:29
  103.5 11.2 %collective-permute-start.5 = (bf16[2,144,512]{2,1,0:T(8,128)(2,1)}, bf16[2,144,512]{2,1,0:T(8,128)(2,1)}, u32[]{:S(2)}, u32[]{:S(2)}) collective-permute-start(bf16[2,144,512]{2,1,0:T(8,128)(2,1)} %slice_bitcast_fusion), channel_id=1, source_target_pairs={{0,4},{1,13},{2,6},{3,15},{4,8},{5,1},{6,10},{7,3},{8,12},{9,5},{1... | collective-permute-start | bytes 884744 | tf_op jit(solution)/shard_map/ppermute | solution.py:29
  105.4 14.1 %collective-permute-start.7 = (bf16[2,2,144,512]{3,2,1,0:T(8,128)(2,1)}, bf16[2,2,144,512]{3,2,1,0:T(8,128)(2,1)}, u32[]{:S(2)}, u32[]{:S(2)}) collective-permute-start(bf16[2,2,144,512]{3,2,1,0:T(8,128)(2,1)} %collective-permute-done.3.refs_2_), channel_id=1, source_target_pairs={{0,1},{1,0},{2,3},{3,2},{4,5},{5,4},{6,7},{7,6},{8,9},{9,8},{10,11... | collective-permute-start | bytes 1769480 | tf_op jit(solution)/shard_map/ppermute | solution.py:33
  108.7 10.8 %collective-permute-start.6 = (bf16[2,2,144,512]{3,2,1,0:T(8,128)(2,1)}, bf16[2,2,144,512]{3,2,1,0:T(8,128)(2,1)}, u32[]{:S(2)}, u32[]{:S(2)}) collective-permute-start(bf16[2,2,144,512]{3,2,1,0:T(8,128)(2,1)} %collective-permute-done.2.refs_1_), channel_id=1, source_target_pairs={{0,1},{1,0},{2,3},{3,2},{4,5},{5,4},{6,7},{7,6},{8,9},{9,8},{10,11... | collective-permute-start | bytes 1769480 | tf_op jit(solution)/shard_map/ppermute | solution.py:33
  111.0 8.5 %collective-permute-start.8 = (bf16[2,2,144,512]{3,2,1,0:T(8,128)(2,1)}, bf16[2,2,144,512]{3,2,1,0:T(8,128)(2,1)}, u32[]{:S(2)}, u32[]{:S(2)}) collective-permute-start(bf16[2,2,144,512]{3,2,1,0:T(8,128)(2,1)} %collective-permute-done.4.refs_3_), channel_id=1, source_target_pairs={{0,1},{1,0},{2,3},{3,2},{4,5},{5,4},{6,7},{7,6},{8,9},{9,8},{10,11... | collective-permute-start | bytes 1769480 | tf_op jit(solution)/shard_map/ppermute | solution.py:34
  114.7 4.8 %collective-permute-start.9 = (bf16[2,144,512]{2,1,0:T(8,128)(2,1)}, bf16[2,144,512]{2,1,0:T(8,128)(2,1)}, u32[]{:S(2)}, u32[]{:S(2)}) collective-permute-start(bf16[2,144,512]{2,1,0:T(8,128)(2,1)} %collective-permute-done.5.refs_4_), channel_id=1, source_target_pairs={{0,1},{1,0},{2,3},{3,2},{4,5},{5,4},{6,7},{7,6},{8,9},{9,8},{10,11... | collective-permute-start | bytes 884744 | tf_op jit(solution)/shard_map/ppermute | solution.py:34
  125.4 102.0 %all-to-all-start.1 = ((bf16[16,256,256]{2,1,0:T(8,128)(2,1)}), bf16[16,256,256]{2,1,0:T(8,128)(2,1)S(1)}, u32[]{:S(2)}, u32[]{:S(2)}) async-start(bf16[16,256,256]{2,1,0:T(8,128)(2,1)} %attend.1), calls=%async_computation.1 | async-start | bytes 4194304 | tf_op jit(solution)/shard_map/all_to_all | solution.py:39
  134.5 53.7 %collective-permute-start.10 = (bf16[144,256]{1,0:T(8,128)(2,1)S(1)}, bf16[144,256]{1,0:T(8,128)(2,1)S(1)}, u32[]{:S(2)}, u32[]{:S(2)}) collective-permute-start(bf16[144,256]{1,0:T(8,128)(2,1)S(1)} %bitcast.37), channel_id=1, source_target_pairs={{0,0},{1,1},{2,32},{3,33},{4,64},{5,65},{6,96},{7,97},{8,128},{9,1... | collective-permute-start | bytes 221192 | tf_op jit(solution)/shard_map/ppermute | solution.py:189
  142.1 46.1 %collective-permute-start.11 = (bf16[144,256]{1,0:T(8,128)(2,1)S(1)}, bf16[144,256]{1,0:T(8,128)(2,1)S(1)}, u32[]{:S(2)}, u32[]{:S(2)}) collective-permute-start(bf16[144,256]{1,0:T(8,128)(2,1)S(1)} %bitcast.38), channel_id=1, source_target_pairs={{0,16},{1,17},{2,48},{3,49},{4,80},{5,81},{6,112},{7,113},{8,144},... | collective-permute-start | bytes 221192 | tf_op jit(solution)/shard_map/ppermute | solution.py:189
  188.3 3.3 %collective-permute-start.12 = (bf16[2,144,256]{2,1,0:T(8,128)(2,1)S(1)}, bf16[2,144,256]{2,1,0:T(8,128)(2,1)S(1)}, u32[]{:S(2)}, u32[]{:S(2)}) collective-permute-start(bf16[2,144,256]{2,1,0:T(8,128)(2,1)S(1)} %get-tuple-element.15), channel_id=1, source_target_pairs={{0,1},{1,0},{2,3},{3,2},{4,5},{5,4},{6,7},{7,6},{8,9},{9,8},{10,11... | collective-permute-start | bytes 442376 | tf_op jit(solution)/shard_map/ppermute | solution.py:23
  191.6 17.8 %collective-permute-start.14 = (bf16[2,2,144,256]{3,2,1,0:T(8,128)(2,1)S(1)}, bf16[2,2,144,256]{3,2,1,0:T(8,128)(2,1)S(1)}, u32[]{:S(2)}, u32[]{:S(2)}) collective-permute-start(bf16[2,2,144,256]{3,2,1,0:T(8,128)(2,1)S(1)} %pad_maximum_fusion.2.refs_0_), channel_id=1, source_target_pairs={{0,4},{1,13},{2,6},{3,15},{4,8},{5,1},{6,10},{7,3},{8,12},{9,5},{1... | collective-permute-start | bytes 884744 | tf_op jit(solution)/shard_map/ppermute | solution.py:29
  198.7 19.4 %collective-permute-start.13 = (bf16[2,2,144,256]{3,2,1,0:T(8,128)(2,1)S(1)}, bf16[2,2,144,256]{3,2,1,0:T(8,128)(2,1)S(1)}, u32[]{:S(2)}, u32[]{:S(2)}) collective-permute-start(bf16[2,2,144,256]{3,2,1,0:T(8,128)(2,1)S(1)} %pad_maximum_fusion.2.refs_0_), channel_id=1, source_target_pairs={{0,2},{1,15},{2,4},{3,1},{4,6},{5,3},{6,8},{7,5},{8,10},{9,7},{10,... | collective-permute-start | bytes 884744 | tf_op jit(solution)/shard_map/ppermute | solution.py:29
  209.4 10.6 %collective-permute-start.15 = (bf16[2,2,144,256]{3,2,1,0:T(8,128)(2,1)S(1)}, bf16[2,2,144,256]{3,2,1,0:T(8,128)(2,1)S(1)}, u32[]{:S(2)}, u32[]{:S(2)}) collective-permute-start(bf16[2,2,144,256]{3,2,1,0:T(8,128)(2,1)S(1)} %collective-permute-done.14.refs_2_), channel_id=1, source_target_pairs={{0,2},{1,15},{2,4},{3,1},{4,6},{5,3},{6,8},{7,5},{8,10},{9,7},{10,... | collective-permute-start | bytes 884744 | tf_op jit(solution)/shard_map/ppermute | solution.py:29
  211.3 11.4 %collective-permute-start.16 = (bf16[2,144,256]{2,1,0:T(8,128)(2,1)S(1)}, bf16[2,144,256]{2,1,0:T(8,128)(2,1)S(1)}, u32[]{:S(2)}, u32[]{:S(2)}) collective-permute-start(bf16[2,144,256]{2,1,0:T(8,128)(2,1)S(1)} %slice_bitcast_fusion.1), channel_id=1, source_target_pairs={{0,4},{1,13},{2,6},{3,15},{4,8},{5,1},{6,10},{7,3},{8,12},{9,5},{1... | collective-permute-start | bytes 442376 | tf_op jit(solution)/shard_map/ppermute | solution.py:29
  215.2 10.8 %collective-permute-start.18 = (bf16[2,2,144,256]{3,2,1,0:T(8,128)(2,1)S(1)}, bf16[2,2,144,256]{3,2,1,0:T(8,128)(2,1)S(1)}, u32[]{:S(2)}, u32[]{:S(2)}) collective-permute-start(bf16[2,2,144,256]{3,2,1,0:T(8,128)(2,1)S(1)} %collective-permute-done.14.refs_2_), channel_id=1, source_target_pairs={{0,1},{1,0},{2,3},{3,2},{4,5},{5,4},{6,7},{7,6},{8,9},{9,8},{10,11... | collective-permute-start | bytes 884744 | tf_op jit(solution)/shard_map/ppermute | solution.py:33
  218.1 7.9 %collective-permute-start.17 = (bf16[2,2,144,256]{3,2,1,0:T(8,128)(2,1)S(1)}, bf16[2,2,144,256]{3,2,1,0:T(8,128)(2,1)S(1)}, u32[]{:S(2)}, u32[]{:S(2)}) collective-permute-start(bf16[2,2,144,256]{3,2,1,0:T(8,128)(2,1)S(1)} %collective-permute-done.13.refs_1_), channel_id=1, source_target_pairs={{0,1},{1,0},{2,3},{3,2},{4,5},{5,4},{6,7},{7,6},{8,9},{9,8},{10,11... | collective-permute-start | bytes 884744 | tf_op jit(solution)/shard_map/ppermute | solution.py:33
  220.0 7.5 %collective-permute-start.19 = (bf16[2,2,144,256]{3,2,1,0:T(8,128)(2,1)S(1)}, bf16[2,2,144,256]{3,2,1,0:T(8,128)(2,1)}, u32[]{:S(2)}, u32[]{:S(2)}) collective-permute-start(bf16[2,2,144,256]{3,2,1,0:T(8,128)(2,1)S(1)} %collective-permute-done.15.refs_3_), channel_id=1, source_target_pairs={{0,1},{1,0},{2,3},{3,2},{4,5},{5,4},{6,7},{7,6},{8,9},{9,8},{10,11... | collective-permute-start | bytes 884744 | tf_op jit(solution)/shard_map/ppermute | solution.py:34
  222.7 3.3 %collective-permute-start.20 = (bf16[2,144,256]{2,1,0:T(8,128)(2,1)S(1)}, bf16[2,144,256]{2,1,0:T(8,128)(2,1)S(1)}, u32[]{:S(2)}, u32[]{:S(2)}) collective-permute-start(bf16[2,144,256]{2,1,0:T(8,128)(2,1)S(1)} %collective-permute-done.16.refs_4_), channel_id=1, source_target_pairs={{0,1},{1,0},{2,3},{3,2},{4,5},{5,4},{6,7},{7,6},{8,9},{9,8},{10,11... | collective-permute-start | bytes 442376 | tf_op jit(solution)/shard_map/ppermute | solution.py:34
  234.1 20.6 %all-to-all-start.2 = ((f32[16,8,256]{2,1,0:T(8,128)}), f32[16,8,256]{2,1,0:T(8,128)S(1)}, u32[]{:S(2)}, u32[]{:S(2)}) async-start(f32[16,8,256]{2,1,0:T(8,128)} %get-tuple-element.8), calls=%async_computation.2 | async-start | bytes 262144 | tf_op jit(solution)/shard_map/all_to_all | solution.py:39
  (18 other events, 373.5 us)
where the time goes:
time: 258 us; the launch traced here: 257 us
  waiting for transfers between devices  130 us (50%)
  starting transfers between devices  102 us (40%)
  Pallas kernels  12.2 us (5%)
  local copies, waits for them, and re-layouts  7.66 us (3%)
  other arithmetic  3.64 us (1%)
    ppermute x1, waiting for transfers between devices, per_device(): w_pair = lax.ppermute(w, 'yl', ring(2, 1))  53.4 us
    ppermute x2, waiting for transfers between devices, turned(): return lax.ppermute(output_weight.T, ('hx', 'hy', 'yl', 'z', 'c'), turn)  44.2 us
    ppermute x8, starting transfers between devices, send(): lax.ppermute(x, ('z', 'c'), [(2 * a + b, 2 * d + e) for (a, b), (d, e) in...  37.9 us
    all_to_all x3, starting transfers between devices, exchanged(): return lax.all_to_all(x, axis, split_axis=0, concat_axis=0, tiled=True)  28 us
    ppermute x8, waiting for transfers between devices, send(): lax.ppermute(x, ('z', 'c'), [(2 * a + b, 2 * d + e) for (a, b), (d, e) in...  18 us
    all_to_all x3, waiting for transfers between devices, exchanged(): return lax.all_to_all(x, axis, split_axis=0, concat_axis=0, tiled=True)  10.6 us
    ppermute x4, starting transfers between devices, z_pieces(): near = [lax.ppermute(p, 'c', ring(2, 1)) for p in (one, two)]  9.92 us
    ppermute x4, starting transfers between devices, z_pieces(): far = [lax.ppermute(p, 'c', ring(2, 1)) for p in (three, four)]  9.63 us
  transfers between devices with their start and end apart: 24, of which 12 were waited for; matrix products, arithmetic and copies ran while one was open for 1% of the time, Pallas kernels for 0%

commit v1 on v0

--- a/solution.py
+++ b/solution.py
@@ -39,12 +39,13 @@
     return lax.all_to_all(x, axis, split_axis=0, concat_axis=0, tiled=True)
 
 
-def norm_kernel(x, normed, first):
+def norm_kernel(stream, normed, first):
     per = 288
+    x = [stream.at[p % 4, p // 4] for p in range(16)]
     acc = jnp.zeros((16, 256), F32)
     for p in range(16):
         for b in range(per // 16):
-            w = x[p, b * 16 : (b + 1) * 16].astype(F32)
+            w = x[p][b * 16 : (b + 1) * 16].astype(F32)
             acc = acc + w * w
     sq = jnp.sum(acc, axis=0, keepdims=True)
     first[...] = jnp.broadcast_to(sq, (8, 256))
@@ -52,15 +53,15 @@
     scale_col = jnp.transpose(jnp.broadcast_to(scale, (128, 256)), (1, 0))
     rows = []
     for p in range(16):
-        rows += [x[p, per : per + 1].astype(F32), x[p, per + 1 : per + 2, :32].astype(F32)]
+        rows += [x[p][per : per + 1].astype(F32), x[p][per + 1 : per + 2, :32].astype(F32)]
     gain = jnp.concatenate(rows, axis=1)
     for b in range(D // 128):
         cols = slice(b * 128, (b + 1) * 128)
         p, at = divmod(b * 128, per)
         if at + 128 <= per:
-            block = x[p, at : at + 128]
+            block = x[p][at : at + 128]
         else:
-            block = jnp.concatenate([x[p, at:per], x[p + 1, : at + 128 - per]], axis=0)
+            block = jnp.concatenate([x[p][at:per], x[p + 1][: at + 128 - per]], axis=0)
         turned = jnp.transpose(block.astype(F32), (1, 0))
         normed[:, cols] = (turned * scale_col * gain[:, cols]).astype(BF)
 
@@ -103,7 +104,7 @@
         total = jnp.sum(weights, axis=1, keepdims=True)
         summed = jnp.dot(weights.astype(BF), values, preferred_element_type=F32)
         o[:, h * 128 : (h + 1) * 128] = (summed / total).astype(BF)
-    moves = [pltpu.make_async_copy(o, out.at[i], sems.at[i]) for i in range(16)]
+    moves = [pltpu.make_async_copy(o, out.at[i], sems.at[i]) for i in range(4)]
     for m in moves:
         m.start()
     for m in moves:
@@ -113,7 +114,7 @@
 def output_kernel(pos, x, gain, att, *refs):
     pieces, (mixed, sums, rows, att_v, *held, w_sems, sems) = refs[:9], refs[9:]
     w_moves = [pltpu.make_async_copy(p, h, w_sems.at[k]) for k, (p, h) in enumerate(zip(pieces, held))]
-    moves = [pltpu.make_async_copy(att.at[g], att_v.at[g], sems.at[g]) for g in range(16)]
+    moves = [pltpu.make_async_copy(att.at[g % 4, g // 4], att_v.at[g], sems.at[g]) for g in range(16)]
     for m in w_moves + moves:
         m.start()
     for m in w_moves + moves:
@@ -165,8 +166,9 @@
 
     x_t = stream_in.T
     gain_rows = jnp.pad(before_gain, (0, 8 * 256 - 288)).reshape(8, 256)
-    packed = jnp.concatenate([x_t, gain_rows], axis=0)
-    stream = exchanged(jnp.broadcast_to(packed, (16, *packed.shape)), hid)
+    packed = jnp.concatenate([x_t, gain_rows], axis=0)[None]
+    column = exchanged(jnp.broadcast_to(packed, (4, *packed.shape[1:])), "hx")
+    stream = exchanged(jnp.broadcast_to(column, (4, *column.shape)), "hy")
     normed, first = pl.pallas_call(
         norm_kernel,
         out_shape=(
@@ -177,7 +179,7 @@
         out_specs=(VMEM, VMEM),
         compiler_params=params(16),
         name="norm_stream",
-    )(stream)
+    )(stream.reshape(4, 4, 296, rows))
 
     def turned(flip):
         turn = [
@@ -200,19 +202,21 @@
     ).astype(F32)
     attended = pl.pallas_call(
         attend_kernel,
-        out_shape=jax.ShapeDtypeStruct((16, rows, 256), BF),
+        out_shape=jax.ShapeDtypeStruct((4, rows, 256), BF),
         in_specs=[SMEM] + [VMEM] * 13,
         out_specs=ANY,
         scratch_shapes=[
             pltpu.VMEM((16, 2, 144, 512), BF),
             pltpu.VMEM((rows, 256), BF),
-            pltpu.SemaphoreType.DMA((16,)),
+            pltpu.SemaphoreType.DMA((4,)),
         ],
         compiler_params=params(24),
         name="attend",
     )(pos, normed, jnp.cos(angles), jnp.sin(angles), mask, *w_pieces)
 
-    gathered = exchanged(attended, hid)
+    att_column = exchanged(attended, "hx")
+    gathered = exchanged(jnp.broadcast_to(att_column, (4, *att_column.shape)), "hy")
+    gathered = gathered.reshape(4, 4, rows, 256)
     after_col = after_gain.astype(F32)[:, None]
     feed_col = feed_gain.astype(F32)[:, None]
     mixed, sums = pl.pallas_call(

time: 258 us -> 197 us (0.76)
  the two profiles are of different devices: /device:TPU:8 before, /device:TPU:1 now
where the time goes in v1:
time: 197 us; the launch traced here: 195 us
  starting transfers between devices  102 us (52%)
  waiting for transfers between devices  45.1 us (23%)
  blocking collectives  21.8 us (11%)
  Pallas kernels  11.4 us (6%)
  local copies, waits for them, and re-layouts  10.4 us (5%)
  other arithmetic  3.64 us (2%)
    ppermute x8, starting transfers between devices, send(): lax.ppermute(x, ('z', 'c'), [(2 * a + b, 2 * d + e) for (a, b), (d, e) in...  45 us
    all_to_all x4, starting transfers between devices, exchanged(): return lax.all_to_all(x, axis, split_axis=0, concat_axis=0, tiled=True)  26.1 us
    all_to_all x1, blocking collectives, exchanged(): return lax.all_to_all(x, axis, split_axis=0, concat_axis=0, tiled=True)  21.8 us
    ppermute x1, waiting for transfers between devices, per_device(): w_pair = lax.ppermute(w, 'yl', ring(2, 1))  13.7 us
    ppermute x8, waiting for transfers between devices, send(): lax.ppermute(x, ('z', 'c'), [(2 * a + b, 2 * d + e) for (a, b), (d, e) in...  12.2 us
    all_to_all x4, waiting for transfers between devices, exchanged(): return lax.all_to_all(x, axis, split_axis=0, concat_axis=0, tiled=True)  9.39 us
    ppermute x4, starting transfers between devices, z_pieces(): far = [lax.ppermute(p, 'c', ring(2, 1)) for p in (three, four)]  8.85 us
    ppermute x4, starting transfers between devices, z_pieces(): near = [lax.ppermute(p, 'c', ring(2, 1)) for p in (one, two)]  8.66 us
  transfers between devices with their start and end apart: 25, of which 10 were waited for; matrix products, arithmetic and copies ran while one was open for 3% of the time, Pallas kernels for 1%

profile of v1, /device:TPU:1, one launch (start us, length us, event | category | flops | bytes accessed | tf_op | source)
XLA Modules:
  0.0 195.5 jit_solution(6165595328381668689)
XLA Ops:
  3.2 7.6 %all-to-all-start = ((bf16[4,296,256]{2,1,0:T(8,128)(2,1)}), bf16[4,296,256]{2,1,0:T(8,128)(2,1)S(1)}, u32[]{:S(2)}, u32[]{:S(2)}) async-start(bf16[4,296,256]{2,1,0:T(8,128)(2,1)} %broadcast_in_dim.9), calls=%async_computation | async-start | bytes 1212416 | tf_op jit(solution)/shard_map/all_to_all | solution.py:39
  11.7 2.3 %collective-permute-start = (bf16[144,512]{1,0:T(8,128)(2,1)S(1)}, bf16[144,512]{1,0:T(8,128)(2,1)S(1)}, u32[]{:S(2)}, u32[]{:S(2)}) collective-permute-start(bf16[144,512]{1,0:T(8,128)(2,1)S(1)} %constant_dynamic-update-slice_fusion), channel_id=1, source_target_pairs={{0,16},{16,0},{1,17},{17,1},{2,18},{18,2},{3,19},{19,3},{4,20},{20... | collective-permute-start | bytes 442376 | tf_op jit(solution)/shard_map/ppermute | solution.py:164
  14.0 13.7 %collective-permute-done = bf16[144,512]{1,0:T(8,128)(2,1)S(1)} collective-permute-done((bf16[144,512]{1,0:T(8,128)(2,1)S(1)}, bf16[144,512]{1,0:T(8,128)(2,1)S(1)}, u32[]{:S(2)}, u32[]{:S(2)}) %collective-permute-start) | collective-permute-done | bytes 147488 | tf_op jit(solution)/shard_map/ppermute | solution.py:164
  27.8 3.4 %collective-permute-start.1 = (bf16[2,144,512]{2,1,0:T(8,128)(2,1)S(1)}, bf16[2,144,512]{2,1,0:T(8,128)(2,1)S(1)}, u32[]{:S(2)}, u32[]{:S(2)}) collective-permute-start(bf16[2,144,512]{2,1,0:T(8,128)(2,1)S(1)} %get-tuple-element.13), channel_id=1, source_target_pairs={{0,1},{1,0},{2,3},{3,2},{4,5},{5,4},{6,7},{7,6},{8,9},{9,8},{10,11... | collective-permute-start | bytes 884744 | tf_op jit(solution)/shard_map/ppermute | solution.py:23
  32.4 10.7 %collective-permute-start.3 = (bf16[2,2,144,512]{3,2,1,0:T(8,128)(2,1)S(1)}, bf16[2,2,144,512]{3,2,1,0:T(8,128)(2,1)}, u32[]{:S(2)}, u32[]{:S(2)}) collective-permute-start(bf16[2,2,144,512]{3,2,1,0:T(8,128)(2,1)S(1)} %pad_maximum_fusion.refs_0_), channel_id=1, source_target_pairs={{0,4},{1,13},{2,6},{3,15},{4,8},{5,1},{6,10},{7,3},{8,12},{9,5},{1... | collective-permute-start | bytes 1769480 | tf_op jit(solution)/shard_map/ppermute | solution.py:29
  44.7 4.1 %all-to-all-start.1 = ((bf16[4,4,296,256]{3,2,1,0:T(8,128)(2,1)}), bf16[4,4,296,256]{3,2,1,0:T(8,128)(2,1)S(1)}, u32[]{:S(2)}, u32[]{:S(2)}) async-start(bf16[4,4,296,256]{3,2,1,0:T(8,128)(2,1)} %broadcast_in_dim.10), calls=%async_computation.1 | async-start | bytes 4849664 | tf_op jit(solution)/shard_map/all_to_all | solution.py:39
  51.0 5.2 %collective-permute-done.3.refs_2_ = bf16[2,2,144,512]{3,2,1,0:T(8,128)(2,1)} collective-permute-done((bf16[2,2,144,512]{3,2,1,0:T(8,128)(2,1)S(1)}, bf16[2,2,144,512]{3,2,1,0:T(8,128)(2,1)}, u32[]{:S(2)}, u32[]{:S(2)}) %collective-permute-start.3) | collective-permute-done | bytes 589856 | tf_op jit(solution)/shard_map/ppermute | solution.py:29
  56.2 3.2 %collective-permute-start.4 = (bf16[2,2,144,512]{3,2,1,0:T(8,128)(2,1)}, bf16[2,2,144,512]{3,2,1,0:T(8,128)(2,1)}, u32[]{:S(2)}, u32[]{:S(2)}) collective-permute-start(bf16[2,2,144,512]{3,2,1,0:T(8,128)(2,1)} %collective-permute-done.3.refs_2_), channel_id=1, source_target_pairs={{0,2},{1,15},{2,4},{3,1},{4,6},{5,3},{6,8},{7,5},{8,10},{9,7},{10,... | collective-permute-start | bytes 1769480 | tf_op jit(solution)/shard_map/ppermute | solution.py:29
  61.2 4.8 %collective-permute-start.5 = (bf16[2,144,512]{2,1,0:T(8,128)(2,1)}, bf16[2,144,512]{2,1,0:T(8,128)(2,1)}, u32[]{:S(2)}, u32[]{:S(2)}) collective-permute-start(bf16[2,144,512]{2,1,0:T(8,128)(2,1)} %slice_bitcast_fusion), channel_id=1, source_target_pairs={{0,4},{1,13},{2,6},{3,15},{4,8},{5,1},{6,10},{7,3},{8,12},{9,5},{1... | collective-permute-start | bytes 884744 | tf_op jit(solution)/shard_map/ppermute | solution.py:29
  67.9 2.4 %collective-permute-start.6 = (bf16[2,2,144,512]{3,2,1,0:T(8,128)(2,1)}, bf16[2,2,144,512]{3,2,1,0:T(8,128)(2,1)}, u32[]{:S(2)}, u32[]{:S(2)}) collective-permute-start(bf16[2,2,144,512]{3,2,1,0:T(8,128)(2,1)} %collective-permute-done.2.refs_1_), channel_id=1, source_target_pairs={{0,1},{1,0},{2,3},{3,2},{4,5},{5,4},{6,7},{7,6},{8,9},{9,8},{10,11... | collective-permute-start | bytes 1769480 | tf_op jit(solution)/shard_map/ppermute | solution.py:33
  79.1 5.1 %attend.1 = bf16[4,256,256]{2,1,0:T(8,128)(2,1)S(1)} custom-call(s32[3]{0:T(128)S(1)} %pad_add_fusion.pos, bf16[256,4608]{1,0:T(8,128)(2,1)S(1)} %get-tuple-element.6.normed, f32[256,64]{1,0:T(8,128)S(1)} %get-tuple-element.19.cos, f32[256,64]{1,0:T(8,128)S(1)} %get-tuple-element.18.sin, f32[256,256]{1,0:T(8,128)S(1)} %fusion.1.mask, ...), custom_call_target="tpu_custom_call" | custom-call | tf_op jit(solution)/shard_map/attend/pallas_call | solution.py:203
  84.2 21.8 %all_to_all.25 = bf16[4,256,256]{2,1,0:T(8,128)(2,1)S(1)} all-to-all(bf16[4,256,256]{2,1,0:T(8,128)(2,1)S(1)} %attend.1), channel_id=1, replica_groups=mesh['hx'=4,'hy'=4,'yl'=2,'z'=8,'c'=2] {'hx'}, dimensions={0} | all-to-all | bytes 1048576 | tf_op jit(solution)/shard_map/all_to_all | solution.py:39
  107.6 4.1 %all-to-all-start.3 = ((bf16[4,4,256,256]{3,2,1,0:T(8,128)(2,1)}), bf16[4,4,256,256]{3,2,1,0:T(8,128)(2,1)S(1)}, u32[]{:S(2)}, u32[]{:S(2)}) async-start(bf16[4,4,256,256]{3,2,1,0:T(8,128)(2,1)} %broadcast_in_dim.11), calls=%async_computation.3 | async-start | bytes 4194304 | tf_op jit(solution)/shard_map/all_to_all | solution.py:39
  114.3 6.4 %collective-permute-done.11 = bf16[144,256]{1,0:T(8,128)(2,1)S(1)} collective-permute-done((bf16[144,256]{1,0:T(8,128)(2,1)S(1)}, bf16[144,256]{1,0:T(8,128)(2,1)S(1)}, u32[]{:S(2)}, u32[]{:S(2)}) %collective-permute-start.11) | collective-permute-done | bytes 73760 | tf_op jit(solution)/shard_map/ppermute | solution.py:191
  120.7 5.1 %collective-permute-start.12 = (bf16[2,144,256]{2,1,0:T(8,128)(2,1)S(1)}, bf16[2,144,256]{2,1,0:T(8,128)(2,1)S(1)}, u32[]{:S(2)}, u32[]{:S(2)}) collective-permute-start(bf16[2,144,256]{2,1,0:T(8,128)(2,1)S(1)} %get-tuple-element.15), channel_id=1, source_target_pairs={{0,1},{1,0},{2,3},{3,2},{4,5},{5,4},{6,7},{7,6},{8,9},{9,8},{10,11... | collective-permute-start | bytes 442376 | tf_op jit(solution)/shard_map/ppermute | solution.py:23
  126.9 14.3 %collective-permute-start.14 = (bf16[2,2,144,256]{3,2,1,0:T(8,128)(2,1)S(1)}, bf16[2,2,144,256]{3,2,1,0:T(8,128)(2,1)S(1)}, u32[]{:S(2)}, u32[]{:S(2)}) collective-permute-start(bf16[2,2,144,256]{3,2,1,0:T(8,128)(2,1)S(1)} %pad_maximum_fusion.2.refs_0_), channel_id=1, source_target_pairs={{0,4},{1,13},{2,6},{3,15},{4,8},{5,1},{6,10},{7,3},{8,12},{9,5},{1... | collective-permute-start | bytes 884744 | tf_op jit(solution)/shard_map/ppermute | solution.py:29
  143.1 4.9 %collective-permute-done.14.refs_2_ = bf16[2,2,144,256]{3,2,1,0:T(8,128)(2,1)S(1)} collective-permute-done((bf16[2,2,144,256]{3,2,1,0:T(8,128)(2,1)S(1)}, bf16[2,2,144,256]{3,2,1,0:T(8,128)(2,1)S(1)}, u32[]{:S(2)}, u32[]{:S(2)}) %collective-permute-start.14) | collective-permute-done | bytes 294944 | tf_op jit(solution)/shard_map/ppermute | solution.py:29
  148.0 2.8 %collective-permute-start.15 = (bf16[2,2,144,256]{3,2,1,0:T(8,128)(2,1)S(1)}, bf16[2,2,144,256]{3,2,1,0:T(8,128)(2,1)S(1)}, u32[]{:S(2)}, u32[]{:S(2)}) collective-permute-start(bf16[2,2,144,256]{3,2,1,0:T(8,128)(2,1)S(1)} %collective-permute-done.14.refs_2_), channel_id=1, source_target_pairs={{0,2},{1,15},{2,4},{3,1},{4,6},{5,3},{6,8},{7,5},{8,10},{9,7},{10,... | collective-permute-start | bytes 884744 | tf_op jit(solution)/shard_map/ppermute | solution.py:29
  150.8 5.2 %collective-permute-start.16 = (bf16[2,144,256]{2,1,0:T(8,128)(2,1)S(1)}, bf16[2,144,256]{2,1,0:T(8,128)(2,1)S(1)}, u32[]{:S(2)}, u32[]{:S(2)}) collective-permute-start(bf16[2,144,256]{2,1,0:T(8,128)(2,1)S(1)} %slice_bitcast_fusion.1), channel_id=1, source_target_pairs={{0,4},{1,13},{2,6},{3,15},{4,8},{5,1},{6,10},{7,3},{8,12},{9,5},{1... | collective-permute-start | bytes 442376 | tf_op jit(solution)/shard_map/ppermute | solution.py:29
  157.9 2.4 %collective-permute-start.18 = (bf16[2,2,144,256]{3,2,1,0:T(8,128)(2,1)S(1)}, bf16[2,2,144,256]{3,2,1,0:T(8,128)(2,1)S(1)}, u32[]{:S(2)}, u32[]{:S(2)}) collective-permute-start(bf16[2,2,144,256]{3,2,1,0:T(8,128)(2,1)S(1)} %collective-permute-done.14.refs_2_), channel_id=1, source_target_pairs={{0,1},{1,0},{2,3},{3,2},{4,5},{5,4},{6,7},{7,6},{8,9},{9,8},{10,11... | collective-permute-start | bytes 884744 | tf_op jit(solution)/shard_map/ppermute | solution.py:33
  160.4 2.8 %collective-permute-start.19 = (bf16[2,2,144,256]{3,2,1,0:T(8,128)(2,1)S(1)}, bf16[2,2,144,256]{3,2,1,0:T(8,128)(2,1)}, u32[]{:S(2)}, u32[]{:S(2)}) collective-permute-start(bf16[2,2,144,256]{3,2,1,0:T(8,128)(2,1)S(1)} %collective-permute-done.15.refs_3_), channel_id=1, source_target_pairs={{0,1},{1,0},{2,3},{3,2},{4,5},{5,4},{6,7},{7,6},{8,9},{9,8},{10,11... | collective-permute-start | bytes 884744 | tf_op jit(solution)/shard_map/ppermute | solution.py:34
  168.7 5.2 %project_out.1 = (f32[288,256]{1,0:T(8,128)}, f32[16,8,256]{2,1,0:T(8,128)}) custom-call(s32[3]{0:T(128)} %copy-done, bf16[288,256]{1,0:T(8,128)(2,1)} %bitcast.27, f32[288,1]{1,0:T(8,128)} %broadcast_in_dim.12.gain, bf16[4,4,256,256]{3,2,1,0:T(8,128)(2,1)} %copy-done.1, bf16[2,2,144,256]{3,2,1,0:T(8,128)(2,1)} %copy-done.3, ...), custom_call_target="tpu_custom_call" | custom-call | tf_op jit(solution)/shard_map/project_out/pallas_call | solution.py:222
  174.0 10.2 %all-to-all-start.4 = ((f32[16,8,256]{2,1,0:T(8,128)}), f32[16,8,256]{2,1,0:T(8,128)S(1)}, u32[]{:S(2)}, u32[]{:S(2)}) async-start(f32[16,8,256]{2,1,0:T(8,128)} %get-tuple-element.8), calls=%async_computation.4 | async-start | bytes 262144 | tf_op jit(solution)/shard_map/all_to_all | solution.py:39
  184.2 9.4 %all-to-all-done.4 = f32[16,8,256]{2,1,0:T(8,128)S(1)} async-done(((f32[16,8,256]{2,1,0:T(8,128)}), f32[16,8,256]{2,1,0:T(8,128)S(1)}, u32[]{:S(2)}, u32[]{:S(2)}) %all-to-all-start.4) | async-done | bytes 131104 | tf_op jit(solution)/shard_map/all_to_all | solution.py:39
  (90 shorter events, 37.2 us)
Async XLA Ops:
  3.2 39.9 %all-to-all-start = ((bf16[4,296,256]{2,1,0:T(8,128)(2,1)}), bf16[4,296,256]{2,1,0:T(8,128)(2,1)S(1)}, u32[]{:S(2)}, u32[]{:S(2)}) async-start(bf16[4,296,256]{2,1,0:T(8,128)(2,1)} %broadcast_in_dim.9), calls=%async_computation | async-start | bytes 1212416 | tf_op jit(solution)/shard_map/all_to_all | solution.py:39
  11.7 16.0 %collective-permute-start = (bf16[144,512]{1,0:T(8,128)(2,1)S(1)}, bf16[144,512]{1,0:T(8,128)(2,1)S(1)}, u32[]{:S(2)}, u32[]{:S(2)}) collective-permute-start(bf16[144,512]{1,0:T(8,128)(2,1)S(1)} %constant_dynamic-update-slice_fusion), channel_id=1, source_target_pairs={{0,16},{16,0},{1,17},{17,1},{2,18},{18,2},{3,19},{19,3},{4,20},{20... | collective-permute-start | bytes 442376 | tf_op jit(solution)/shard_map/ppermute | solution.py:164
  27.8 4.6 %collective-permute-start.1 = (bf16[2,144,512]{2,1,0:T(8,128)(2,1)S(1)}, bf16[2,144,512]{2,1,0:T(8,128)(2,1)S(1)}, u32[]{:S(2)}, u32[]{:S(2)}) collective-permute-start(bf16[2,144,512]{2,1,0:T(8,128)(2,1)S(1)} %get-tuple-element.13), channel_id=1, source_target_pairs={{0,1},{1,0},{2,3},{3,2},{4,5},{5,4},{6,7},{7,6},{8,9},{9,8},{10,11... | collective-permute-start | bytes 884744 | tf_op jit(solution)/shard_map/ppermute | solution.py:23
  32.4 23.8 %collective-permute-start.3 = (bf16[2,2,144,512]{3,2,1,0:T(8,128)(2,1)S(1)}, bf16[2,2,144,512]{3,2,1,0:T(8,128)(2,1)}, u32[]{:S(2)}, u32[]{:S(2)}) collective-permute-start(bf16[2,2,144,512]{3,2,1,0:T(8,128)(2,1)S(1)} %pad_maximum_fusion.refs_0_), channel_id=1, source_target_pairs={{0,4},{1,13},{2,6},{3,15},{4,8},{5,1},{6,10},{7,3},{8,12},{9,5},{1... | collective-permute-start | bytes 1769480 | tf_op jit(solution)/shard_map/ppermute | solution.py:29
  44.7 32.7 %all-to-all-start.1 = ((bf16[4,4,296,256]{3,2,1,0:T(8,128)(2,1)}), bf16[4,4,296,256]{3,2,1,0:T(8,128)(2,1)S(1)}, u32[]{:S(2)}, u32[]{:S(2)}) async-start(bf16[4,4,296,256]{3,2,1,0:T(8,128)(2,1)} %broadcast_in_dim.10), calls=%async_computation.1 | async-start | bytes 4849664 | tf_op jit(solution)/shard_map/all_to_all | solution.py:39
  48.8 19.1 %collective-permute-start.2 = (bf16[2,2,144,512]{3,2,1,0:T(8,128)(2,1)S(1)}, bf16[2,2,144,512]{3,2,1,0:T(8,128)(2,1)}, u32[]{:S(2)}, u32[]{:S(2)}) collective-permute-start(bf16[2,2,144,512]{3,2,1,0:T(8,128)(2,1)S(1)} %pad_maximum_fusion.refs_0_), channel_id=1, source_target_pairs={{0,2},{1,15},{2,4},{3,1},{4,6},{5,3},{6,8},{7,5},{8,10},{9,7},{10,... | collective-permute-start | bytes 1769480 | tf_op jit(solution)/shard_map/ppermute | solution.py:29
  56.2 14.1 %collective-permute-start.4 = (bf16[2,2,144,512]{3,2,1,0:T(8,128)(2,1)}, bf16[2,2,144,512]{3,2,1,0:T(8,128)(2,1)}, u32[]{:S(2)}, u32[]{:S(2)}) collective-permute-start(bf16[2,2,144,512]{3,2,1,0:T(8,128)(2,1)} %collective-permute-done.3.refs_2_), channel_id=1, source_target_pairs={{0,2},{1,15},{2,4},{3,1},{4,6},{5,3},{6,8},{7,5},{8,10},{9,7},{10,... | collective-permute-start | bytes 1769480 | tf_op jit(solution)/shard_map/ppermute | solution.py:29
  61.2 14.1 %collective-permute-start.5 = (bf16[2,144,512]{2,1,0:T(8,128)(2,1)}, bf16[2,144,512]{2,1,0:T(8,128)(2,1)}, u32[]{:S(2)}, u32[]{:S(2)}) collective-permute-start(bf16[2,144,512]{2,1,0:T(8,128)(2,1)} %slice_bitcast_fusion), channel_id=1, source_target_pairs={{0,4},{1,13},{2,6},{3,15},{4,8},{5,1},{6,10},{7,3},{8,12},{9,5},{1... | collective-permute-start | bytes 884744 | tf_op jit(solution)/shard_map/ppermute | solution.py:29
  66.0 12.5 %collective-permute-start.7 = (bf16[2,2,144,512]{3,2,1,0:T(8,128)(2,1)}, bf16[2,2,144,512]{3,2,1,0:T(8,128)(2,1)}, u32[]{:S(2)}, u32[]{:S(2)}) collective-permute-start(bf16[2,2,144,512]{3,2,1,0:T(8,128)(2,1)} %collective-permute-done.3.refs_2_), channel_id=1, source_target_pairs={{0,1},{1,0},{2,3},{3,2},{4,5},{5,4},{6,7},{7,6},{8,9},{9,8},{10,11... | collective-permute-start | bytes 1769480 | tf_op jit(solution)/shard_map/ppermute | solution.py:33
  67.9 10.5 %collective-permute-start.6 = (bf16[2,2,144,512]{3,2,1,0:T(8,128)(2,1)}, bf16[2,2,144,512]{3,2,1,0:T(8,128)(2,1)}, u32[]{:S(2)}, u32[]{:S(2)}) collective-permute-start(bf16[2,2,144,512]{3,2,1,0:T(8,128)(2,1)} %collective-permute-done.2.refs_1_), channel_id=1, source_target_pairs={{0,1},{1,0},{2,3},{3,2},{4,5},{5,4},{6,7},{7,6},{8,9},{9,8},{10,11... | collective-permute-start | bytes 1769480 | tf_op jit(solution)/shard_map/ppermute | solution.py:33
  70.4 8.7 %collective-permute-start.8 = (bf16[2,2,144,512]{3,2,1,0:T(8,128)(2,1)}, bf16[2,2,144,512]{3,2,1,0:T(8,128)(2,1)}, u32[]{:S(2)}, u32[]{:S(2)}) collective-permute-start(bf16[2,2,144,512]{3,2,1,0:T(8,128)(2,1)} %collective-permute-done.4.refs_3_), channel_id=1, source_target_pairs={{0,1},{1,0},{2,3},{3,2},{4,5},{5,4},{6,7},{7,6},{8,9},{9,8},{10,11... | collective-permute-start | bytes 1769480 | tf_op jit(solution)/shard_map/ppermute | solution.py:34
  75.3 3.8 %collective-permute-start.9 = (bf16[2,144,512]{2,1,0:T(8,128)(2,1)}, bf16[2,144,512]{2,1,0:T(8,128)(2,1)}, u32[]{:S(2)}, u32[]{:S(2)}) collective-permute-start(bf16[2,144,512]{2,1,0:T(8,128)(2,1)} %collective-permute-done.5.refs_4_), channel_id=1, source_target_pairs={{0,1},{1,0},{2,3},{3,2},{4,5},{5,4},{6,7},{7,6},{8,9},{9,8},{10,11... | collective-permute-start | bytes 884744 | tf_op jit(solution)/shard_map/ppermute | solution.py:34
  107.6 59.8 %all-to-all-start.3 = ((bf16[4,4,256,256]{3,2,1,0:T(8,128)(2,1)}), bf16[4,4,256,256]{3,2,1,0:T(8,128)(2,1)S(1)}, u32[]{:S(2)}, u32[]{:S(2)}) async-start(bf16[4,4,256,256]{3,2,1,0:T(8,128)(2,1)} %broadcast_in_dim.11), calls=%async_computation.3 | async-start | bytes 4194304 | tf_op jit(solution)/shard_map/all_to_all | solution.py:39
  111.7 9.0 %collective-permute-start.11 = (bf16[144,256]{1,0:T(8,128)(2,1)S(1)}, bf16[144,256]{1,0:T(8,128)(2,1)S(1)}, u32[]{:S(2)}, u32[]{:S(2)}) collective-permute-start(bf16[144,256]{1,0:T(8,128)(2,1)S(1)} %bitcast.37), channel_id=1, source_target_pairs={{0,16},{1,17},{2,48},{3,49},{4,80},{5,81},{6,112},{7,113},{8,144},... | collective-permute-start | bytes 221192 | tf_op jit(solution)/shard_map/ppermute | solution.py:191
  113.6 7.1 %collective-permute-start.10 = (bf16[144,256]{1,0:T(8,128)(2,1)S(1)}, bf16[144,256]{1,0:T(8,128)(2,1)S(1)}, u32[]{:S(2)}, u32[]{:S(2)}) collective-permute-start(bf16[144,256]{1,0:T(8,128)(2,1)S(1)} %bitcast.38), channel_id=1, source_target_pairs={{0,0},{1,1},{2,32},{3,33},{4,64},{5,65},{6,96},{7,97},{8,128},{9,1... | collective-permute-start | bytes 221192 | tf_op jit(solution)/shard_map/ppermute | solution.py:191
  120.7 6.1 %collective-permute-start.12 = (bf16[2,144,256]{2,1,0:T(8,128)(2,1)S(1)}, bf16[2,144,256]{2,1,0:T(8,128)(2,1)S(1)}, u32[]{:S(2)}, u32[]{:S(2)}) collective-permute-start(bf16[2,144,256]{2,1,0:T(8,128)(2,1)S(1)} %get-tuple-element.15), channel_id=1, source_target_pairs={{0,1},{1,0},{2,3},{3,2},{4,5},{5,4},{6,7},{7,6},{8,9},{9,8},{10,11... | collective-permute-start | bytes 442376 | tf_op jit(solution)/shard_map/ppermute | solution.py:23
  126.9 21.2 %collective-permute-start.14 = (bf16[2,2,144,256]{3,2,1,0:T(8,128)(2,1)S(1)}, bf16[2,2,144,256]{3,2,1,0:T(8,128)(2,1)S(1)}, u32[]{:S(2)}, u32[]{:S(2)}) collective-permute-start(bf16[2,2,144,256]{3,2,1,0:T(8,128)(2,1)S(1)} %pad_maximum_fusion.2.refs_0_), channel_id=1, source_target_pairs={{0,4},{1,13},{2,6},{3,15},{4,8},{5,1},{6,10},{7,3},{8,12},{9,5},{1... | collective-permute-start | bytes 884744 | tf_op jit(solution)/shard_map/ppermute | solution.py:29
  141.2 14.8 %collective-permute-start.13 = (bf16[2,2,144,256]{3,2,1,0:T(8,128)(2,1)S(1)}, bf16[2,2,144,256]{3,2,1,0:T(8,128)(2,1)S(1)}, u32[]{:S(2)}, u32[]{:S(2)}) collective-permute-start(bf16[2,2,144,256]{3,2,1,0:T(8,128)(2,1)S(1)} %pad_maximum_fusion.2.refs_0_), channel_id=1, source_target_pairs={{0,2},{1,15},{2,4},{3,1},{4,6},{5,3},{6,8},{7,5},{8,10},{9,7},{10,... | collective-permute-start | bytes 884744 | tf_op jit(solution)/shard_map/ppermute | solution.py:29
  148.0 12.3 %collective-permute-start.15 = (bf16[2,2,144,256]{3,2,1,0:T(8,128)(2,1)S(1)}, bf16[2,2,144,256]{3,2,1,0:T(8,128)(2,1)S(1)}, u32[]{:S(2)}, u32[]{:S(2)}) collective-permute-start(bf16[2,2,144,256]{3,2,1,0:T(8,128)(2,1)S(1)} %collective-permute-done.14.refs_2_), channel_id=1, source_target_pairs={{0,2},{1,15},{2,4},{3,1},{4,6},{5,3},{6,8},{7,5},{8,10},{9,7},{10,... | collective-permute-start | bytes 884744 | tf_op jit(solution)/shard_map/ppermute | solution.py:29
  150.8 12.3 %collective-permute-start.16 = (bf16[2,144,256]{2,1,0:T(8,128)(2,1)S(1)}, bf16[2,144,256]{2,1,0:T(8,128)(2,1)S(1)}, u32[]{:S(2)}, u32[]{:S(2)}) collective-permute-start(bf16[2,144,256]{2,1,0:T(8,128)(2,1)S(1)} %slice_bitcast_fusion.1), channel_id=1, source_target_pairs={{0,4},{1,13},{2,6},{3,15},{4,8},{5,1},{6,10},{7,3},{8,12},{9,5},{1... | collective-permute-start | bytes 442376 | tf_op jit(solution)/shard_map/ppermute | solution.py:29
  156.0 9.9 %collective-permute-start.17 = (bf16[2,2,144,256]{3,2,1,0:T(8,128)(2,1)S(1)}, bf16[2,2,144,256]{3,2,1,0:T(8,128)(2,1)S(1)}, u32[]{:S(2)}, u32[]{:S(2)}) collective-permute-start(bf16[2,2,144,256]{3,2,1,0:T(8,128)(2,1)S(1)} %collective-permute-done.13.refs_1_), channel_id=1, source_target_pairs={{0,1},{1,0},{2,3},{3,2},{4,5},{5,4},{6,7},{7,6},{8,9},{9,8},{10,11... | collective-permute-start | bytes 884744 | tf_op jit(solution)/shard_map/ppermute | solution.py:33
  157.9 8.0 %collective-permute-start.18 = (bf16[2,2,144,256]{3,2,1,0:T(8,128)(2,1)S(1)}, bf16[2,2,144,256]{3,2,1,0:T(8,128)(2,1)S(1)}, u32[]{:S(2)}, u32[]{:S(2)}) collective-permute-start(bf16[2,2,144,256]{3,2,1,0:T(8,128)(2,1)S(1)} %collective-permute-done.14.refs_2_), channel_id=1, source_target_pairs={{0,1},{1,0},{2,3},{3,2},{4,5},{5,4},{6,7},{7,6},{8,9},{9,8},{10,11... | collective-permute-start | bytes 884744 | tf_op jit(solution)/shard_map/ppermute | solution.py:33
  160.4 7.0 %collective-permute-start.19 = (bf16[2,2,144,256]{3,2,1,0:T(8,128)(2,1)S(1)}, bf16[2,2,144,256]{3,2,1,0:T(8,128)(2,1)}, u32[]{:S(2)}, u32[]{:S(2)}) collective-permute-start(bf16[2,2,144,256]{3,2,1,0:T(8,128)(2,1)S(1)} %collective-permute-done.15.refs_3_), channel_id=1, source_target_pairs={{0,1},{1,0},{2,3},{3,2},{4,5},{5,4},{6,7},{7,6},{8,9},{9,8},{10,11... | collective-permute-start | bytes 884744 | tf_op jit(solution)/shard_map/ppermute | solution.py:34
  174.0 19.6 %all-to-all-start.4 = ((f32[16,8,256]{2,1,0:T(8,128)}), f32[16,8,256]{2,1,0:T(8,128)S(1)}, u32[]{:S(2)}, u32[]{:S(2)}) async-start(f32[16,8,256]{2,1,0:T(8,128)} %get-tuple-element.8), calls=%async_computation.4 | async-start | bytes 262144 | tf_op jit(solution)/shard_map/all_to_all | solution.py:39
  (18 other events, 257.7 us)

commit v2 on v1

--- a/solution.py
+++ b/solution.py
@@ -37,6 +37,28 @@
 
 def exchanged(x, axis):
     return lax.all_to_all(x, axis, split_axis=0, concat_axis=0, tiled=True)
+
+
+def pack_kernel(q, k, v, x, gain, w, packed, g, last, sems):
+    get = pltpu.make_async_copy(gain, g, sems.at[0])
+    moves = [
+        pltpu.make_async_copy(q, w.at[:, pl.ds(0, 256)], sems.at[1]),
+        pltpu.make_async_copy(k, w.at[:, pl.ds(256, 128)], sems.at[2]),
+        pltpu.make_async_copy(v, w.at[:, pl.ds(384, 128)], sems.at[3]),
+    ]
+    moves += [pltpu.make_async_copy(x, packed.at[i, pl.ds(0, 288)], sems.at[4 + i]) for i in range(4)]
+    get.start()
+    for m in moves:
+        m.start()
+    get.wait()
+    row = g[...].astype(F32).reshape(1, 288)
+    tail = jnp.concatenate([row[:, 256:], jnp.zeros((1, 224), F32)], axis=1)
+    last[...] = jnp.concatenate([row[:, :256], tail, jnp.zeros((6, 256), F32)], axis=0).astype(BF)
+    ends = [pltpu.make_async_copy(last, packed.at[i, pl.ds(288, 8)], sems.at[8 + i]) for i in range(4)]
+    for m in ends:
+        m.start()
+    for m in moves + ends:
+        m.wait()
 
 
 def norm_kernel(stream, normed, first):
@@ -112,19 +134,21 @@
 
 
 def output_kernel(pos, x, gain, att, *refs):
-    pieces, (mixed, sums, rows, att_v, *held, w_sems, sems) = refs[:9], refs[9:]
+    pieces, (mixed, sums, rows, *held, w_sems) = refs[:9], refs[9:]
     w_moves = [pltpu.make_async_copy(p, h, w_sems.at[k]) for k, (p, h) in enumerate(zip(pieces, held))]
-    moves = [pltpu.make_async_copy(att.at[g % 4, g // 4], att_v.at[g], sems.at[g]) for g in range(16)]
-    for m in w_moves + moves:
+    for m in w_moves:
         m.start()
-    for m in w_moves + moves:
+    for m in w_moves:
         m.wait()
     for k, i, r, t, core in blocks(pos):
         rows[t, core] = held[k][r] if i is None else held[k][i, r]
     total = jnp.zeros((288, 256), F32)
     for g in range(16):
         term = lax.dot_general(
-            rows[g].reshape(288, 256), att_v[g], (((1,), (1,)), ((), ())), preferred_element_type=F32
+            rows[g].reshape(288, 256),
+            att[g % 4, g // 4],
+            (((1,), (1,)), ((), ())),
+            preferred_element_type=F32,
         )
         total = total + term.astype(BF).astype(F32)
     mixed[...] = total
@@ -137,6 +161,7 @@
 
 
 ANY = pl.BlockSpec(memory_space=pl.ANY)
+HBM = pl.BlockSpec(memory_space=pltpu.HBM)
 VMEM = pl.BlockSpec(memory_space=pltpu.VMEM)
 SMEM = pl.BlockSpec(memory_space=pltpu.SMEM)
 
@@ -160,14 +185,27 @@
     pos = jnp.stack([lax.axis_index(a) for a in ("yl", "z", "c")]).astype(jnp.int32)
     rows = LENGTH
 
-    w = jnp.concatenate([query_weight, key_weight, value_weight], axis=1)
+    x_t = stream_in.T
+    w, packed = pl.pallas_call(
+        pack_kernel,
+        out_shape=(
+            jax.ShapeDtypeStruct((144, 512), BF),
+            jax.ShapeDtypeStruct((4, 296, rows), BF),
+        ),
+        in_specs=[HBM] * 5,
+        out_specs=(HBM, HBM),
+        scratch_shapes=[
+            pltpu.VMEM((288,), BF),
+            pltpu.VMEM((8, 256), BF),
+            pltpu.SemaphoreType.DMA((12,)),
+        ],
+        compiler_params=params(60),
+        name="pack",
+    )(query_weight, key_weight, value_weight, x_t, before_gain)
     w_pair = lax.ppermute(w, "yl", ring(2, 1))
     w_pieces = z_pieces(both_cores(jnp.stack([w, w_pair])))
 
-    x_t = stream_in.T
-    gain_rows = jnp.pad(before_gain, (0, 8 * 256 - 288)).reshape(8, 256)
-    packed = jnp.concatenate([x_t, gain_rows], axis=0)[None]
-    column = exchanged(jnp.broadcast_to(packed, (4, *packed.shape[1:])), "hx")
+    column = exchanged(packed, "hx")
     stream = exchanged(jnp.broadcast_to(column, (4, *column.shape)), "hy")
     normed, first = pl.pallas_call(
         norm_kernel,
@@ -225,14 +263,12 @@
             jax.ShapeDtypeStruct((288, rows), F32),
             jax.ShapeDtypeStruct((16, 8, rows), F32),
         ),
-        in_specs=[SMEM, VMEM, VMEM] + [ANY] * 10,
+        in_specs=[SMEM] + [VMEM] * 3 + [ANY] * 9,
         out_specs=(VMEM, VMEM),
         scratch_shapes=[
             pltpu.VMEM((16, 2, 144, 256), BF),
-            pltpu.VMEM((16, rows, 256), BF),
             *[pltpu.VMEM(p.shape, BF) for p in wo_pieces],
             pltpu.SemaphoreType.DMA((9,)),
-            pltpu.SemaphoreType.DMA((16,)),
         ],
         compiler_params=params(56),
         name="project_out",

time: 197 us -> 219 us (1.11)
  Pallas kernels: 11.4 us -> 34.9 us
  local copies, waits for them, and re-layouts: 10.4 us -> 7.91 us
    pallas_call x0 -> x1, Pallas kernels: none -> 23.6 us  [per_device(): pl.pallas_call(pack_kernel, out_shape=(jax.ShapeDtypeStruct((144, 512), B...]
  transfers between devices with their start and end apart: 25 -> 25, of which waited for: 10 -> 10; matrix products, arithmetic and copies ran while one was open for 3% -> 3% of each run, Pallas kernels for 1% -> 0%
where the time goes in v2:
time: 219 us; the launch traced here: 217 us
  starting transfers between devices  102 us (47%)
  waiting for transfers between devices  46 us (21%)
  Pallas kernels  34.9 us (16%)
  blocking collectives  21.8 us (10%)
  local copies, waits for them, and re-layouts  7.91 us (4%)
  other arithmetic  3.63 us (2%)
    ppermute x8, starting transfers between devices, send(): lax.ppermute(x, ('z', 'c'), [(2 * a + b, 2 * d + e) for (a, b), (d, e) in...  45 us
    all_to_all x4, starting transfers between devices, exchanged(): return lax.all_to_all(x, axis, split_axis=0, concat_axis=0, tiled=True)  26.1 us
    pallas_call x1, Pallas kernels, per_device(): pl.pallas_call(pack_kernel, out_shape=(jax.ShapeDtypeStruct((144, 512), B...  23.6 us
    all_to_all x1, blocking collectives, exchanged(): return lax.all_to_all(x, axis, split_axis=0, concat_axis=0, tiled=True)  21.8 us
    ppermute x1, waiting for transfers between devices, per_device(): w_pair = lax.ppermute(w, 'yl', ring(2, 1))  14.7 us
    ppermute x8, waiting for transfers between devices, send(): lax.ppermute(x, ('z', 'c'), [(2 * a + b, 2 * d + e) for (a, b), (d, e) in...  12.2 us
    all_to_all x4, waiting for transfers between devices, exchanged(): return lax.all_to_all(x, axis, split_axis=0, concat_axis=0, tiled=True)  9.39 us
    ppermute x4, starting transfers between devices, z_pieces(): far = [lax.ppermute(p, 'c', ring(2, 1)) for p in (three, four)]  8.85 us
  transfers between devices with their start and end apart: 25, of which 10 were waited for; matrix products, arithmetic and copies ran while one was open for 3% of the time, Pallas kernels for 0%

profile of v2, /device:TPU:1, one launch (start us, length us, event | category | flops | bytes accessed | tf_op | source)
XLA Modules:
  0.0 217.3 jit_solution(4807923536666539825)
XLA Ops:
  0.6 23.6 %pack.1 = (bf16[144,512]{1,0:T(8,128)(2,1)}, bf16[4,296,256]{2,1,0:T(8,128)(2,1)}) custom-call(bf16[144,256]{1,0:T(8,128)(2,1)} %q.1, bf16[144,128]{1,0:T(8,128)(2,1)} %k.1, bf16[144,128]{1,0:T(8,128)(2,1)} %v.1, bf16[288,256]{1,0:T(8,128)(2,1)} %bitcast.26, bf16[288]{0:T(512)(128)(2,1)} %gain.1), custom_call_target="tpu_custom_call" | custom-call | tf_op jit(solution)/shard_map/pack/pallas_call | solution.py:189
  24.2 7.6 %all-to-all-start = ((bf16[4,296,256]{2,1,0:T(8,128)(2,1)}), bf16[4,296,256]{2,1,0:T(8,128)(2,1)S(1)}, u32[]{:S(2)}, u32[]{:S(2)}) async-start(bf16[4,296,256]{2,1,0:T(8,128)(2,1)} %get-tuple-element.8), calls=%async_computation | async-start | bytes 1212416 | tf_op jit(solution)/shard_map/all_to_all | solution.py:39
  34.1 14.7 %collective-permute-done = bf16[144,512]{1,0:T(8,128)(2,1)S(1)} collective-permute-done((bf16[144,512]{1,0:T(8,128)(2,1)}, bf16[144,512]{1,0:T(8,128)(2,1)S(1)}, u32[]{:S(2)}, u32[]{:S(2)}) %collective-permute-start) | collective-permute-done | bytes 147488 | tf_op jit(solution)/shard_map/ppermute | solution.py:205
  49.7 3.4 %collective-permute-start.1 = (bf16[2,144,512]{2,1,0:T(8,128)(2,1)S(1)}, bf16[2,144,512]{2,1,0:T(8,128)(2,1)S(1)}, u32[]{:S(2)}, u32[]{:S(2)}) collective-permute-start(bf16[2,144,512]{2,1,0:T(8,128)(2,1)S(1)} %get-tuple-element.17), channel_id=1, source_target_pairs={{0,1},{1,0},{2,3},{3,2},{4,5},{5,4},{6,7},{7,6},{8,9},{9,8},{10,11... | collective-permute-start | bytes 884744 | tf_op jit(solution)/shard_map/ppermute | solution.py:23
  54.4 10.7 %collective-permute-start.3 = (bf16[2,2,144,512]{3,2,1,0:T(8,128)(2,1)S(1)}, bf16[2,2,144,512]{3,2,1,0:T(8,128)(2,1)}, u32[]{:S(2)}, u32[]{:S(2)}) collective-permute-start(bf16[2,2,144,512]{3,2,1,0:T(8,128)(2,1)S(1)} %pad_maximum_fusion.refs_0_), channel_id=1, source_target_pairs={{0,4},{1,13},{2,6},{3,15},{4,8},{5,1},{6,10},{7,3},{8,12},{9,5},{1... | collective-permute-start | bytes 1769480 | tf_op jit(solution)/shard_map/ppermute | solution.py:29
  66.7 4.1 %all-to-all-start.1 = ((bf16[4,4,296,256]{3,2,1,0:T(8,128)(2,1)}), bf16[4,4,296,256]{3,2,1,0:T(8,128)(2,1)S(1)}, u32[]{:S(2)}, u32[]{:S(2)}) async-start(bf16[4,4,296,256]{3,2,1,0:T(8,128)(2,1)} %broadcast_in_dim.7), calls=%async_computation.1 | async-start | bytes 4849664 | tf_op jit(solution)/shard_map/all_to_all | solution.py:39
  73.0 5.2 %collective-permute-done.3.refs_2_ = bf16[2,2,144,512]{3,2,1,0:T(8,128)(2,1)} collective-permute-done((bf16[2,2,144,512]{3,2,1,0:T(8,128)(2,1)S(1)}, bf16[2,2,144,512]{3,2,1,0:T(8,128)(2,1)}, u32[]{:S(2)}, u32[]{:S(2)}) %collective-permute-start.3) | collective-permute-done | bytes 589856 | tf_op jit(solution)/shard_map/ppermute | solution.py:29
  78.2 3.2 %collective-permute-start.4 = (bf16[2,2,144,512]{3,2,1,0:T(8,128)(2,1)}, bf16[2,2,144,512]{3,2,1,0:T(8,128)(2,1)}, u32[]{:S(2)}, u32[]{:S(2)}) collective-permute-start(bf16[2,2,144,512]{3,2,1,0:T(8,128)(2,1)} %collective-permute-done.3.refs_2_), channel_id=1, source_target_pairs={{0,2},{1,15},{2,4},{3,1},{4,6},{5,3},{6,8},{7,5},{8,10},{9,7},{10,... | collective-permute-start | bytes 1769480 | tf_op jit(solution)/shard_map/ppermute | solution.py:29
  83.1 4.8 %collective-permute-start.5 = (bf16[2,144,512]{2,1,0:T(8,128)(2,1)}, bf16[2,144,512]{2,1,0:T(8,128)(2,1)}, u32[]{:S(2)}, u32[]{:S(2)}) collective-permute-start(bf16[2,144,512]{2,1,0:T(8,128)(2,1)} %slice_bitcast_fusion), channel_id=1, source_target_pairs={{0,4},{1,13},{2,6},{3,15},{4,8},{5,1},{6,10},{7,3},{8,12},{9,5},{1... | collective-permute-start | bytes 884744 | tf_op jit(solution)/shard_map/ppermute | solution.py:29
  89.9 2.4 %collective-permute-start.6 = (bf16[2,2,144,512]{3,2,1,0:T(8,128)(2,1)}, bf16[2,2,144,512]{3,2,1,0:T(8,128)(2,1)}, u32[]{:S(2)}, u32[]{:S(2)}) collective-permute-start(bf16[2,2,144,512]{3,2,1,0:T(8,128)(2,1)} %collective-permute-done.2.refs_1_), channel_id=1, source_target_pairs={{0,1},{1,0},{2,3},{3,2},{4,5},{5,4},{6,7},{7,6},{8,9},{9,8},{10,11... | collective-permute-start | bytes 1769480 | tf_op jit(solution)/shard_map/ppermute | solution.py:33
  101.1 5.1 %attend.1 = bf16[4,256,256]{2,1,0:T(8,128)(2,1)S(1)} custom-call(s32[3]{0:T(128)S(1)} %pad_add_fusion.pos, bf16[256,4608]{1,0:T(8,128)(2,1)S(1)} %get-tuple-element.9.normed, f32[256,64]{1,0:T(8,128)S(1)} %get-tuple-element.23.cos, f32[256,64]{1,0:T(8,128)S(1)} %get-tuple-element.22.sin, f32[256,256]{1,0:T(8,128)S(1)} %fusion.1.mask, ...), custom_call_target="tpu_custom_call" | custom-call | tf_op jit(solution)/shard_map/attend/pallas_call | solution.py:241
  106.2 21.8 %all_to_all.25 = bf16[4,256,256]{2,1,0:T(8,128)(2,1)S(1)} all-to-all(bf16[4,256,256]{2,1,0:T(8,128)(2,1)S(1)} %attend.1), channel_id=1, replica_groups=mesh['hx'=4,'hy'=4,'yl'=2,'z'=8,'c'=2] {'hx'}, dimensions={0} | all-to-all | bytes 1048576 | tf_op jit(solution)/shard_map/all_to_all | solution.py:39
  129.5 4.1 %all-to-all-start.3 = ((bf16[4,4,256,256]{3,2,1,0:T(8,128)(2,1)}), bf16[4,4,256,256]{3,2,1,0:T(8,128)(2,1)S(1)}, u32[]{:S(2)}, u32[]{:S(2)}) async-start(bf16[4,4,256,256]{3,2,1,0:T(8,128)(2,1)} %broadcast_in_dim.8), calls=%async_computation.3 | async-start | bytes 4194304 | tf_op jit(solution)/shard_map/all_to_all | solution.py:39
  136.2 6.4 %collective-permute-done.11 = bf16[144,256]{1,0:T(8,128)(2,1)S(1)} collective-permute-done((bf16[144,256]{1,0:T(8,128)(2,1)S(1)}, bf16[144,256]{1,0:T(8,128)(2,1)S(1)}, u32[]{:S(2)}, u32[]{:S(2)}) %collective-permute-start.11) | collective-permute-done | bytes 73760 | tf_op jit(solution)/shard_map/ppermute | solution.py:229
  142.7 5.1 %collective-permute-start.12 = (bf16[2,144,256]{2,1,0:T(8,128)(2,1)S(1)}, bf16[2,144,256]{2,1,0:T(8,128)(2,1)S(1)}, u32[]{:S(2)}, u32[]{:S(2)}) collective-permute-start(bf16[2,144,256]{2,1,0:T(8,128)(2,1)S(1)} %get-tuple-element.19), channel_id=1, source_target_pairs={{0,1},{1,0},{2,3},{3,2},{4,5},{5,4},{6,7},{7,6},{8,9},{9,8},{10,11... | collective-permute-start | bytes 442376 | tf_op jit(solution)/shard_map/ppermute | solution.py:23
  148.8 14.3 %collective-permute-start.14 = (bf16[2,2,144,256]{3,2,1,0:T(8,128)(2,1)S(1)}, bf16[2,2,144,256]{3,2,1,0:T(8,128)(2,1)S(1)}, u32[]{:S(2)}, u32[]{:S(2)}) collective-permute-start(bf16[2,2,144,256]{3,2,1,0:T(8,128)(2,1)S(1)} %pad_maximum_fusion.2.refs_0_), channel_id=1, source_target_pairs={{0,4},{1,13},{2,6},{3,15},{4,8},{5,1},{6,10},{7,3},{8,12},{9,5},{1... | collective-permute-start | bytes 884744 | tf_op jit(solution)/shard_map/ppermute | solution.py:29
  165.1 4.9 %collective-permute-done.14.refs_2_ = bf16[2,2,144,256]{3,2,1,0:T(8,128)(2,1)S(1)} collective-permute-done((bf16[2,2,144,256]{3,2,1,0:T(8,128)(2,1)S(1)}, bf16[2,2,144,256]{3,2,1,0:T(8,128)(2,1)S(1)}, u32[]{:S(2)}, u32[]{:S(2)}) %collective-permute-start.14) | collective-permute-done | bytes 294944 | tf_op jit(solution)/shard_map/ppermute | solution.py:29
  170.0 2.8 %collective-permute-start.15 = (bf16[2,2,144,256]{3,2,1,0:T(8,128)(2,1)S(1)}, bf16[2,2,144,256]{3,2,1,0:T(8,128)(2,1)S(1)}, u32[]{:S(2)}, u32[]{:S(2)}) collective-permute-start(bf16[2,2,144,256]{3,2,1,0:T(8,128)(2,1)S(1)} %collective-permute-done.14.refs_2_), channel_id=1, source_target_pairs={{0,2},{1,15},{2,4},{3,1},{4,6},{5,3},{6,8},{7,5},{8,10},{9,7},{10,... | collective-permute-start | bytes 884744 | tf_op jit(solution)/shard_map/ppermute | solution.py:29
  172.8 5.2 %collective-permute-start.16 = (bf16[2,144,256]{2,1,0:T(8,128)(2,1)S(1)}, bf16[2,144,256]{2,1,0:T(8,128)(2,1)S(1)}, u32[]{:S(2)}, u32[]{:S(2)}) collective-permute-start(bf16[2,144,256]{2,1,0:T(8,128)(2,1)S(1)} %slice_bitcast_fusion.1), channel_id=1, source_target_pairs={{0,4},{1,13},{2,6},{3,15},{4,8},{5,1},{6,10},{7,3},{8,12},{9,5},{1... | collective-permute-start | bytes 442376 | tf_op jit(solution)/shard_map/ppermute | solution.py:29
  179.9 2.4 %collective-permute-start.18 = (bf16[2,2,144,256]{3,2,1,0:T(8,128)(2,1)S(1)}, bf16[2,2,144,256]{3,2,1,0:T(8,128)(2,1)S(1)}, u32[]{:S(2)}, u32[]{:S(2)}) collective-permute-start(bf16[2,2,144,256]{3,2,1,0:T(8,128)(2,1)S(1)} %collective-permute-done.14.refs_2_), channel_id=1, source_target_pairs={{0,1},{1,0},{2,3},{3,2},{4,5},{5,4},{6,7},{7,6},{8,9},{9,8},{10,11... | collective-permute-start | bytes 884744 | tf_op jit(solution)/shard_map/ppermute | solution.py:33
  182.3 2.8 %collective-permute-start.19 = (bf16[2,2,144,256]{3,2,1,0:T(8,128)(2,1)S(1)}, bf16[2,2,144,256]{3,2,1,0:T(8,128)(2,1)}, u32[]{:S(2)}, u32[]{:S(2)}) collective-permute-start(bf16[2,2,144,256]{3,2,1,0:T(8,128)(2,1)S(1)} %collective-permute-done.15.refs_3_), channel_id=1, source_target_pairs={{0,1},{1,0},{2,3},{3,2},{4,5},{5,4},{6,7},{7,6},{8,9},{9,8},{10,11... | collective-permute-start | bytes 884744 | tf_op jit(solution)/shard_map/ppermute | solution.py:34
  190.7 5.2 %project_out.1 = (f32[288,256]{1,0:T(8,128)}, f32[16,8,256]{2,1,0:T(8,128)}) custom-call(s32[3]{0:T(128)} %copy-done, bf16[288,256]{1,0:T(8,128)(2,1)} %bitcast.27, f32[288,1]{1,0:T(8,128)} %broadcast_in_dim.9.gain, bf16[4,4,256,256]{3,2,1,0:T(8,128)(2,1)} %copy-done.1, bf16[2,2,144,256]{3,2,1,0:T(8,128)(2,1)} %copy-done.3, ...), custom_call_target="tpu_custom_call" | custom-call | tf_op jit(solution)/shard_map/project_out/pallas_call | solution.py:260
  195.9 10.2 %all-to-all-start.4 = ((f32[16,8,256]{2,1,0:T(8,128)}), f32[16,8,256]{2,1,0:T(8,128)S(1)}, u32[]{:S(2)}, u32[]{:S(2)}) async-start(f32[16,8,256]{2,1,0:T(8,128)} %get-tuple-element.12), calls=%async_computation.4 | async-start | bytes 262144 | tf_op jit(solution)/shard_map/all_to_all | solution.py:39
  206.1 9.4 %all-to-all-done.4 = f32[16,8,256]{2,1,0:T(8,128)S(1)} async-done(((f32[16,8,256]{2,1,0:T(8,128)}), f32[16,8,256]{2,1,0:T(8,128)S(1)}, u32[]{:S(2)}, u32[]{:S(2)}) %all-to-all-start.4) | async-done | bytes 131104 | tf_op jit(solution)/shard_map/all_to_all | solution.py:39
  (80 shorter events, 36.9 us)
Async XLA Ops:
  24.2 40.9 %all-to-all-start = ((bf16[4,296,256]{2,1,0:T(8,128)(2,1)}), bf16[4,296,256]{2,1,0:T(8,128)(2,1)S(1)}, u32[]{:S(2)}, u32[]{:S(2)}) async-start(bf16[4,296,256]{2,1,0:T(8,128)(2,1)} %get-tuple-element.8), calls=%async_computation | async-start | bytes 1212416 | tf_op jit(solution)/shard_map/all_to_all | solution.py:39
  31.8 17.0 %collective-permute-start = (bf16[144,512]{1,0:T(8,128)(2,1)}, bf16[144,512]{1,0:T(8,128)(2,1)S(1)}, u32[]{:S(2)}, u32[]{:S(2)}) collective-permute-start(bf16[144,512]{1,0:T(8,128)(2,1)} %get-tuple-element.10), channel_id=1, source_target_pairs={{0,16},{16,0},{1,17},{17,1},{2,18},{18,2},{3,19},{19,3},{4,20},{20... | collective-permute-start | bytes 442376 | tf_op jit(solution)/shard_map/ppermute | solution.py:205
  49.7 4.6 %collective-permute-start.1 = (bf16[2,144,512]{2,1,0:T(8,128)(2,1)S(1)}, bf16[2,144,512]{2,1,0:T(8,128)(2,1)S(1)}, u32[]{:S(2)}, u32[]{:S(2)}) collective-permute-start(bf16[2,144,512]{2,1,0:T(8,128)(2,1)S(1)} %get-tuple-element.17), channel_id=1, source_target_pairs={{0,1},{1,0},{2,3},{3,2},{4,5},{5,4},{6,7},{7,6},{8,9},{9,8},{10,11... | collective-permute-start | bytes 884744 | tf_op jit(solution)/shard_map/ppermute | solution.py:23
  54.4 23.8 %collective-permute-start.3 = (bf16[2,2,144,512]{3,2,1,0:T(8,128)(2,1)S(1)}, bf16[2,2,144,512]{3,2,1,0:T(8,128)(2,1)}, u32[]{:S(2)}, u32[]{:S(2)}) collective-permute-start(bf16[2,2,144,512]{3,2,1,0:T(8,128)(2,1)S(1)} %pad_maximum_fusion.refs_0_), channel_id=1, source_target_pairs={{0,4},{1,13},{2,6},{3,15},{4,8},{5,1},{6,10},{7,3},{8,12},{9,5},{1... | collective-permute-start | bytes 1769480 | tf_op jit(solution)/shard_map/ppermute | solution.py:29
  66.7 32.7 %all-to-all-start.1 = ((bf16[4,4,296,256]{3,2,1,0:T(8,128)(2,1)}), bf16[4,4,296,256]{3,2,1,0:T(8,128)(2,1)S(1)}, u32[]{:S(2)}, u32[]{:S(2)}) async-start(bf16[4,4,296,256]{3,2,1,0:T(8,128)(2,1)} %broadcast_in_dim.7), calls=%async_computation.1 | async-start | bytes 4849664 | tf_op jit(solution)/shard_map/all_to_all | solution.py:39
  70.8 19.1 %collective-permute-start.2 = (bf16[2,2,144,512]{3,2,1,0:T(8,128)(2,1)S(1)}, bf16[2,2,144,512]{3,2,1,0:T(8,128)(2,1)}, u32[]{:S(2)}, u32[]{:S(2)}) collective-permute-start(bf16[2,2,144,512]{3,2,1,0:T(8,128)(2,1)S(1)} %pad_maximum_fusion.refs_0_), channel_id=1, source_target_pairs={{0,2},{1,15},{2,4},{3,1},{4,6},{5,3},{6,8},{7,5},{8,10},{9,7},{10,... | collective-permute-start | bytes 1769480 | tf_op jit(solution)/shard_map/ppermute | solution.py:29
  78.2 14.1 %collective-permute-start.4 = (bf16[2,2,144,512]{3,2,1,0:T(8,128)(2,1)}, bf16[2,2,144,512]{3,2,1,0:T(8,128)(2,1)}, u32[]{:S(2)}, u32[]{:S(2)}) collective-permute-start(bf16[2,2,144,512]{3,2,1,0:T(8,128)(2,1)} %collective-permute-done.3.refs_2_), channel_id=1, source_target_pairs={{0,2},{1,15},{2,4},{3,1},{4,6},{5,3},{6,8},{7,5},{8,10},{9,7},{10,... | collective-permute-start | bytes 1769480 | tf_op jit(solution)/shard_map/ppermute | solution.py:29
  83.1 14.1 %collective-permute-start.5 = (bf16[2,144,512]{2,1,0:T(8,128)(2,1)}, bf16[2,144,512]{2,1,0:T(8,128)(2,1)}, u32[]{:S(2)}, u32[]{:S(2)}) collective-permute-start(bf16[2,144,512]{2,1,0:T(8,128)(2,1)} %slice_bitcast_fusion), channel_id=1, source_target_pairs={{0,4},{1,13},{2,6},{3,15},{4,8},{5,1},{6,10},{7,3},{8,12},{9,5},{1... | collective-permute-start | bytes 884744 | tf_op jit(solution)/shard_map/ppermute | solution.py:29
  88.0 12.5 %collective-permute-start.7 = (bf16[2,2,144,512]{3,2,1,0:T(8,128)(2,1)}, bf16[2,2,144,512]{3,2,1,0:T(8,128)(2,1)}, u32[]{:S(2)}, u32[]{:S(2)}) collective-permute-start(bf16[2,2,144,512]{3,2,1,0:T(8,128)(2,1)} %collective-permute-done.3.refs_2_), channel_id=1, source_target_pairs={{0,1},{1,0},{2,3},{3,2},{4,5},{5,4},{6,7},{7,6},{8,9},{9,8},{10,11... | collective-permute-start | bytes 1769480 | tf_op jit(solution)/shard_map/ppermute | solution.py:33
  89.9 10.5 %collective-permute-start.6 = (bf16[2,2,144,512]{3,2,1,0:T(8,128)(2,1)}, bf16[2,2,144,512]{3,2,1,0:T(8,128)(2,1)}, u32[]{:S(2)}, u32[]{:S(2)}) collective-permute-start(bf16[2,2,144,512]{3,2,1,0:T(8,128)(2,1)} %collective-permute-done.2.refs_1_), channel_id=1, source_target_pairs={{0,1},{1,0},{2,3},{3,2},{4,5},{5,4},{6,7},{7,6},{8,9},{9,8},{10,11... | collective-permute-start | bytes 1769480 | tf_op jit(solution)/shard_map/ppermute | solution.py:33
  92.3 8.7 %collective-permute-start.8 = (bf16[2,2,144,512]{3,2,1,0:T(8,128)(2,1)}, bf16[2,2,144,512]{3,2,1,0:T(8,128)(2,1)}, u32[]{:S(2)}, u32[]{:S(2)}) collective-permute-start(bf16[2,2,144,512]{3,2,1,0:T(8,128)(2,1)} %collective-permute-done.4.refs_3_), channel_id=1, source_target_pairs={{0,1},{1,0},{2,3},{3,2},{4,5},{5,4},{6,7},{7,6},{8,9},{9,8},{10,11... | collective-permute-start | bytes 1769480 | tf_op jit(solution)/shard_map/ppermute | solution.py:34
  97.2 3.8 %collective-permute-start.9 = (bf16[2,144,512]{2,1,0:T(8,128)(2,1)}, bf16[2,144,512]{2,1,0:T(8,128)(2,1)}, u32[]{:S(2)}, u32[]{:S(2)}) collective-permute-start(bf16[2,144,512]{2,1,0:T(8,128)(2,1)} %collective-permute-done.5.refs_4_), channel_id=1, source_target_pairs={{0,1},{1,0},{2,3},{3,2},{4,5},{5,4},{6,7},{7,6},{8,9},{9,8},{10,11... | collective-permute-start | bytes 884744 | tf_op jit(solution)/shard_map/ppermute | solution.py:34
  129.5 59.8 %all-to-all-start.3 = ((bf16[4,4,256,256]{3,2,1,0:T(8,128)(2,1)}), bf16[4,4,256,256]{3,2,1,0:T(8,128)(2,1)S(1)}, u32[]{:S(2)}, u32[]{:S(2)}) async-start(bf16[4,4,256,256]{3,2,1,0:T(8,128)(2,1)} %broadcast_in_dim.8), calls=%async_computation.3 | async-start | bytes 4194304 | tf_op jit(solution)/shard_map/all_to_all | solution.py:39
  133.7 9.0 %collective-permute-start.11 = (bf16[144,256]{1,0:T(8,128)(2,1)S(1)}, bf16[144,256]{1,0:T(8,128)(2,1)S(1)}, u32[]{:S(2)}, u32[]{:S(2)}) collective-permute-start(bf16[144,256]{1,0:T(8,128)(2,1)S(1)} %bitcast.37), channel_id=1, source_target_pairs={{0,16},{1,17},{2,48},{3,49},{4,80},{5,81},{6,112},{7,113},{8,144},... | collective-permute-start | bytes 221192 | tf_op jit(solution)/shard_map/ppermute | solution.py:229
  135.6 7.1 %collective-permute-start.10 = (bf16[144,256]{1,0:T(8,128)(2,1)S(1)}, bf16[144,256]{1,0:T(8,128)(2,1)S(1)}, u32[]{:S(2)}, u32[]{:S(2)}) collective-permute-start(bf16[144,256]{1,0:T(8,128)(2,1)S(1)} %bitcast.38), channel_id=1, source_target_pairs={{0,0},{1,1},{2,32},{3,33},{4,64},{5,65},{6,96},{7,97},{8,128},{9,1... | collective-permute-start | bytes 221192 | tf_op jit(solution)/shard_map/ppermute | solution.py:229
  142.7 6.1 %collective-permute-start.12 = (bf16[2,144,256]{2,1,0:T(8,128)(2,1)S(1)}, bf16[2,144,256]{2,1,0:T(8,128)(2,1)S(1)}, u32[]{:S(2)}, u32[]{:S(2)}) collective-permute-start(bf16[2,144,256]{2,1,0:T(8,128)(2,1)S(1)} %get-tuple-element.19), channel_id=1, source_target_pairs={{0,1},{1,0},{2,3},{3,2},{4,5},{5,4},{6,7},{7,6},{8,9},{9,8},{10,11... | collective-permute-start | bytes 442376 | tf_op jit(solution)/shard_map/ppermute | solution.py:23
  148.8 21.1 %collective-permute-start.14 = (bf16[2,2,144,256]{3,2,1,0:T(8,128)(2,1)S(1)}, bf16[2,2,144,256]{3,2,1,0:T(8,128)(2,1)S(1)}, u32[]{:S(2)}, u32[]{:S(2)}) collective-permute-start(bf16[2,2,144,256]{3,2,1,0:T(8,128)(2,1)S(1)} %pad_maximum_fusion.2.refs_0_), channel_id=1, source_target_pairs={{0,4},{1,13},{2,6},{3,15},{4,8},{5,1},{6,10},{7,3},{8,12},{9,5},{1... | collective-permute-start | bytes 884744 | tf_op jit(solution)/shard_map/ppermute | solution.py:29
  163.2 14.8 %collective-permute-start.13 = (bf16[2,2,144,256]{3,2,1,0:T(8,128)(2,1)S(1)}, bf16[2,2,144,256]{3,2,1,0:T(8,128)(2,1)S(1)}, u32[]{:S(2)}, u32[]{:S(2)}) collective-permute-start(bf16[2,2,144,256]{3,2,1,0:T(8,128)(2,1)S(1)} %pad_maximum_fusion.2.refs_0_), channel_id=1, source_target_pairs={{0,2},{1,15},{2,4},{3,1},{4,6},{5,3},{6,8},{7,5},{8,10},{9,7},{10,... | collective-permute-start | bytes 884744 | tf_op jit(solution)/shard_map/ppermute | solution.py:29
  170.0 12.3 %collective-permute-start.15 = (bf16[2,2,144,256]{3,2,1,0:T(8,128)(2,1)S(1)}, bf16[2,2,144,256]{3,2,1,0:T(8,128)(2,1)S(1)}, u32[]{:S(2)}, u32[]{:S(2)}) collective-permute-start(bf16[2,2,144,256]{3,2,1,0:T(8,128)(2,1)S(1)} %collective-permute-done.14.refs_2_), channel_id=1, source_target_pairs={{0,2},{1,15},{2,4},{3,1},{4,6},{5,3},{6,8},{7,5},{8,10},{9,7},{10,... | collective-permute-start | bytes 884744 | tf_op jit(solution)/shard_map/ppermute | solution.py:29
  172.8 12.3 %collective-permute-start.16 = (bf16[2,144,256]{2,1,0:T(8,128)(2,1)S(1)}, bf16[2,144,256]{2,1,0:T(8,128)(2,1)S(1)}, u32[]{:S(2)}, u32[]{:S(2)}) collective-permute-start(bf16[2,144,256]{2,1,0:T(8,128)(2,1)S(1)} %slice_bitcast_fusion.1), channel_id=1, source_target_pairs={{0,4},{1,13},{2,6},{3,15},{4,8},{5,1},{6,10},{7,3},{8,12},{9,5},{1... | collective-permute-start | bytes 442376 | tf_op jit(solution)/shard_map/ppermute | solution.py:29
  178.0 9.9 %collective-permute-start.17 = (bf16[2,2,144,256]{3,2,1,0:T(8,128)(2,1)S(1)}, bf16[2,2,144,256]{3,2,1,0:T(8,128)(2,1)S(1)}, u32[]{:S(2)}, u32[]{:S(2)}) collective-permute-start(bf16[2,2,144,256]{3,2,1,0:T(8,128)(2,1)S(1)} %collective-permute-done.13.refs_1_), channel_id=1, source_target_pairs={{0,1},{1,0},{2,3},{3,2},{4,5},{5,4},{6,7},{7,6},{8,9},{9,8},{10,11... | collective-permute-start | bytes 884744 | tf_op jit(solution)/shard_map/ppermute | solution.py:33
  179.9 8.0 %collective-permute-start.18 = (bf16[2,2,144,256]{3,2,1,0:T(8,128)(2,1)S(1)}, bf16[2,2,144,256]{3,2,1,0:T(8,128)(2,1)S(1)}, u32[]{:S(2)}, u32[]{:S(2)}) collective-permute-start(bf16[2,2,144,256]{3,2,1,0:T(8,128)(2,1)S(1)} %collective-permute-done.14.refs_2_), channel_id=1, source_target_pairs={{0,1},{1,0},{2,3},{3,2},{4,5},{5,4},{6,7},{7,6},{8,9},{9,8},{10,11... | collective-permute-start | bytes 884744 | tf_op jit(solution)/shard_map/ppermute | solution.py:33
  182.3 7.0 %collective-permute-start.19 = (bf16[2,2,144,256]{3,2,1,0:T(8,128)(2,1)S(1)}, bf16[2,2,144,256]{3,2,1,0:T(8,128)(2,1)}, u32[]{:S(2)}, u32[]{:S(2)}) collective-permute-start(bf16[2,2,144,256]{3,2,1,0:T(8,128)(2,1)S(1)} %collective-permute-done.15.refs_3_), channel_id=1, source_target_pairs={{0,1},{1,0},{2,3},{3,2},{4,5},{5,4},{6,7},{7,6},{8,9},{9,8},{10,11... | collective-permute-start | bytes 884744 | tf_op jit(solution)/shard_map/ppermute | solution.py:34
  195.9 19.6 %all-to-all-start.4 = ((f32[16,8,256]{2,1,0:T(8,128)}), f32[16,8,256]{2,1,0:T(8,128)S(1)}, u32[]{:S(2)}, u32[]{:S(2)}) async-start(f32[16,8,256]{2,1,0:T(8,128)} %get-tuple-element.12), calls=%async_computation.4 | async-start | bytes 262144 | tf_op jit(solution)/shard_map/all_to_all | solution.py:39
  (16 other events, 235.4 us)

commit v3 on v2

--- a/solution.py
+++ b/solution.py
@@ -39,26 +39,27 @@
     return lax.all_to_all(x, axis, split_axis=0, concat_axis=0, tiled=True)
 
 
-def pack_kernel(q, k, v, x, gain, w, packed, g, last, sems):
+def pack_kernel(q, k, v, x, gain, w, packed, g, sems):
     get = pltpu.make_async_copy(gain, g, sems.at[0])
     moves = [
         pltpu.make_async_copy(q, w.at[:, pl.ds(0, 256)], sems.at[1]),
         pltpu.make_async_copy(k, w.at[:, pl.ds(256, 128)], sems.at[2]),
         pltpu.make_async_copy(v, w.at[:, pl.ds(384, 128)], sems.at[3]),
+        pltpu.make_async_copy(x, packed.at[0, pl.ds(0, 288)], sems.at[4]),
     ]
-    moves += [pltpu.make_async_copy(x, packed.at[i, pl.ds(0, 288)], sems.at[4 + i]) for i in range(4)]
     get.start()
     for m in moves:
         m.start()
     get.wait()
     row = g[...].astype(F32).reshape(1, 288)
     tail = jnp.concatenate([row[:, 256:], jnp.zeros((1, 224), F32)], axis=1)
-    last[...] = jnp.concatenate([row[:, :256], tail, jnp.zeros((6, 256), F32)], axis=0).astype(BF)
-    ends = [pltpu.make_async_copy(last, packed.at[i, pl.ds(288, 8)], sems.at[8 + i]) for i in range(4)]
-    for m in ends:
-        m.start()
-    for m in moves + ends:
+    last = jnp.concatenate([row[:, :256], tail, jnp.zeros((6, 256), F32)], axis=0).astype(BF)
+    for i in range(4):
+        packed[i, 288:] = last
+    for m in moves:
         m.wait()
+    for i in range(1, 4):
+        packed[i, :288] = packed[0, :288]
 
 
 def norm_kernel(stream, normed, first):
@@ -193,12 +194,8 @@
             jax.ShapeDtypeStruct((4, 296, rows), BF),
         ),
         in_specs=[HBM] * 5,
-        out_specs=(HBM, HBM),
-        scratch_shapes=[
-            pltpu.VMEM((288,), BF),
-            pltpu.VMEM((8, 256), BF),
-            pltpu.SemaphoreType.DMA((12,)),
-        ],
+        out_specs=(VMEM, VMEM),
+        scratch_shapes=[pltpu.VMEM((288,), BF), pltpu.SemaphoreType.DMA((5,))],
         compiler_params=params(60),
         name="pack",
     )(query_weight, key_weight, value_weight, x_t, before_gain)
@@ -302,4 +299,6 @@
     )
     out_specs = (P(tok, hid), P(tok, hid))
 
-    return jax.shard_map(per_device, mesh=fine, in_specs=in_specs, out_specs=out_specs, check_vma=False)
+    return jax.shard_map(
+        per_device, mesh=fine, in_specs=in_specs, out_specs=out_specs, check_vma=False
+    )

time: 219 us -> 197 us (0.90)
  Pallas kernels: 34.9 us -> 13.2 us
    pallas_call x1, Pallas kernels: 23.6 us -> 1.93 us  [per_device(): pl.pallas_call(pack_kernel, out_shape=(jax.ShapeDtypeStruct((144, 512), B...]
  transfers between devices with their start and end apart: 25 -> 25, of which waited for: 10 -> 10; matrix products, arithmetic and copies ran while one was open for 3% -> 3% of each run, Pallas kernels for 0% -> 1%
where the time goes in v3:
time: 197 us; the launch traced here: 196 us
  starting transfers between devices  102 us (52%)
  waiting for transfers between devices  46 us (23%)
  blocking collectives  21.8 us (11%)
  Pallas kernels  13.2 us (7%)
  local copies, waits for them, and re-layouts  7.91 us (4%)
  other arithmetic  3.63 us (2%)
    ppermute x8, starting transfers between devices, send(): lax.ppermute(x, ('z', 'c'), [(2 * a + b, 2 * d + e) for (a, b), (d, e) in...  45 us
    all_to_all x4, starting transfers between devices, exchanged(): return lax.all_to_all(x, axis, split_axis=0, concat_axis=0, tiled=True)  26.1 us
    all_to_all x1, blocking collectives, exchanged(): return lax.all_to_all(x, axis, split_axis=0, concat_axis=0, tiled=True)  21.8 us
    ppermute x1, waiting for transfers between devices, per_device(): w_pair = lax.ppermute(w, 'yl', ring(2, 1))  14.7 us
    ppermute x8, waiting for transfers between devices, send(): lax.ppermute(x, ('z', 'c'), [(2 * a + b, 2 * d + e) for (a, b), (d, e) in...  12.2 us
    all_to_all x4, waiting for transfers between devices, exchanged(): return lax.all_to_all(x, axis, split_axis=0, concat_axis=0, tiled=True)  9.39 us
    ppermute x4, starting transfers between devices, z_pieces(): far = [lax.ppermute(p, 'c', ring(2, 1)) for p in (three, four)]  8.85 us
    ppermute x4, starting transfers between devices, z_pieces(): near = [lax.ppermute(p, 'c', ring(2, 1)) for p in (one, two)]  8.66 us
  transfers between devices with their start and end apart: 25, of which 10 were waited for; matrix products, arithmetic and copies ran while one was open for 3% of the time, Pallas kernels for 1%

profile of v3, /device:TPU:1, one launch (start us, length us, event | category | flops | bytes accessed | tf_op | source)
XLA Modules:
  0.0 195.7 jit_solution(6888911123383734350)
XLA Ops:
  2.6 7.6 %all-to-all-start = ((bf16[4,296,256]{2,1,0:T(8,128)(2,1)}), bf16[4,296,256]{2,1,0:T(8,128)(2,1)S(1)}, u32[]{:S(2)}, u32[]{:S(2)}) async-start(bf16[4,296,256]{2,1,0:T(8,128)(2,1)} %get-tuple-element.8), calls=%async_computation | async-start | bytes 1212416 | tf_op jit(solution)/shard_map/all_to_all | solution.py:39
  10.2 2.3 %collective-permute-start = (bf16[144,512]{1,0:T(8,128)(2,1)}, bf16[144,512]{1,0:T(8,128)(2,1)S(1)}, u32[]{:S(2)}, u32[]{:S(2)}) collective-permute-start(bf16[144,512]{1,0:T(8,128)(2,1)} %get-tuple-element.10), channel_id=1, source_target_pairs={{0,16},{16,0},{1,17},{17,1},{2,18},{18,2},{3,19},{19,3},{4,20},{20... | collective-permute-start | bytes 442376 | tf_op jit(solution)/shard_map/ppermute | solution.py:202
  12.5 14.7 %collective-permute-done = bf16[144,512]{1,0:T(8,128)(2,1)S(1)} collective-permute-done((bf16[144,512]{1,0:T(8,128)(2,1)}, bf16[144,512]{1,0:T(8,128)(2,1)S(1)}, u32[]{:S(2)}, u32[]{:S(2)}) %collective-permute-start) | collective-permute-done | bytes 147488 | tf_op jit(solution)/shard_map/ppermute | solution.py:202
  28.1 3.4 %collective-permute-start.1 = (bf16[2,144,512]{2,1,0:T(8,128)(2,1)S(1)}, bf16[2,144,512]{2,1,0:T(8,128)(2,1)S(1)}, u32[]{:S(2)}, u32[]{:S(2)}) collective-permute-start(bf16[2,144,512]{2,1,0:T(8,128)(2,1)S(1)} %get-tuple-element.17), channel_id=1, source_target_pairs={{0,1},{1,0},{2,3},{3,2},{4,5},{5,4},{6,7},{7,6},{8,9},{9,8},{10,11... | collective-permute-start | bytes 884744 | tf_op jit(solution)/shard_map/ppermute | solution.py:23
  32.8 10.7 %collective-permute-start.3 = (bf16[2,2,144,512]{3,2,1,0:T(8,128)(2,1)S(1)}, bf16[2,2,144,512]{3,2,1,0:T(8,128)(2,1)}, u32[]{:S(2)}, u32[]{:S(2)}) collective-permute-start(bf16[2,2,144,512]{3,2,1,0:T(8,128)(2,1)S(1)} %pad_maximum_fusion.refs_0_), channel_id=1, source_target_pairs={{0,4},{1,13},{2,6},{3,15},{4,8},{5,1},{6,10},{7,3},{8,12},{9,5},{1... | collective-permute-start | bytes 1769480 | tf_op jit(solution)/shard_map/ppermute | solution.py:29
  45.0 4.1 %all-to-all-start.1 = ((bf16[4,4,296,256]{3,2,1,0:T(8,128)(2,1)}), bf16[4,4,296,256]{3,2,1,0:T(8,128)(2,1)S(1)}, u32[]{:S(2)}, u32[]{:S(2)}) async-start(bf16[4,4,296,256]{3,2,1,0:T(8,128)(2,1)} %broadcast_in_dim.7), calls=%async_computation.1 | async-start | bytes 4849664 | tf_op jit(solution)/shard_map/all_to_all | solution.py:39
  51.4 5.2 %collective-permute-done.3.refs_2_ = bf16[2,2,144,512]{3,2,1,0:T(8,128)(2,1)} collective-permute-done((bf16[2,2,144,512]{3,2,1,0:T(8,128)(2,1)S(1)}, bf16[2,2,144,512]{3,2,1,0:T(8,128)(2,1)}, u32[]{:S(2)}, u32[]{:S(2)}) %collective-permute-start.3) | collective-permute-done | bytes 589856 | tf_op jit(solution)/shard_map/ppermute | solution.py:29
  56.6 3.2 %collective-permute-start.4 = (bf16[2,2,144,512]{3,2,1,0:T(8,128)(2,1)}, bf16[2,2,144,512]{3,2,1,0:T(8,128)(2,1)}, u32[]{:S(2)}, u32[]{:S(2)}) collective-permute-start(bf16[2,2,144,512]{3,2,1,0:T(8,128)(2,1)} %collective-permute-done.3.refs_2_), channel_id=1, source_target_pairs={{0,2},{1,15},{2,4},{3,1},{4,6},{5,3},{6,8},{7,5},{8,10},{9,7},{10,... | collective-permute-start | bytes 1769480 | tf_op jit(solution)/shard_map/ppermute | solution.py:29
  61.5 4.8 %collective-permute-start.5 = (bf16[2,144,512]{2,1,0:T(8,128)(2,1)}, bf16[2,144,512]{2,1,0:T(8,128)(2,1)}, u32[]{:S(2)}, u32[]{:S(2)}) collective-permute-start(bf16[2,144,512]{2,1,0:T(8,128)(2,1)} %slice_bitcast_fusion), channel_id=1, source_target_pairs={{0,4},{1,13},{2,6},{3,15},{4,8},{5,1},{6,10},{7,3},{8,12},{9,5},{1... | collective-permute-start | bytes 884744 | tf_op jit(solution)/shard_map/ppermute | solution.py:29
  68.3 2.4 %collective-permute-start.6 = (bf16[2,2,144,512]{3,2,1,0:T(8,128)(2,1)}, bf16[2,2,144,512]{3,2,1,0:T(8,128)(2,1)}, u32[]{:S(2)}, u32[]{:S(2)}) collective-permute-start(bf16[2,2,144,512]{3,2,1,0:T(8,128)(2,1)} %collective-permute-done.2.refs_1_), channel_id=1, source_target_pairs={{0,1},{1,0},{2,3},{3,2},{4,5},{5,4},{6,7},{7,6},{8,9},{9,8},{10,11... | collective-permute-start | bytes 1769480 | tf_op jit(solution)/shard_map/ppermute | solution.py:33
  79.4 5.1 %attend.1 = bf16[4,256,256]{2,1,0:T(8,128)(2,1)S(1)} custom-call(s32[3]{0:T(128)S(1)} %pad_add_fusion.pos, bf16[256,4608]{1,0:T(8,128)(2,1)S(1)} %get-tuple-element.9.normed, f32[256,64]{1,0:T(8,128)S(1)} %get-tuple-element.23.cos, f32[256,64]{1,0:T(8,128)S(1)} %get-tuple-element.22.sin, f32[256,256]{1,0:T(8,128)S(1)} %fusion.1.mask, ...), custom_call_target="tpu_custom_call" | custom-call | tf_op jit(solution)/shard_map/attend/pallas_call | solution.py:238
  84.5 21.8 %all_to_all.25 = bf16[4,256,256]{2,1,0:T(8,128)(2,1)S(1)} all-to-all(bf16[4,256,256]{2,1,0:T(8,128)(2,1)S(1)} %attend.1), channel_id=1, replica_groups=mesh['hx'=4,'hy'=4,'yl'=2,'z'=8,'c'=2] {'hx'}, dimensions={0} | all-to-all | bytes 1048576 | tf_op jit(solution)/shard_map/all_to_all | solution.py:39
  107.9 4.1 %all-to-all-start.3 = ((bf16[4,4,256,256]{3,2,1,0:T(8,128)(2,1)}), bf16[4,4,256,256]{3,2,1,0:T(8,128)(2,1)S(1)}, u32[]{:S(2)}, u32[]{:S(2)}) async-start(bf16[4,4,256,256]{3,2,1,0:T(8,128)(2,1)} %broadcast_in_dim.8), calls=%async_computation.3 | async-start | bytes 4194304 | tf_op jit(solution)/shard_map/all_to_all | solution.py:39
  114.6 6.4 %collective-permute-done.11 = bf16[144,256]{1,0:T(8,128)(2,1)S(1)} collective-permute-done((bf16[144,256]{1,0:T(8,128)(2,1)S(1)}, bf16[144,256]{1,0:T(8,128)(2,1)S(1)}, u32[]{:S(2)}, u32[]{:S(2)}) %collective-permute-start.11) | collective-permute-done | bytes 73760 | tf_op jit(solution)/shard_map/ppermute | solution.py:226
  121.1 5.1 %collective-permute-start.12 = (bf16[2,144,256]{2,1,0:T(8,128)(2,1)S(1)}, bf16[2,144,256]{2,1,0:T(8,128)(2,1)S(1)}, u32[]{:S(2)}, u32[]{:S(2)}) collective-permute-start(bf16[2,144,256]{2,1,0:T(8,128)(2,1)S(1)} %get-tuple-element.19), channel_id=1, source_target_pairs={{0,1},{1,0},{2,3},{3,2},{4,5},{5,4},{6,7},{7,6},{8,9},{9,8},{10,11... | collective-permute-start | bytes 442376 | tf_op jit(solution)/shard_map/ppermute | solution.py:23
  127.2 14.3 %collective-permute-start.14 = (bf16[2,2,144,256]{3,2,1,0:T(8,128)(2,1)S(1)}, bf16[2,2,144,256]{3,2,1,0:T(8,128)(2,1)S(1)}, u32[]{:S(2)}, u32[]{:S(2)}) collective-permute-start(bf16[2,2,144,256]{3,2,1,0:T(8,128)(2,1)S(1)} %pad_maximum_fusion.2.refs_0_), channel_id=1, source_target_pairs={{0,4},{1,13},{2,6},{3,15},{4,8},{5,1},{6,10},{7,3},{8,12},{9,5},{1... | collective-permute-start | bytes 884744 | tf_op jit(solution)/shard_map/ppermute | solution.py:29
  143.5 4.9 %collective-permute-done.14.refs_2_ = bf16[2,2,144,256]{3,2,1,0:T(8,128)(2,1)S(1)} collective-permute-done((bf16[2,2,144,256]{3,2,1,0:T(8,128)(2,1)S(1)}, bf16[2,2,144,256]{3,2,1,0:T(8,128)(2,1)S(1)}, u32[]{:S(2)}, u32[]{:S(2)}) %collective-permute-start.14) | collective-permute-done | bytes 294944 | tf_op jit(solution)/shard_map/ppermute | solution.py:29
  148.3 2.8 %collective-permute-start.15 = (bf16[2,2,144,256]{3,2,1,0:T(8,128)(2,1)S(1)}, bf16[2,2,144,256]{3,2,1,0:T(8,128)(2,1)S(1)}, u32[]{:S(2)}, u32[]{:S(2)}) collective-permute-start(bf16[2,2,144,256]{3,2,1,0:T(8,128)(2,1)S(1)} %collective-permute-done.14.refs_2_), channel_id=1, source_target_pairs={{0,2},{1,15},{2,4},{3,1},{4,6},{5,3},{6,8},{7,5},{8,10},{9,7},{10,... | collective-permute-start | bytes 884744 | tf_op jit(solution)/shard_map/ppermute | solution.py:29
  151.1 5.1 %collective-permute-start.16 = (bf16[2,144,256]{2,1,0:T(8,128)(2,1)S(1)}, bf16[2,144,256]{2,1,0:T(8,128)(2,1)S(1)}, u32[]{:S(2)}, u32[]{:S(2)}) collective-permute-start(bf16[2,144,256]{2,1,0:T(8,128)(2,1)S(1)} %slice_bitcast_fusion.1), channel_id=1, source_target_pairs={{0,4},{1,13},{2,6},{3,15},{4,8},{5,1},{6,10},{7,3},{8,12},{9,5},{1... | collective-permute-start | bytes 442376 | tf_op jit(solution)/shard_map/ppermute | solution.py:29
  158.3 2.4 %collective-permute-start.18 = (bf16[2,2,144,256]{3,2,1,0:T(8,128)(2,1)S(1)}, bf16[2,2,144,256]{3,2,1,0:T(8,128)(2,1)S(1)}, u32[]{:S(2)}, u32[]{:S(2)}) collective-permute-start(bf16[2,2,144,256]{3,2,1,0:T(8,128)(2,1)S(1)} %collective-permute-done.14.refs_2_), channel_id=1, source_target_pairs={{0,1},{1,0},{2,3},{3,2},{4,5},{5,4},{6,7},{7,6},{8,9},{9,8},{10,11... | collective-permute-start | bytes 884744 | tf_op jit(solution)/shard_map/ppermute | solution.py:33
  160.7 2.8 %collective-permute-start.19 = (bf16[2,2,144,256]{3,2,1,0:T(8,128)(2,1)S(1)}, bf16[2,2,144,256]{3,2,1,0:T(8,128)(2,1)}, u32[]{:S(2)}, u32[]{:S(2)}) collective-permute-start(bf16[2,2,144,256]{3,2,1,0:T(8,128)(2,1)S(1)} %collective-permute-done.15.refs_3_), channel_id=1, source_target_pairs={{0,1},{1,0},{2,3},{3,2},{4,5},{5,4},{6,7},{7,6},{8,9},{9,8},{10,11... | collective-permute-start | bytes 884744 | tf_op jit(solution)/shard_map/ppermute | solution.py:34
  169.0 5.2 %project_out.1 = (f32[288,256]{1,0:T(8,128)}, f32[16,8,256]{2,1,0:T(8,128)}) custom-call(s32[3]{0:T(128)} %copy-done, bf16[288,256]{1,0:T(8,128)(2,1)} %bitcast.27, f32[288,1]{1,0:T(8,128)} %broadcast_in_dim.9.gain, bf16[4,4,256,256]{3,2,1,0:T(8,128)(2,1)} %copy-done.1, bf16[2,2,144,256]{3,2,1,0:T(8,128)(2,1)} %copy-done.3, ...), custom_call_target="tpu_custom_call" | custom-call | tf_op jit(solution)/shard_map/project_out/pallas_call | solution.py:257
  174.2 10.2 %all-to-all-start.4 = ((f32[16,8,256]{2,1,0:T(8,128)}), f32[16,8,256]{2,1,0:T(8,128)S(1)}, u32[]{:S(2)}, u32[]{:S(2)}) async-start(f32[16,8,256]{2,1,0:T(8,128)} %get-tuple-element.12), calls=%async_computation.4 | async-start | bytes 262144 | tf_op jit(solution)/shard_map/all_to_all | solution.py:39
  184.5 9.4 %all-to-all-done.4 = f32[16,8,256]{2,1,0:T(8,128)S(1)} async-done(((f32[16,8,256]{2,1,0:T(8,128)}), f32[16,8,256]{2,1,0:T(8,128)S(1)}, u32[]{:S(2)}, u32[]{:S(2)}) %all-to-all-start.4) | async-done | bytes 131104 | tf_op jit(solution)/shard_map/all_to_all | solution.py:39
  (80 shorter events, 36.6 us)
Async XLA Ops:
  2.6 40.9 %all-to-all-start = ((bf16[4,296,256]{2,1,0:T(8,128)(2,1)}), bf16[4,296,256]{2,1,0:T(8,128)(2,1)S(1)}, u32[]{:S(2)}, u32[]{:S(2)}) async-start(bf16[4,296,256]{2,1,0:T(8,128)(2,1)} %get-tuple-element.8), calls=%async_computation | async-start | bytes 1212416 | tf_op jit(solution)/shard_map/all_to_all | solution.py:39
  10.2 17.0 %collective-permute-start = (bf16[144,512]{1,0:T(8,128)(2,1)}, bf16[144,512]{1,0:T(8,128)(2,1)S(1)}, u32[]{:S(2)}, u32[]{:S(2)}) collective-permute-start(bf16[144,512]{1,0:T(8,128)(2,1)} %get-tuple-element.10), channel_id=1, source_target_pairs={{0,16},{16,0},{1,17},{17,1},{2,18},{18,2},{3,19},{19,3},{4,20},{20... | collective-permute-start | bytes 442376 | tf_op jit(solution)/shard_map/ppermute | solution.py:202
  28.1 4.6 %collective-permute-start.1 = (bf16[2,144,512]{2,1,0:T(8,128)(2,1)S(1)}, bf16[2,144,512]{2,1,0:T(8,128)(2,1)S(1)}, u32[]{:S(2)}, u32[]{:S(2)}) collective-permute-start(bf16[2,144,512]{2,1,0:T(8,128)(2,1)S(1)} %get-tuple-element.17), channel_id=1, source_target_pairs={{0,1},{1,0},{2,3},{3,2},{4,5},{5,4},{6,7},{7,6},{8,9},{9,8},{10,11... | collective-permute-start | bytes 884744 | tf_op jit(solution)/shard_map/ppermute | solution.py:23
  32.8 23.8 %collective-permute-start.3 = (bf16[2,2,144,512]{3,2,1,0:T(8,128)(2,1)S(1)}, bf16[2,2,144,512]{3,2,1,0:T(8,128)(2,1)}, u32[]{:S(2)}, u32[]{:S(2)}) collective-permute-start(bf16[2,2,144,512]{3,2,1,0:T(8,128)(2,1)S(1)} %pad_maximum_fusion.refs_0_), channel_id=1, source_target_pairs={{0,4},{1,13},{2,6},{3,15},{4,8},{5,1},{6,10},{7,3},{8,12},{9,5},{1... | collective-permute-start | bytes 1769480 | tf_op jit(solution)/shard_map/ppermute | solution.py:29
  45.0 32.7 %all-to-all-start.1 = ((bf16[4,4,296,256]{3,2,1,0:T(8,128)(2,1)}), bf16[4,4,296,256]{3,2,1,0:T(8,128)(2,1)S(1)}, u32[]{:S(2)}, u32[]{:S(2)}) async-start(bf16[4,4,296,256]{3,2,1,0:T(8,128)(2,1)} %broadcast_in_dim.7), calls=%async_computation.1 | async-start | bytes 4849664 | tf_op jit(solution)/shard_map/all_to_all | solution.py:39
  49.2 19.1 %collective-permute-start.2 = (bf16[2,2,144,512]{3,2,1,0:T(8,128)(2,1)S(1)}, bf16[2,2,144,512]{3,2,1,0:T(8,128)(2,1)}, u32[]{:S(2)}, u32[]{:S(2)}) collective-permute-start(bf16[2,2,144,512]{3,2,1,0:T(8,128)(2,1)S(1)} %pad_maximum_fusion.refs_0_), channel_id=1, source_target_pairs={{0,2},{1,15},{2,4},{3,1},{4,6},{5,3},{6,8},{7,5},{8,10},{9,7},{10,... | collective-permute-start | bytes 1769480 | tf_op jit(solution)/shard_map/ppermute | solution.py:29
  56.6 14.1 %collective-permute-start.4 = (bf16[2,2,144,512]{3,2,1,0:T(8,128)(2,1)}, bf16[2,2,144,512]{3,2,1,0:T(8,128)(2,1)}, u32[]{:S(2)}, u32[]{:S(2)}) collective-permute-start(bf16[2,2,144,512]{3,2,1,0:T(8,128)(2,1)} %collective-permute-done.3.refs_2_), channel_id=1, source_target_pairs={{0,2},{1,15},{2,4},{3,1},{4,6},{5,3},{6,8},{7,5},{8,10},{9,7},{10,... | collective-permute-start | bytes 1769480 | tf_op jit(solution)/shard_map/ppermute | solution.py:29
  61.5 14.1 %collective-permute-start.5 = (bf16[2,144,512]{2,1,0:T(8,128)(2,1)}, bf16[2,144,512]{2,1,0:T(8,128)(2,1)}, u32[]{:S(2)}, u32[]{:S(2)}) collective-permute-start(bf16[2,144,512]{2,1,0:T(8,128)(2,1)} %slice_bitcast_fusion), channel_id=1, source_target_pairs={{0,4},{1,13},{2,6},{3,15},{4,8},{5,1},{6,10},{7,3},{8,12},{9,5},{1... | collective-permute-start | bytes 884744 | tf_op jit(solution)/shard_map/ppermute | solution.py:29
  66.3 12.5 %collective-permute-start.7 = (bf16[2,2,144,512]{3,2,1,0:T(8,128)(2,1)}, bf16[2,2,144,512]{3,2,1,0:T(8,128)(2,1)}, u32[]{:S(2)}, u32[]{:S(2)}) collective-permute-start(bf16[2,2,144,512]{3,2,1,0:T(8,128)(2,1)} %collective-permute-done.3.refs_2_), channel_id=1, source_target_pairs={{0,1},{1,0},{2,3},{3,2},{4,5},{5,4},{6,7},{7,6},{8,9},{9,8},{10,11... | collective-permute-start | bytes 1769480 | tf_op jit(solution)/shard_map/ppermute | solution.py:33
  68.3 10.5 %collective-permute-start.6 = (bf16[2,2,144,512]{3,2,1,0:T(8,128)(2,1)}, bf16[2,2,144,512]{3,2,1,0:T(8,128)(2,1)}, u32[]{:S(2)}, u32[]{:S(2)}) collective-permute-start(bf16[2,2,144,512]{3,2,1,0:T(8,128)(2,1)} %collective-permute-done.2.refs_1_), channel_id=1, source_target_pairs={{0,1},{1,0},{2,3},{3,2},{4,5},{5,4},{6,7},{7,6},{8,9},{9,8},{10,11... | collective-permute-start | bytes 1769480 | tf_op jit(solution)/shard_map/ppermute | solution.py:33
  70.7 8.7 %collective-permute-start.8 = (bf16[2,2,144,512]{3,2,1,0:T(8,128)(2,1)}, bf16[2,2,144,512]{3,2,1,0:T(8,128)(2,1)}, u32[]{:S(2)}, u32[]{:S(2)}) collective-permute-start(bf16[2,2,144,512]{3,2,1,0:T(8,128)(2,1)} %collective-permute-done.4.refs_3_), channel_id=1, source_target_pairs={{0,1},{1,0},{2,3},{3,2},{4,5},{5,4},{6,7},{7,6},{8,9},{9,8},{10,11... | collective-permute-start | bytes 1769480 | tf_op jit(solution)/shard_map/ppermute | solution.py:34
  75.6 3.8 %collective-permute-start.9 = (bf16[2,144,512]{2,1,0:T(8,128)(2,1)}, bf16[2,144,512]{2,1,0:T(8,128)(2,1)}, u32[]{:S(2)}, u32[]{:S(2)}) collective-permute-start(bf16[2,144,512]{2,1,0:T(8,128)(2,1)} %collective-permute-done.5.refs_4_), channel_id=1, source_target_pairs={{0,1},{1,0},{2,3},{3,2},{4,5},{5,4},{6,7},{7,6},{8,9},{9,8},{10,11... | collective-permute-start | bytes 884744 | tf_op jit(solution)/shard_map/ppermute | solution.py:34
  107.9 59.8 %all-to-all-start.3 = ((bf16[4,4,256,256]{3,2,1,0:T(8,128)(2,1)}), bf16[4,4,256,256]{3,2,1,0:T(8,128)(2,1)S(1)}, u32[]{:S(2)}, u32[]{:S(2)}) async-start(bf16[4,4,256,256]{3,2,1,0:T(8,128)(2,1)} %broadcast_in_dim.8), calls=%async_computation.3 | async-start | bytes 4194304 | tf_op jit(solution)/shard_map/all_to_all | solution.py:39
  112.0 9.0 %collective-permute-start.11 = (bf16[144,256]{1,0:T(8,128)(2,1)S(1)}, bf16[144,256]{1,0:T(8,128)(2,1)S(1)}, u32[]{:S(2)}, u32[]{:S(2)}) collective-permute-start(bf16[144,256]{1,0:T(8,128)(2,1)S(1)} %bitcast.37), channel_id=1, source_target_pairs={{0,16},{1,17},{2,48},{3,49},{4,80},{5,81},{6,112},{7,113},{8,144},... | collective-permute-start | bytes 221192 | tf_op jit(solution)/shard_map/ppermute | solution.py:226
  113.9 7.1 %collective-permute-start.10 = (bf16[144,256]{1,0:T(8,128)(2,1)S(1)}, bf16[144,256]{1,0:T(8,128)(2,1)S(1)}, u32[]{:S(2)}, u32[]{:S(2)}) collective-permute-start(bf16[144,256]{1,0:T(8,128)(2,1)S(1)} %bitcast.38), channel_id=1, source_target_pairs={{0,0},{1,1},{2,32},{3,33},{4,64},{5,65},{6,96},{7,97},{8,128},{9,1... | collective-permute-start | bytes 221192 | tf_op jit(solution)/shard_map/ppermute | solution.py:226
  121.1 6.1 %collective-permute-start.12 = (bf16[2,144,256]{2,1,0:T(8,128)(2,1)S(1)}, bf16[2,144,256]{2,1,0:T(8,128)(2,1)S(1)}, u32[]{:S(2)}, u32[]{:S(2)}) collective-permute-start(bf16[2,144,256]{2,1,0:T(8,128)(2,1)S(1)} %get-tuple-element.19), channel_id=1, source_target_pairs={{0,1},{1,0},{2,3},{3,2},{4,5},{5,4},{6,7},{7,6},{8,9},{9,8},{10,11... | collective-permute-start | bytes 442376 | tf_op jit(solution)/shard_map/ppermute | solution.py:23
  127.2 21.1 %collective-permute-start.14 = (bf16[2,2,144,256]{3,2,1,0:T(8,128)(2,1)S(1)}, bf16[2,2,144,256]{3,2,1,0:T(8,128)(2,1)S(1)}, u32[]{:S(2)}, u32[]{:S(2)}) collective-permute-start(bf16[2,2,144,256]{3,2,1,0:T(8,128)(2,1)S(1)} %pad_maximum_fusion.2.refs_0_), channel_id=1, source_target_pairs={{0,4},{1,13},{2,6},{3,15},{4,8},{5,1},{6,10},{7,3},{8,12},{9,5},{1... | collective-permute-start | bytes 884744 | tf_op jit(solution)/shard_map/ppermute | solution.py:29
  141.5 14.8 %collective-permute-start.13 = (bf16[2,2,144,256]{3,2,1,0:T(8,128)(2,1)S(1)}, bf16[2,2,144,256]{3,2,1,0:T(8,128)(2,1)S(1)}, u32[]{:S(2)}, u32[]{:S(2)}) collective-permute-start(bf16[2,2,144,256]{3,2,1,0:T(8,128)(2,1)S(1)} %pad_maximum_fusion.2.refs_0_), channel_id=1, source_target_pairs={{0,2},{1,15},{2,4},{3,1},{4,6},{5,3},{6,8},{7,5},{8,10},{9,7},{10,... | collective-permute-start | bytes 884744 | tf_op jit(solution)/shard_map/ppermute | solution.py:29
  148.3 12.3 %collective-permute-start.15 = (bf16[2,2,144,256]{3,2,1,0:T(8,128)(2,1)S(1)}, bf16[2,2,144,256]{3,2,1,0:T(8,128)(2,1)S(1)}, u32[]{:S(2)}, u32[]{:S(2)}) collective-permute-start(bf16[2,2,144,256]{3,2,1,0:T(8,128)(2,1)S(1)} %collective-permute-done.14.refs_2_), channel_id=1, source_target_pairs={{0,2},{1,15},{2,4},{3,1},{4,6},{5,3},{6,8},{7,5},{8,10},{9,7},{10,... | collective-permute-start | bytes 884744 | tf_op jit(solution)/shard_map/ppermute | solution.py:29
  151.1 12.3 %collective-permute-start.16 = (bf16[2,144,256]{2,1,0:T(8,128)(2,1)S(1)}, bf16[2,144,256]{2,1,0:T(8,128)(2,1)S(1)}, u32[]{:S(2)}, u32[]{:S(2)}) collective-permute-start(bf16[2,144,256]{2,1,0:T(8,128)(2,1)S(1)} %slice_bitcast_fusion.1), channel_id=1, source_target_pairs={{0,4},{1,13},{2,6},{3,15},{4,8},{5,1},{6,10},{7,3},{8,12},{9,5},{1... | collective-permute-start | bytes 442376 | tf_op jit(solution)/shard_map/ppermute | solution.py:29
  156.3 9.9 %collective-permute-start.17 = (bf16[2,2,144,256]{3,2,1,0:T(8,128)(2,1)S(1)}, bf16[2,2,144,256]{3,2,1,0:T(8,128)(2,1)S(1)}, u32[]{:S(2)}, u32[]{:S(2)}) collective-permute-start(bf16[2,2,144,256]{3,2,1,0:T(8,128)(2,1)S(1)} %collective-permute-done.13.refs_1_), channel_id=1, source_target_pairs={{0,1},{1,0},{2,3},{3,2},{4,5},{5,4},{6,7},{7,6},{8,9},{9,8},{10,11... | collective-permute-start | bytes 884744 | tf_op jit(solution)/shard_map/ppermute | solution.py:33
  158.3 8.0 %collective-permute-start.18 = (bf16[2,2,144,256]{3,2,1,0:T(8,128)(2,1)S(1)}, bf16[2,2,144,256]{3,2,1,0:T(8,128)(2,1)S(1)}, u32[]{:S(2)}, u32[]{:S(2)}) collective-permute-start(bf16[2,2,144,256]{3,2,1,0:T(8,128)(2,1)S(1)} %collective-permute-done.14.refs_2_), channel_id=1, source_target_pairs={{0,1},{1,0},{2,3},{3,2},{4,5},{5,4},{6,7},{7,6},{8,9},{9,8},{10,11... | collective-permute-start | bytes 884744 | tf_op jit(solution)/shard_map/ppermute | solution.py:33
  160.7 7.0 %collective-permute-start.19 = (bf16[2,2,144,256]{3,2,1,0:T(8,128)(2,1)S(1)}, bf16[2,2,144,256]{3,2,1,0:T(8,128)(2,1)}, u32[]{:S(2)}, u32[]{:S(2)}) collective-permute-start(bf16[2,2,144,256]{3,2,1,0:T(8,128)(2,1)S(1)} %collective-permute-done.15.refs_3_), channel_id=1, source_target_pairs={{0,1},{1,0},{2,3},{3,2},{4,5},{5,4},{6,7},{7,6},{8,9},{9,8},{10,11... | collective-permute-start | bytes 884744 | tf_op jit(solution)/shard_map/ppermute | solution.py:34
  174.2 19.6 %all-to-all-start.4 = ((f32[16,8,256]{2,1,0:T(8,128)}), f32[16,8,256]{2,1,0:T(8,128)S(1)}, u32[]{:S(2)}, u32[]{:S(2)}) async-start(f32[16,8,256]{2,1,0:T(8,128)} %get-tuple-element.12), calls=%async_computation.4 | async-start | bytes 262144 | tf_op jit(solution)/shard_map/all_to_all | solution.py:39
  (16 other events, 235.4 us)

commit v4 on v3

--- a/solution.py
+++ b/solution.py
@@ -23,13 +23,13 @@
     return jnp.stack([x, lax.ppermute(x, "c", ring(2, 1))])
 
 
-def z_pieces(own):
+def z_pieces(own, relay):
     def send(x, s):
         up_down = [((z, c), ((z + (s if c == 0 else -s)) % 8, c)) for z in range(8) for c in range(2)]
         return lax.ppermute(x, ("z", "c"), [(2 * a + b, 2 * d + e) for (a, b), (d, e) in up_down])
 
     one, two = send(own, 1), send(own, 2)
-    three, four = send(two, 1), send(two[0], 2)
+    three, four = (send(two, 1), send(two[0], 2)) if relay else (send(own, 3), send(own[0], 4))
     near = [lax.ppermute(p, "c", ring(2, 1)) for p in (one, two)]
     far = [lax.ppermute(p, "c", ring(2, 1)) for p in (three, four)]
     return [own, one, two, three, four, *near, *far]
@@ -134,15 +134,13 @@
         m.wait()
 
 
-def output_kernel(pos, x, gain, att, *refs):
-    pieces, (mixed, sums, rows, *held, w_sems) = refs[:9], refs[9:]
-    w_moves = [pltpu.make_async_copy(p, h, w_sems.at[k]) for k, (p, h) in enumerate(zip(pieces, held))]
-    for m in w_moves:
-        m.start()
-    for m in w_moves:
-        m.wait()
+def place_kernel(pos, *refs):
+    pieces, rows = refs[:9], refs[9]
     for k, i, r, t, core in blocks(pos):
-        rows[t, core] = held[k][r] if i is None else held[k][i, r]
+        rows[t, core] = pieces[k][r] if i is None else pieces[k][i, r]
+
+
+def output_kernel(x, gain, att, rows, mixed, sums):
     total = jnp.zeros((288, 256), F32)
     for g in range(16):
         term = lax.dot_general(
@@ -200,7 +198,7 @@
         name="pack",
     )(query_weight, key_weight, value_weight, x_t, before_gain)
     w_pair = lax.ppermute(w, "yl", ring(2, 1))
-    w_pieces = z_pieces(both_cores(jnp.stack([w, w_pair])))
+    w_pieces = z_pieces(both_cores(jnp.stack([w, w_pair])), True)
 
     column = exchanged(packed, "hx")
     stream = exchanged(jnp.broadcast_to(column, (4, *column.shape)), "hy")
@@ -225,8 +223,9 @@
         ]
         return lax.ppermute(output_weight.T, ("hx", "hy", "yl", "z", "c"), turn)
 
-    wo = jnp.stack([turned(0), turned(8)])
-    wo_pieces = z_pieces(both_cores(wo))
+    wo_here = turned(0)
+    wo = jnp.stack([wo_here, turned(8)])
+    wo_pieces = z_pieces(both_cores(wo), False)
 
     half_width = HEAD // 2
     frequency = 10000.0 ** (-jnp.arange(half_width, dtype=F32) / half_width)
@@ -254,22 +253,25 @@
     gathered = gathered.reshape(4, 4, rows, 256)
     after_col = after_gain.astype(F32)[:, None]
     feed_col = feed_gain.astype(F32)[:, None]
+    wo_rows = pl.pallas_call(
+        place_kernel,
+        out_shape=jax.ShapeDtypeStruct((16, 2, 144, 256), BF),
+        in_specs=[SMEM] + [VMEM] * 9,
+        out_specs=VMEM,
+        compiler_params=params(12),
+        name="place",
+    )(pos, *wo_pieces)
     mixed, sums = pl.pallas_call(
         output_kernel,
         out_shape=(
             jax.ShapeDtypeStruct((288, rows), F32),
             jax.ShapeDtypeStruct((16, 8, rows), F32),
         ),
-        in_specs=[SMEM] + [VMEM] * 3 + [ANY] * 9,
+        in_specs=[VMEM] * 4,
         out_specs=(VMEM, VMEM),
-        scratch_shapes=[
-            pltpu.VMEM((16, 2, 144, 256), BF),
-            *[pltpu.VMEM(p.shape, BF) for p in wo_pieces],
-            pltpu.SemaphoreType.DMA((9,)),
-        ],
-        compiler_params=params(56),
+        compiler_params=params(16),
         name="project_out",
-    )(pos, x_t, after_col, gathered, *wo_pieces)
+    )(x_t, after_col, gathered, wo_rows)
 
     sums = exchanged(sums, hid).sum(axis=0)
     after_sq, cross_sum, branch_sq = sums[0:1], sums[1:2], sums[2:3]

time: 197 us -> 200 us (1.015)
  starting transfers between devices: 102 us -> 115 us
  waiting for transfers between devices: 46 us -> 41.6 us
  local copies, waits for them, and re-layouts: 7.91 us -> 4.95 us
    ppermute x4, starting transfers between devices: 8.85 us -> 17.7 us  [z_pieces(): far = [lax.ppermute(p, 'c', ring(2, 1)) for p in (three, four)]]
    ppermute x8, waiting for transfers between devices: 12.2 us -> 7.31 us  [send(): lax.ppermute(x, ('z', 'c'), [(2 * a + b, 2 * d + e) for (a, b), (d, e) in...]
    all_to_all x4, starting transfers between devices: 26.1 us -> 28.8 us  [exchanged(): return lax.all_to_all(x, axis, split_axis=0, concat_axis=0, tiled=True)]
    unnamed x30 -> x10, local copies, waits for them, and re-layouts: 2.28 us -> 0.02 us
    pallas_call x1, Pallas kernels: 5.18 us -> 3.13 us  [per_device(): pl.pallas_call(output_kernel, out_shape=(jax.ShapeDtypeStruct((288, rows)...]
  transfers between devices with their start and end apart: 25 -> 25, of which waited for: 10 -> 9; matrix products, arithmetic and copies ran while one was open for 3% -> 3% of each run, Pallas kernels for 1% -> 1%
where the time goes in v4:
time: 200 us; the launch traced here: 199 us
  starting transfers between devices  115 us (58%)
  waiting for transfers between devices  41.6 us (21%)
  blocking collectives  21.8 us (11%)
  Pallas kernels  11.9 us (6%)
  local copies, waits for them, and re-layouts  4.95 us (2%)
  other arithmetic  2.66 us (1%)
    ppermute x8, starting transfers between devices, send(): lax.ppermute(x, ('z', 'c'), [(2 * a + b, 2 * d + e) for (a, b), (d, e) in...  46.4 us
    all_to_all x4, starting transfers between devices, exchanged(): return lax.all_to_all(x, axis, split_axis=0, concat_axis=0, tiled=True)  28.8 us
    all_to_all x1, blocking collectives, exchanged(): return lax.all_to_all(x, axis, split_axis=0, concat_axis=0, tiled=True)  21.8 us
    ppermute x4, starting transfers between devices, z_pieces(): far = [lax.ppermute(p, 'c', ring(2, 1)) for p in (three, four)]  17.7 us
    ppermute x1, waiting for transfers between devices, per_device(): w_pair = lax.ppermute(w, 'yl', ring(2, 1))  14.7 us
    all_to_all x4, waiting for transfers between devices, exchanged(): return lax.all_to_all(x, axis, split_axis=0, concat_axis=0, tiled=True)  9.22 us
    ppermute x4, starting transfers between devices, z_pieces(): near = [lax.ppermute(p, 'c', ring(2, 1)) for p in (one, two)]  8.66 us
    ppermute x2, starting transfers between devices, both_cores(): return jnp.stack([x, lax.ppermute(x, 'c', ring(2, 1))])  8.21 us
  transfers between devices with their start and end apart: 25, of which 9 were waited for; matrix products, arithmetic and copies ran while one was open for 3% of the time, Pallas kernels for 1%

profile of v4, /device:TPU:1, one launch (start us, length us, event | category | flops | bytes accessed | tf_op | source)
XLA Modules:
  0.0 198.5 jit_solution(10149360024514176062)
XLA Ops:
  2.6 7.6 %all-to-all-start = ((bf16[4,296,256]{2,1,0:T(8,128)(2,1)}), bf16[4,296,256]{2,1,0:T(8,128)(2,1)S(1)}, u32[]{:S(2)}, u32[]{:S(2)}) async-start(bf16[4,296,256]{2,1,0:T(8,128)(2,1)} %get-tuple-element.8), calls=%async_computation | async-start | bytes 1212416 | tf_op jit(solution)/shard_map/all_to_all | solution.py:39
  10.2 2.3 %collective-permute-start = (bf16[144,512]{1,0:T(8,128)(2,1)}, bf16[144,512]{1,0:T(8,128)(2,1)S(1)}, u32[]{:S(2)}, u32[]{:S(2)}) collective-permute-start(bf16[144,512]{1,0:T(8,128)(2,1)} %get-tuple-element.10), channel_id=1, source_target_pairs={{0,16},{16,0},{1,17},{17,1},{2,18},{18,2},{3,19},{19,3},{4,20},{20... | collective-permute-start | bytes 442376 | tf_op jit(solution)/shard_map/ppermute | solution.py:200
  12.5 14.7 %collective-permute-done = bf16[144,512]{1,0:T(8,128)(2,1)S(1)} collective-permute-done((bf16[144,512]{1,0:T(8,128)(2,1)}, bf16[144,512]{1,0:T(8,128)(2,1)S(1)}, u32[]{:S(2)}, u32[]{:S(2)}) %collective-permute-start) | collective-permute-done | bytes 147488 | tf_op jit(solution)/shard_map/ppermute | solution.py:200
  28.1 3.4 %collective-permute-start.1 = (bf16[2,144,512]{2,1,0:T(8,128)(2,1)S(1)}, bf16[2,144,512]{2,1,0:T(8,128)(2,1)S(1)}, u32[]{:S(2)}, u32[]{:S(2)}) collective-permute-start(bf16[2,144,512]{2,1,0:T(8,128)(2,1)S(1)} %get-tuple-element.17), channel_id=1, source_target_pairs={{0,1},{1,0},{2,3},{3,2},{4,5},{5,4},{6,7},{7,6},{8,9},{9,8},{10,11... | collective-permute-start | bytes 884744 | tf_op jit(solution)/shard_map/ppermute | solution.py:23
  32.8 10.7 %collective-permute-start.3 = (bf16[2,2,144,512]{3,2,1,0:T(8,128)(2,1)S(1)}, bf16[2,2,144,512]{3,2,1,0:T(8,128)(2,1)}, u32[]{:S(2)}, u32[]{:S(2)}) collective-permute-start(bf16[2,2,144,512]{3,2,1,0:T(8,128)(2,1)S(1)} %pad_maximum_fusion.refs_0_), channel_id=1, source_target_pairs={{0,4},{1,13},{2,6},{3,15},{4,8},{5,1},{6,10},{7,3},{8,12},{9,5},{1... | collective-permute-start | bytes 1769480 | tf_op jit(solution)/shard_map/ppermute | solution.py:29
  45.1 4.1 %all-to-all-start.1 = ((bf16[4,4,296,256]{3,2,1,0:T(8,128)(2,1)}), bf16[4,4,296,256]{3,2,1,0:T(8,128)(2,1)S(1)}, u32[]{:S(2)}, u32[]{:S(2)}) async-start(bf16[4,4,296,256]{3,2,1,0:T(8,128)(2,1)} %broadcast_in_dim.7), calls=%async_computation.1 | async-start | bytes 4849664 | tf_op jit(solution)/shard_map/all_to_all | solution.py:39
  51.4 5.2 %collective-permute-done.3.refs_2_ = bf16[2,2,144,512]{3,2,1,0:T(8,128)(2,1)} collective-permute-done((bf16[2,2,144,512]{3,2,1,0:T(8,128)(2,1)S(1)}, bf16[2,2,144,512]{3,2,1,0:T(8,128)(2,1)}, u32[]{:S(2)}, u32[]{:S(2)}) %collective-permute-start.3) | collective-permute-done | bytes 589856 | tf_op jit(solution)/shard_map/ppermute | solution.py:29
  56.6 3.2 %collective-permute-start.4 = (bf16[2,2,144,512]{3,2,1,0:T(8,128)(2,1)}, bf16[2,2,144,512]{3,2,1,0:T(8,128)(2,1)}, u32[]{:S(2)}, u32[]{:S(2)}) collective-permute-start(bf16[2,2,144,512]{3,2,1,0:T(8,128)(2,1)} %collective-permute-done.3.refs_2_), channel_id=1, source_target_pairs={{0,2},{1,15},{2,4},{3,1},{4,6},{5,3},{6,8},{7,5},{8,10},{9,7},{10,... | collective-permute-start | bytes 1769480 | tf_op jit(solution)/shard_map/ppermute | solution.py:29
  61.5 4.8 %collective-permute-start.5 = (bf16[2,144,512]{2,1,0:T(8,128)(2,1)}, bf16[2,144,512]{2,1,0:T(8,128)(2,1)}, u32[]{:S(2)}, u32[]{:S(2)}) collective-permute-start(bf16[2,144,512]{2,1,0:T(8,128)(2,1)} %slice_bitcast_fusion), channel_id=1, source_target_pairs={{0,4},{1,13},{2,6},{3,15},{4,8},{5,1},{6,10},{7,3},{8,12},{9,5},{1... | collective-permute-start | bytes 884744 | tf_op jit(solution)/shard_map/ppermute | solution.py:29
  68.3 2.4 %collective-permute-start.6 = (bf16[2,2,144,512]{3,2,1,0:T(8,128)(2,1)}, bf16[2,2,144,512]{3,2,1,0:T(8,128)(2,1)}, u32[]{:S(2)}, u32[]{:S(2)}) collective-permute-start(bf16[2,2,144,512]{3,2,1,0:T(8,128)(2,1)} %collective-permute-done.2.refs_1_), channel_id=1, source_target_pairs={{0,1},{1,0},{2,3},{3,2},{4,5},{5,4},{6,7},{7,6},{8,9},{9,8},{10,11... | collective-permute-start | bytes 1769480 | tf_op jit(solution)/shard_map/ppermute | solution.py:33
  79.4 5.1 %attend.1 = bf16[4,256,256]{2,1,0:T(8,128)(2,1)S(1)} custom-call(s32[3]{0:T(128)S(1)} %pad_add_fusion.pos, bf16[256,4608]{1,0:T(8,128)(2,1)S(1)} %get-tuple-element.9.normed, f32[256,64]{1,0:T(8,128)S(1)} %get-tuple-element.23.cos, f32[256,64]{1,0:T(8,128)S(1)} %get-tuple-element.22.sin, f32[256,256]{1,0:T(8,128)S(1)} %fusion.1.mask, ...), custom_call_target="tpu_custom_call" | custom-call | tf_op jit(solution)/shard_map/attend/pallas_call | solution.py:237
  84.5 21.8 %all_to_all.25 = bf16[4,256,256]{2,1,0:T(8,128)(2,1)S(1)} all-to-all(bf16[4,256,256]{2,1,0:T(8,128)(2,1)S(1)} %attend.1), channel_id=1, replica_groups=mesh['hx'=4,'hy'=4,'yl'=2,'z'=8,'c'=2] {'hx'}, dimensions={0} | all-to-all | bytes 1048576 | tf_op jit(solution)/shard_map/all_to_all | solution.py:39
  107.9 4.6 %all-to-all-start.3 = ((bf16[4,4,256,256]{3,2,1,0:T(8,128)(2,1)}), bf16[4,4,256,256]{3,2,1,0:T(8,128)(2,1)}, u32[]{:S(2)}, u32[]{:S(2)}) async-start(bf16[4,4,256,256]{3,2,1,0:T(8,128)(2,1)} %broadcast_in_dim.8), calls=%async_computation.3 | async-start | bytes 4194304 | tf_op jit(solution)/shard_map/all_to_all | solution.py:39
  115.1 6.4 %collective-permute-done.11 = bf16[144,256]{1,0:T(8,128)(2,1)S(1)} collective-permute-done((bf16[144,256]{1,0:T(8,128)(2,1)S(1)}, bf16[144,256]{1,0:T(8,128)(2,1)S(1)}, u32[]{:S(2)}, u32[]{:S(2)}) %collective-permute-start.11) | collective-permute-done | bytes 73760 | tf_op jit(solution)/shard_map/ppermute | solution.py:224
  121.5 4.8 %collective-permute-start.12 = (bf16[2,144,256]{2,1,0:T(8,128)(2,1)S(1)}, bf16[2,144,256]{2,1,0:T(8,128)(2,1)S(1)}, u32[]{:S(2)}, u32[]{:S(2)}) collective-permute-start(bf16[2,144,256]{2,1,0:T(8,128)(2,1)S(1)} %get-tuple-element.19), channel_id=1, source_target_pairs={{0,1},{1,0},{2,3},{3,2},{4,5},{5,4},{6,7},{7,6},{8,9},{9,8},{10,11... | collective-permute-start | bytes 442376 | tf_op jit(solution)/shard_map/ppermute | solution.py:23
  127.3 13.5 %collective-permute-start.13 = (bf16[2,2,144,256]{3,2,1,0:T(8,128)(2,1)S(1)}, bf16[2,2,144,256]{3,2,1,0:T(8,128)(2,1)S(1)}, u32[]{:S(2)}, u32[]{:S(2)}) collective-permute-start(bf16[2,2,144,256]{3,2,1,0:T(8,128)(2,1)S(1)} %pad_maximum_fusion.2.refs_0_), channel_id=1, source_target_pairs={{0,2},{1,15},{2,4},{3,1},{4,6},{5,3},{6,8},{7,5},{8,10},{9,7},{10,... | collective-permute-start | bytes 884744 | tf_op jit(solution)/shard_map/ppermute | solution.py:29
  140.8 2.6 %collective-permute-start.14 = (bf16[2,2,144,256]{3,2,1,0:T(8,128)(2,1)S(1)}, bf16[2,2,144,256]{3,2,1,0:T(8,128)(2,1)S(1)}, u32[]{:S(2)}, u32[]{:S(2)}) collective-permute-start(bf16[2,2,144,256]{3,2,1,0:T(8,128)(2,1)S(1)} %pad_maximum_fusion.2.refs_0_), channel_id=1, source_target_pairs={{0,4},{1,13},{2,6},{3,15},{4,8},{5,1},{6,10},{7,3},{8,12},{9,5},{1... | collective-permute-start | bytes 884744 | tf_op jit(solution)/shard_map/ppermute | solution.py:29
  143.4 4.9 %collective-permute-start.15 = (bf16[2,2,144,256]{3,2,1,0:T(8,128)(2,1)S(1)}, bf16[2,2,144,256]{3,2,1,0:T(8,128)(2,1)S(1)}, u32[]{:S(2)}, u32[]{:S(2)}) collective-permute-start(bf16[2,2,144,256]{3,2,1,0:T(8,128)(2,1)S(1)} %pad_maximum_fusion.2.refs_0_), channel_id=1, source_target_pairs={{0,6},{1,11},{2,8},{3,13},{4,10},{5,15},{6,12},{7,1},{8,14},{9,3},... | collective-permute-start | bytes 884744 | tf_op jit(solution)/shard_map/ppermute | solution.py:29
  148.4 4.5 %collective-permute-start.16 = (bf16[2,144,256]{2,1,0:T(8,128)(2,1)S(1)}, bf16[2,144,256]{2,1,0:T(8,128)(2,1)S(1)}, u32[]{:S(2)}, u32[]{:S(2)}) collective-permute-start(bf16[2,144,256]{2,1,0:T(8,128)(2,1)S(1)} %get-tuple-element.19), channel_id=1, source_target_pairs={{0,8},{1,9},{2,10},{3,11},{4,12},{5,13},{6,14},{7,15},{8,0},{9,1},... | collective-permute-start | bytes 442376 | tf_op jit(solution)/shard_map/ppermute | solution.py:29
  154.9 2.4 %collective-permute-start.18 = (bf16[2,2,144,256]{3,2,1,0:T(8,128)(2,1)S(1)}, bf16[2,2,144,256]{3,2,1,0:T(8,128)(2,1)S(1)}, u32[]{:S(2)}, u32[]{:S(2)}) collective-permute-start(bf16[2,2,144,256]{3,2,1,0:T(8,128)(2,1)S(1)} %collective-permute-done.14.refs_2_), channel_id=1, source_target_pairs={{0,1},{1,0},{2,3},{3,2},{4,5},{5,4},{6,7},{7,6},{8,9},{9,8},{10,11... | collective-permute-start | bytes 884744 | tf_op jit(solution)/shard_map/ppermute | solution.py:33
  157.3 11.5 %collective-permute-start.19 = (bf16[2,2,144,256]{3,2,1,0:T(8,128)(2,1)S(1)}, bf16[2,2,144,256]{3,2,1,0:T(8,128)(2,1)S(1)}, u32[]{:S(2)}, u32[]{:S(2)}) collective-permute-start(bf16[2,2,144,256]{3,2,1,0:T(8,128)(2,1)S(1)} %collective-permute-done.15.refs_3_), channel_id=1, source_target_pairs={{0,1},{1,0},{2,3},{3,2},{4,5},{5,4},{6,7},{7,6},{8,9},{9,8},{10,11... | collective-permute-start | bytes 884744 | tf_op jit(solution)/shard_map/ppermute | solution.py:34
  172.9 3.1 %project_out.1 = (f32[288,256]{1,0:T(8,128)S(1)}, f32[16,8,256]{2,1,0:T(8,128)}) custom-call(bf16[288,256]{1,0:T(8,128)(2,1)S(1)} %bitcast.25, f32[288,1]{1,0:T(8,128)S(1)} %broadcast_in_dim.9.gain, bf16[4,4,256,256]{3,2,1,0:T(8,128)(2,1)} %all-to-all-done.3.att, bf16[16,2,144,256]{3,2,1,0:T(8,128)(2,1)S(1)} %place.1.rows), custom_call_target="tpu_custom_call" | custom-call | tf_op jit(solution)/shard_map/project_out/pallas_call | solution.py:264
  176.0 12.4 %all-to-all-start.4 = ((f32[16,8,256]{2,1,0:T(8,128)}), f32[16,8,256]{2,1,0:T(8,128)S(1)}, u32[]{:S(2)}, u32[]{:S(2)}) async-start(f32[16,8,256]{2,1,0:T(8,128)} %get-tuple-element.12), calls=%async_computation.4 | async-start | bytes 262144 | tf_op jit(solution)/shard_map/all_to_all | solution.py:39
  188.4 9.2 %all-to-all-done.4 = f32[16,8,256]{2,1,0:T(8,128)S(1)} async-done(((f32[16,8,256]{2,1,0:T(8,128)}), f32[16,8,256]{2,1,0:T(8,128)S(1)}, u32[]{:S(2)}, u32[]{:S(2)}) %all-to-all-start.4) | async-done | bytes 131104 | tf_op jit(solution)/shard_map/all_to_all | solution.py:39
  (60 shorter events, 32.2 us)
Async XLA Ops:
  2.6 40.9 %all-to-all-start = ((bf16[4,296,256]{2,1,0:T(8,128)(2,1)}), bf16[4,296,256]{2,1,0:T(8,128)(2,1)S(1)}, u32[]{:S(2)}, u32[]{:S(2)}) async-start(bf16[4,296,256]{2,1,0:T(8,128)(2,1)} %get-tuple-element.8), calls=%async_computation | async-start | bytes 1212416 | tf_op jit(solution)/shard_map/all_to_all | solution.py:39
  10.2 17.0 %collective-permute-start = (bf16[144,512]{1,0:T(8,128)(2,1)}, bf16[144,512]{1,0:T(8,128)(2,1)S(1)}, u32[]{:S(2)}, u32[]{:S(2)}) collective-permute-start(bf16[144,512]{1,0:T(8,128)(2,1)} %get-tuple-element.10), channel_id=1, source_target_pairs={{0,16},{16,0},{1,17},{17,1},{2,18},{18,2},{3,19},{19,3},{4,20},{20... | collective-permute-start | bytes 442376 | tf_op jit(solution)/shard_map/ppermute | solution.py:200
  28.1 4.6 %collective-permute-start.1 = (bf16[2,144,512]{2,1,0:T(8,128)(2,1)S(1)}, bf16[2,144,512]{2,1,0:T(8,128)(2,1)S(1)}, u32[]{:S(2)}, u32[]{:S(2)}) collective-permute-start(bf16[2,144,512]{2,1,0:T(8,128)(2,1)S(1)} %get-tuple-element.17), channel_id=1, source_target_pairs={{0,1},{1,0},{2,3},{3,2},{4,5},{5,4},{6,7},{7,6},{8,9},{9,8},{10,11... | collective-permute-start | bytes 884744 | tf_op jit(solution)/shard_map/ppermute | solution.py:23
  32.8 23.8 %collective-permute-start.3 = (bf16[2,2,144,512]{3,2,1,0:T(8,128)(2,1)S(1)}, bf16[2,2,144,512]{3,2,1,0:T(8,128)(2,1)}, u32[]{:S(2)}, u32[]{:S(2)}) collective-permute-start(bf16[2,2,144,512]{3,2,1,0:T(8,128)(2,1)S(1)} %pad_maximum_fusion.refs_0_), channel_id=1, source_target_pairs={{0,4},{1,13},{2,6},{3,15},{4,8},{5,1},{6,10},{7,3},{8,12},{9,5},{1... | collective-permute-start | bytes 1769480 | tf_op jit(solution)/shard_map/ppermute | solution.py:29
  45.1 32.7 %all-to-all-start.1 = ((bf16[4,4,296,256]{3,2,1,0:T(8,128)(2,1)}), bf16[4,4,296,256]{3,2,1,0:T(8,128)(2,1)S(1)}, u32[]{:S(2)}, u32[]{:S(2)}) async-start(bf16[4,4,296,256]{3,2,1,0:T(8,128)(2,1)} %broadcast_in_dim.7), calls=%async_computation.1 | async-start | bytes 4849664 | tf_op jit(solution)/shard_map/all_to_all | solution.py:39
  49.2 19.0 %collective-permute-start.2 = (bf16[2,2,144,512]{3,2,1,0:T(8,128)(2,1)S(1)}, bf16[2,2,144,512]{3,2,1,0:T(8,128)(2,1)}, u32[]{:S(2)}, u32[]{:S(2)}) collective-permute-start(bf16[2,2,144,512]{3,2,1,0:T(8,128)(2,1)S(1)} %pad_maximum_fusion.refs_0_), channel_id=1, source_target_pairs={{0,2},{1,15},{2,4},{3,1},{4,6},{5,3},{6,8},{7,5},{8,10},{9,7},{10,... | collective-permute-start | bytes 1769480 | tf_op jit(solution)/shard_map/ppermute | solution.py:29
  56.6 14.1 %collective-permute-start.4 = (bf16[2,2,144,512]{3,2,1,0:T(8,128)(2,1)}, bf16[2,2,144,512]{3,2,1,0:T(8,128)(2,1)}, u32[]{:S(2)}, u32[]{:S(2)}) collective-permute-start(bf16[2,2,144,512]{3,2,1,0:T(8,128)(2,1)} %collective-permute-done.3.refs_2_), channel_id=1, source_target_pairs={{0,2},{1,15},{2,4},{3,1},{4,6},{5,3},{6,8},{7,5},{8,10},{9,7},{10,... | collective-permute-start | bytes 1769480 | tf_op jit(solution)/shard_map/ppermute | solution.py:29
  61.5 14.1 %collective-permute-start.5 = (bf16[2,144,512]{2,1,0:T(8,128)(2,1)}, bf16[2,144,512]{2,1,0:T(8,128)(2,1)}, u32[]{:S(2)}, u32[]{:S(2)}) collective-permute-start(bf16[2,144,512]{2,1,0:T(8,128)(2,1)} %slice_bitcast_fusion), channel_id=1, source_target_pairs={{0,4},{1,13},{2,6},{3,15},{4,8},{5,1},{6,10},{7,3},{8,12},{9,5},{1... | collective-permute-start | bytes 884744 | tf_op jit(solution)/shard_map/ppermute | solution.py:29
  66.3 12.5 %collective-permute-start.7 = (bf16[2,2,144,512]{3,2,1,0:T(8,128)(2,1)}, bf16[2,2,144,512]{3,2,1,0:T(8,128)(2,1)}, u32[]{:S(2)}, u32[]{:S(2)}) collective-permute-start(bf16[2,2,144,512]{3,2,1,0:T(8,128)(2,1)} %collective-permute-done.3.refs_2_), channel_id=1, source_target_pairs={{0,1},{1,0},{2,3},{3,2},{4,5},{5,4},{6,7},{7,6},{8,9},{9,8},{10,11... | collective-permute-start | bytes 1769480 | tf_op jit(solution)/shard_map/ppermute | solution.py:33
  68.3 10.5 %collective-permute-start.6 = (bf16[2,2,144,512]{3,2,1,0:T(8,128)(2,1)}, bf16[2,2,144,512]{3,2,1,0:T(8,128)(2,1)}, u32[]{:S(2)}, u32[]{:S(2)}) collective-permute-start(bf16[2,2,144,512]{3,2,1,0:T(8,128)(2,1)} %collective-permute-done.2.refs_1_), channel_id=1, source_target_pairs={{0,1},{1,0},{2,3},{3,2},{4,5},{5,4},{6,7},{7,6},{8,9},{9,8},{10,11... | collective-permute-start | bytes 1769480 | tf_op jit(solution)/shard_map/ppermute | solution.py:33
  70.7 8.8 %collective-permute-start.8 = (bf16[2,2,144,512]{3,2,1,0:T(8,128)(2,1)}, bf16[2,2,144,512]{3,2,1,0:T(8,128)(2,1)}, u32[]{:S(2)}, u32[]{:S(2)}) collective-permute-start(bf16[2,2,144,512]{3,2,1,0:T(8,128)(2,1)} %collective-permute-done.4.refs_3_), channel_id=1, source_target_pairs={{0,1},{1,0},{2,3},{3,2},{4,5},{5,4},{6,7},{7,6},{8,9},{9,8},{10,11... | collective-permute-start | bytes 1769480 | tf_op jit(solution)/shard_map/ppermute | solution.py:34
  75.6 3.8 %collective-permute-start.9 = (bf16[2,144,512]{2,1,0:T(8,128)(2,1)}, bf16[2,144,512]{2,1,0:T(8,128)(2,1)}, u32[]{:S(2)}, u32[]{:S(2)}) collective-permute-start(bf16[2,144,512]{2,1,0:T(8,128)(2,1)} %collective-permute-done.5.refs_4_), channel_id=1, source_target_pairs={{0,1},{1,0},{2,3},{3,2},{4,5},{5,4},{6,7},{7,6},{8,9},{9,8},{10,11... | collective-permute-start | bytes 884744 | tf_op jit(solution)/shard_map/ppermute | solution.py:34
  107.9 65.0 %all-to-all-start.3 = ((bf16[4,4,256,256]{3,2,1,0:T(8,128)(2,1)}), bf16[4,4,256,256]{3,2,1,0:T(8,128)(2,1)}, u32[]{:S(2)}, u32[]{:S(2)}) async-start(bf16[4,4,256,256]{3,2,1,0:T(8,128)(2,1)} %broadcast_in_dim.8), calls=%async_computation.3 | async-start | bytes 4194304 | tf_op jit(solution)/shard_map/all_to_all | solution.py:39
  112.5 9.0 %collective-permute-start.11 = (bf16[144,256]{1,0:T(8,128)(2,1)S(1)}, bf16[144,256]{1,0:T(8,128)(2,1)S(1)}, u32[]{:S(2)}, u32[]{:S(2)}) collective-permute-start(bf16[144,256]{1,0:T(8,128)(2,1)S(1)} %bitcast.35), channel_id=1, source_target_pairs={{0,16},{1,17},{2,48},{3,49},{4,80},{5,81},{6,112},{7,113},{8,144},... | collective-permute-start | bytes 221192 | tf_op jit(solution)/shard_map/ppermute | solution.py:224
  114.4 7.1 %collective-permute-start.10 = (bf16[144,256]{1,0:T(8,128)(2,1)S(1)}, bf16[144,256]{1,0:T(8,128)(2,1)S(1)}, u32[]{:S(2)}, u32[]{:S(2)}) collective-permute-start(bf16[144,256]{1,0:T(8,128)(2,1)S(1)} %bitcast.36), channel_id=1, source_target_pairs={{0,0},{1,1},{2,32},{3,33},{4,64},{5,65},{6,96},{7,97},{8,128},{9,1... | collective-permute-start | bytes 221192 | tf_op jit(solution)/shard_map/ppermute | solution.py:224
  121.5 5.8 %collective-permute-start.12 = (bf16[2,144,256]{2,1,0:T(8,128)(2,1)S(1)}, bf16[2,144,256]{2,1,0:T(8,128)(2,1)S(1)}, u32[]{:S(2)}, u32[]{:S(2)}) collective-permute-start(bf16[2,144,256]{2,1,0:T(8,128)(2,1)S(1)} %get-tuple-element.19), channel_id=1, source_target_pairs={{0,1},{1,0},{2,3},{3,2},{4,5},{5,4},{6,7},{7,6},{8,9},{9,8},{10,11... | collective-permute-start | bytes 442376 | tf_op jit(solution)/shard_map/ppermute | solution.py:23
  127.3 25.6 %collective-permute-start.13 = (bf16[2,2,144,256]{3,2,1,0:T(8,128)(2,1)S(1)}, bf16[2,2,144,256]{3,2,1,0:T(8,128)(2,1)S(1)}, u32[]{:S(2)}, u32[]{:S(2)}) collective-permute-start(bf16[2,2,144,256]{3,2,1,0:T(8,128)(2,1)S(1)} %pad_maximum_fusion.2.refs_0_), channel_id=1, source_target_pairs={{0,2},{1,15},{2,4},{3,1},{4,6},{5,3},{6,8},{7,5},{8,10},{9,7},{10,... | collective-permute-start | bytes 884744 | tf_op jit(solution)/shard_map/ppermute | solution.py:29
  140.8 14.0 %collective-permute-start.14 = (bf16[2,2,144,256]{3,2,1,0:T(8,128)(2,1)S(1)}, bf16[2,2,144,256]{3,2,1,0:T(8,128)(2,1)S(1)}, u32[]{:S(2)}, u32[]{:S(2)}) collective-permute-start(bf16[2,2,144,256]{3,2,1,0:T(8,128)(2,1)S(1)} %pad_maximum_fusion.2.refs_0_), channel_id=1, source_target_pairs={{0,4},{1,13},{2,6},{3,15},{4,8},{5,1},{6,10},{7,3},{8,12},{9,5},{1... | collective-permute-start | bytes 884744 | tf_op jit(solution)/shard_map/ppermute | solution.py:29
  143.4 13.8 %collective-permute-start.15 = (bf16[2,2,144,256]{3,2,1,0:T(8,128)(2,1)S(1)}, bf16[2,2,144,256]{3,2,1,0:T(8,128)(2,1)S(1)}, u32[]{:S(2)}, u32[]{:S(2)}) collective-permute-start(bf16[2,2,144,256]{3,2,1,0:T(8,128)(2,1)S(1)} %pad_maximum_fusion.2.refs_0_), channel_id=1, source_target_pairs={{0,6},{1,11},{2,8},{3,13},{4,10},{5,15},{6,12},{7,1},{8,14},{9,3},... | collective-permute-start | bytes 884744 | tf_op jit(solution)/shard_map/ppermute | solution.py:29
  148.4 20.4 %collective-permute-start.16 = (bf16[2,144,256]{2,1,0:T(8,128)(2,1)S(1)}, bf16[2,144,256]{2,1,0:T(8,128)(2,1)S(1)}, u32[]{:S(2)}, u32[]{:S(2)}) collective-permute-start(bf16[2,144,256]{2,1,0:T(8,128)(2,1)S(1)} %get-tuple-element.19), channel_id=1, source_target_pairs={{0,8},{1,9},{2,10},{3,11},{4,12},{5,13},{6,14},{7,15},{8,0},{9,1},... | collective-permute-start | bytes 442376 | tf_op jit(solution)/shard_map/ppermute | solution.py:29
  152.9 19.2 %collective-permute-start.17 = (bf16[2,2,144,256]{3,2,1,0:T(8,128)(2,1)S(1)}, bf16[2,2,144,256]{3,2,1,0:T(8,128)(2,1)S(1)}, u32[]{:S(2)}, u32[]{:S(2)}) collective-permute-start(bf16[2,2,144,256]{3,2,1,0:T(8,128)(2,1)S(1)} %collective-permute-done.13.refs_1_), channel_id=1, source_target_pairs={{0,1},{1,0},{2,3},{3,2},{4,5},{5,4},{6,7},{7,6},{8,9},{9,8},{10,11... | collective-permute-start | bytes 884744 | tf_op jit(solution)/shard_map/ppermute | solution.py:33
  154.9 17.2 %collective-permute-start.18 = (bf16[2,2,144,256]{3,2,1,0:T(8,128)(2,1)S(1)}, bf16[2,2,144,256]{3,2,1,0:T(8,128)(2,1)S(1)}, u32[]{:S(2)}, u32[]{:S(2)}) collective-permute-start(bf16[2,2,144,256]{3,2,1,0:T(8,128)(2,1)S(1)} %collective-permute-done.14.refs_2_), channel_id=1, source_target_pairs={{0,1},{1,0},{2,3},{3,2},{4,5},{5,4},{6,7},{7,6},{8,9},{9,8},{10,11... | collective-permute-start | bytes 884744 | tf_op jit(solution)/shard_map/ppermute | solution.py:33
  157.3 14.8 %collective-permute-start.19 = (bf16[2,2,144,256]{3,2,1,0:T(8,128)(2,1)S(1)}, bf16[2,2,144,256]{3,2,1,0:T(8,128)(2,1)S(1)}, u32[]{:S(2)}, u32[]{:S(2)}) collective-permute-start(bf16[2,2,144,256]{3,2,1,0:T(8,128)(2,1)S(1)} %collective-permute-done.15.refs_3_), channel_id=1, source_target_pairs={{0,1},{1,0},{2,3},{3,2},{4,5},{5,4},{6,7},{7,6},{8,9},{9,8},{10,11... | collective-permute-start | bytes 884744 | tf_op jit(solution)/shard_map/ppermute | solution.py:34
  176.0 21.7 %all-to-all-start.4 = ((f32[16,8,256]{2,1,0:T(8,128)}), f32[16,8,256]{2,1,0:T(8,128)S(1)}, u32[]{:S(2)}, u32[]{:S(2)}) async-start(f32[16,8,256]{2,1,0:T(8,128)} %get-tuple-element.12), calls=%async_computation.4 | async-start | bytes 262144 | tf_op jit(solution)/shard_map/all_to_all | solution.py:39
  (6 other events, 120.9 us)

commit v5 on v4

--- a/solution.py
+++ b/solution.py
@@ -28,7 +28,8 @@
         up_down = [((z, c), ((z + (s if c == 0 else -s)) % 8, c)) for z in range(8) for c in range(2)]
         return lax.ppermute(x, ("z", "c"), [(2 * a + b, 2 * d + e) for (a, b), (d, e) in up_down])
 
-    one, two = send(own, 1), send(own, 2)
+    two = send(own, 2)
+    one = send(own, 1)
     three, four = (send(two, 1), send(two[0], 2)) if relay else (send(own, 3), send(own[0], 4))
     near = [lax.ppermute(p, "c", ring(2, 1)) for p in (one, two)]
     far = [lax.ppermute(p, "c", ring(2, 1)) for p in (three, four)]
@@ -225,7 +226,7 @@
 
     wo_here = turned(0)
     wo = jnp.stack([wo_here, turned(8)])
-    wo_pieces = z_pieces(both_cores(wo), False)
+    wo_pieces = z_pieces(both_cores(wo), True)
 
     half_width = HEAD // 2
     frequency = 10000.0 ** (-jnp.arange(half_width, dtype=F32) / half_width)

time: 200 us -> 192 us (0.960)
  starting transfers between devices: 115 us -> 103 us
  waiting for transfers between devices: 41.6 us -> 46.4 us
    ppermute x4, starting transfers between devices: 17.7 us -> 8.51 us  [z_pieces(): far = [lax.ppermute(p, 'c', ring(2, 1)) for p in (three, four)]]
    ppermute x8, waiting for transfers between devices: 7.31 us -> 12.2 us  [send(): lax.ppermute(x, ('z', 'c'), [(2 * a + b, 2 * d + e) for (a, b), (d, e) in...]
  transfers between devices with their start and end apart: 25 -> 25, of which waited for: 9 -> 10; matrix products, arithmetic and copies ran while one was open for 3% -> 3% of each run, Pallas kernels for 1% -> 1%
where the time goes in v5:
time: 192 us; the launch traced here: 191 us
  starting transfers between devices  103 us (54%)
  waiting for transfers between devices  46.4 us (24%)
  blocking collectives  21.8 us (11%)
  Pallas kernels  11.9 us (6%)
  local copies, waits for them, and re-layouts  4.96 us (3%)
  other arithmetic  2.66 us (1%)
    ppermute x8, starting transfers between devices, send(): lax.ppermute(x, ('z', 'c'), [(2 * a + b, 2 * d + e) for (a, b), (d, e) in...  44.8 us
    all_to_all x4, starting transfers between devices, exchanged(): return lax.all_to_all(x, axis, split_axis=0, concat_axis=0, tiled=True)  27.4 us
    all_to_all x1, blocking collectives, exchanged(): return lax.all_to_all(x, axis, split_axis=0, concat_axis=0, tiled=True)  21.8 us
    ppermute x1, waiting for transfers between devices, per_device(): w_pair = lax.ppermute(w, 'yl', ring(2, 1))  14.7 us
    ppermute x8, waiting for transfers between devices, send(): lax.ppermute(x, ('z', 'c'), [(2 * a + b, 2 * d + e) for (a, b), (d, e) in...  12.2 us
    all_to_all x4, waiting for transfers between devices, exchanged(): return lax.all_to_all(x, axis, split_axis=0, concat_axis=0, tiled=True)  9.39 us
    ppermute x4, starting transfers between devices, z_pieces(): near = [lax.ppermute(p, 'c', ring(2, 1)) for p in (one, two)]  8.66 us
    ppermute x4, starting transfers between devices, z_pieces(): far = [lax.ppermute(p, 'c', ring(2, 1)) for p in (three, four)]  8.51 us
  transfers between devices with their start and end apart: 25, of which 10 were waited for; matrix products, arithmetic and copies ran while one was open for 3% of the time, Pallas kernels for 1%

profile of v5, /device:TPU:1, one launch (start us, length us, event | category | flops | bytes accessed | tf_op | source)
XLA Modules:
  0.0 191.3 jit_solution(1211356605595364088)
XLA Ops:
  2.6 7.6 %all-to-all-start = ((bf16[4,296,256]{2,1,0:T(8,128)(2,1)}), bf16[4,296,256]{2,1,0:T(8,128)(2,1)S(1)}, u32[]{:S(2)}, u32[]{:S(2)}) async-start(bf16[4,296,256]{2,1,0:T(8,128)(2,1)} %get-tuple-element.8), calls=%async_computation | async-start | bytes 1212416 | tf_op jit(solution)/shard_map/all_to_all | solution.py:40
  10.2 2.3 %collective-permute-start = (bf16[144,512]{1,0:T(8,128)(2,1)}, bf16[144,512]{1,0:T(8,128)(2,1)S(1)}, u32[]{:S(2)}, u32[]{:S(2)}) collective-permute-start(bf16[144,512]{1,0:T(8,128)(2,1)} %get-tuple-element.10), channel_id=1, source_target_pairs={{0,16},{16,0},{1,17},{17,1},{2,18},{18,2},{3,19},{19,3},{4,20},{20... | collective-permute-start | bytes 442376 | tf_op jit(solution)/shard_map/ppermute | solution.py:201
  12.5 14.7 %collective-permute-done = bf16[144,512]{1,0:T(8,128)(2,1)S(1)} collective-permute-done((bf16[144,512]{1,0:T(8,128)(2,1)}, bf16[144,512]{1,0:T(8,128)(2,1)S(1)}, u32[]{:S(2)}, u32[]{:S(2)}) %collective-permute-start) | collective-permute-done | bytes 147488 | tf_op jit(solution)/shard_map/ppermute | solution.py:201
  28.1 3.4 %collective-permute-start.1 = (bf16[2,144,512]{2,1,0:T(8,128)(2,1)S(1)}, bf16[2,144,512]{2,1,0:T(8,128)(2,1)S(1)}, u32[]{:S(2)}, u32[]{:S(2)}) collective-permute-start(bf16[2,144,512]{2,1,0:T(8,128)(2,1)S(1)} %get-tuple-element.17), channel_id=1, source_target_pairs={{0,1},{1,0},{2,3},{3,2},{4,5},{5,4},{6,7},{7,6},{8,9},{9,8},{10,11... | collective-permute-start | bytes 884744 | tf_op jit(solution)/shard_map/ppermute | solution.py:23
  32.8 10.7 %collective-permute-start.3 = (bf16[2,2,144,512]{3,2,1,0:T(8,128)(2,1)S(1)}, bf16[2,2,144,512]{3,2,1,0:T(8,128)(2,1)}, u32[]{:S(2)}, u32[]{:S(2)}) collective-permute-start(bf16[2,2,144,512]{3,2,1,0:T(8,128)(2,1)S(1)} %pad_maximum_fusion.refs_0_), channel_id=1, source_target_pairs={{0,4},{1,13},{2,6},{3,15},{4,8},{5,1},{6,10},{7,3},{8,12},{9,5},{1... | collective-permute-start | bytes 1769480 | tf_op jit(solution)/shard_map/ppermute | solution.py:29
  45.1 4.1 %all-to-all-start.1 = ((bf16[4,4,296,256]{3,2,1,0:T(8,128)(2,1)}), bf16[4,4,296,256]{3,2,1,0:T(8,128)(2,1)S(1)}, u32[]{:S(2)}, u32[]{:S(2)}) async-start(bf16[4,4,296,256]{3,2,1,0:T(8,128)(2,1)} %broadcast_in_dim.7), calls=%async_computation.1 | async-start | bytes 4849664 | tf_op jit(solution)/shard_map/all_to_all | solution.py:40
  51.4 5.2 %collective-permute-done.3.refs_2_ = bf16[2,2,144,512]{3,2,1,0:T(8,128)(2,1)} collective-permute-done((bf16[2,2,144,512]{3,2,1,0:T(8,128)(2,1)S(1)}, bf16[2,2,144,512]{3,2,1,0:T(8,128)(2,1)}, u32[]{:S(2)}, u32[]{:S(2)}) %collective-permute-start.3) | collective-permute-done | bytes 589856 | tf_op jit(solution)/shard_map/ppermute | solution.py:29
  56.6 3.2 %collective-permute-start.4 = (bf16[2,2,144,512]{3,2,1,0:T(8,128)(2,1)}, bf16[2,2,144,512]{3,2,1,0:T(8,128)(2,1)}, u32[]{:S(2)}, u32[]{:S(2)}) collective-permute-start(bf16[2,2,144,512]{3,2,1,0:T(8,128)(2,1)} %collective-permute-done.3.refs_2_), channel_id=1, source_target_pairs={{0,2},{1,15},{2,4},{3,1},{4,6},{5,3},{6,8},{7,5},{8,10},{9,7},{10,... | collective-permute-start | bytes 1769480 | tf_op jit(solution)/shard_map/ppermute | solution.py:29
  61.5 4.8 %collective-permute-start.5 = (bf16[2,144,512]{2,1,0:T(8,128)(2,1)}, bf16[2,144,512]{2,1,0:T(8,128)(2,1)}, u32[]{:S(2)}, u32[]{:S(2)}) collective-permute-start(bf16[2,144,512]{2,1,0:T(8,128)(2,1)} %slice_bitcast_fusion), channel_id=1, source_target_pairs={{0,4},{1,13},{2,6},{3,15},{4,8},{5,1},{6,10},{7,3},{8,12},{9,5},{1... | collective-permute-start | bytes 884744 | tf_op jit(solution)/shard_map/ppermute | solution.py:29
  68.3 2.4 %collective-permute-start.6 = (bf16[2,2,144,512]{3,2,1,0:T(8,128)(2,1)}, bf16[2,2,144,512]{3,2,1,0:T(8,128)(2,1)}, u32[]{:S(2)}, u32[]{:S(2)}) collective-permute-start(bf16[2,2,144,512]{3,2,1,0:T(8,128)(2,1)} %collective-permute-done.2.refs_1_), channel_id=1, source_target_pairs={{0,1},{1,0},{2,3},{3,2},{4,5},{5,4},{6,7},{7,6},{8,9},{9,8},{10,11... | collective-permute-start | bytes 1769480 | tf_op jit(solution)/shard_map/ppermute | solution.py:34
  79.4 5.1 %attend.1 = bf16[4,256,256]{2,1,0:T(8,128)(2,1)S(1)} custom-call(s32[3]{0:T(128)S(1)} %pad_add_fusion.pos, bf16[256,4608]{1,0:T(8,128)(2,1)S(1)} %get-tuple-element.9.normed, f32[256,64]{1,0:T(8,128)S(1)} %get-tuple-element.23.cos, f32[256,64]{1,0:T(8,128)S(1)} %get-tuple-element.22.sin, f32[256,256]{1,0:T(8,128)S(1)} %fusion.1.mask, ...), custom_call_target="tpu_custom_call" | custom-call | tf_op jit(solution)/shard_map/attend/pallas_call | solution.py:238
  84.5 21.8 %all_to_all.25 = bf16[4,256,256]{2,1,0:T(8,128)(2,1)S(1)} all-to-all(bf16[4,256,256]{2,1,0:T(8,128)(2,1)S(1)} %attend.1), channel_id=1, replica_groups=mesh['hx'=4,'hy'=4,'yl'=2,'z'=8,'c'=2] {'hx'}, dimensions={0} | all-to-all | bytes 1048576 | tf_op jit(solution)/shard_map/all_to_all | solution.py:40
  107.9 4.6 %all-to-all-start.3 = ((bf16[4,4,256,256]{3,2,1,0:T(8,128)(2,1)}), bf16[4,4,256,256]{3,2,1,0:T(8,128)(2,1)}, u32[]{:S(2)}, u32[]{:S(2)}) async-start(bf16[4,4,256,256]{3,2,1,0:T(8,128)(2,1)} %broadcast_in_dim.8), calls=%async_computation.3 | async-start | bytes 4194304 | tf_op jit(solution)/shard_map/all_to_all | solution.py:40
  115.1 6.4 %collective-permute-done.11 = bf16[144,256]{1,0:T(8,128)(2,1)S(1)} collective-permute-done((bf16[144,256]{1,0:T(8,128)(2,1)S(1)}, bf16[144,256]{1,0:T(8,128)(2,1)S(1)}, u32[]{:S(2)}, u32[]{:S(2)}) %collective-permute-start.11) | collective-permute-done | bytes 73760 | tf_op jit(solution)/shard_map/ppermute | solution.py:225
  121.5 4.8 %collective-permute-start.12 = (bf16[2,144,256]{2,1,0:T(8,128)(2,1)S(1)}, bf16[2,144,256]{2,1,0:T(8,128)(2,1)S(1)}, u32[]{:S(2)}, u32[]{:S(2)}) collective-permute-start(bf16[2,144,256]{2,1,0:T(8,128)(2,1)S(1)} %get-tuple-element.19), channel_id=1, source_target_pairs={{0,1},{1,0},{2,3},{3,2},{4,5},{5,4},{6,7},{7,6},{8,9},{9,8},{10,11... | collective-permute-start | bytes 442376 | tf_op jit(solution)/shard_map/ppermute | solution.py:23
  127.3 14.2 %collective-permute-start.14 = (bf16[2,2,144,256]{3,2,1,0:T(8,128)(2,1)S(1)}, bf16[2,2,144,256]{3,2,1,0:T(8,128)(2,1)S(1)}, u32[]{:S(2)}, u32[]{:S(2)}) collective-permute-start(bf16[2,2,144,256]{3,2,1,0:T(8,128)(2,1)S(1)} %pad_maximum_fusion.2.refs_0_), channel_id=1, source_target_pairs={{0,4},{1,13},{2,6},{3,15},{4,8},{5,1},{6,10},{7,3},{8,12},{9,5},{1... | collective-permute-start | bytes 884744 | tf_op jit(solution)/shard_map/ppermute | solution.py:29
  143.4 4.9 %collective-permute-done.14.refs_2_ = bf16[2,2,144,256]{3,2,1,0:T(8,128)(2,1)S(1)} collective-permute-done((bf16[2,2,144,256]{3,2,1,0:T(8,128)(2,1)S(1)}, bf16[2,2,144,256]{3,2,1,0:T(8,128)(2,1)S(1)}, u32[]{:S(2)}, u32[]{:S(2)}) %collective-permute-start.14) | collective-permute-done | bytes 294944 | tf_op jit(solution)/shard_map/ppermute | solution.py:29
  148.4 2.5 %collective-permute-start.15 = (bf16[2,2,144,256]{3,2,1,0:T(8,128)(2,1)S(1)}, bf16[2,2,144,256]{3,2,1,0:T(8,128)(2,1)S(1)}, u32[]{:S(2)}, u32[]{:S(2)}) collective-permute-start(bf16[2,2,144,256]{3,2,1,0:T(8,128)(2,1)S(1)} %collective-permute-done.14.refs_2_), channel_id=1, source_target_pairs={{0,2},{1,15},{2,4},{3,1},{4,6},{5,3},{6,8},{7,5},{8,10},{9,7},{10,... | collective-permute-start | bytes 884744 | tf_op jit(solution)/shard_map/ppermute | solution.py:29
  150.9 5.4 %collective-permute-start.16 = (bf16[2,144,256]{2,1,0:T(8,128)(2,1)S(1)}, bf16[2,144,256]{2,1,0:T(8,128)(2,1)S(1)}, u32[]{:S(2)}, u32[]{:S(2)}) collective-permute-start(bf16[2,144,256]{2,1,0:T(8,128)(2,1)S(1)} %slice_bitcast_fusion.1), channel_id=1, source_target_pairs={{0,4},{1,13},{2,6},{3,15},{4,8},{5,1},{6,10},{7,3},{8,12},{9,5},{1... | collective-permute-start | bytes 442376 | tf_op jit(solution)/shard_map/ppermute | solution.py:29
  158.2 2.4 %collective-permute-start.18 = (bf16[2,2,144,256]{3,2,1,0:T(8,128)(2,1)S(1)}, bf16[2,2,144,256]{3,2,1,0:T(8,128)(2,1)S(1)}, u32[]{:S(2)}, u32[]{:S(2)}) collective-permute-start(bf16[2,2,144,256]{3,2,1,0:T(8,128)(2,1)S(1)} %collective-permute-done.14.refs_2_), channel_id=1, source_target_pairs={{0,1},{1,0},{2,3},{3,2},{4,5},{5,4},{6,7},{7,6},{8,9},{9,8},{10,11... | collective-permute-start | bytes 884744 | tf_op jit(solution)/shard_map/ppermute | solution.py:34
  162.6 2.4 %collective-permute-start.20 = (bf16[2,144,256]{2,1,0:T(8,128)(2,1)S(1)}, bf16[2,144,256]{2,1,0:T(8,128)(2,1)S(1)}, u32[]{:S(2)}, u32[]{:S(2)}) collective-permute-start(bf16[2,144,256]{2,1,0:T(8,128)(2,1)S(1)} %collective-permute-done.16.refs_4_), channel_id=1, source_target_pairs={{0,1},{1,0},{2,3},{3,2},{4,5},{5,4},{6,7},{7,6},{8,9},{9,8},{10,11... | collective-permute-start | bytes 442376 | tf_op jit(solution)/shard_map/ppermute | solution.py:35
  166.7 3.1 %project_out.1 = (f32[288,256]{1,0:T(8,128)S(1)}, f32[16,8,256]{2,1,0:T(8,128)}) custom-call(bf16[288,256]{1,0:T(8,128)(2,1)S(1)} %bitcast.27, f32[288,1]{1,0:T(8,128)S(1)} %broadcast_in_dim.9.gain, bf16[4,4,256,256]{3,2,1,0:T(8,128)(2,1)} %all-to-all-done.3.att, bf16[16,2,144,256]{3,2,1,0:T(8,128)(2,1)S(1)} %place.1.rows), custom_call_target="tpu_custom_call" | custom-call | tf_op jit(solution)/shard_map/project_out/pallas_call | solution.py:265
  169.9 11.1 %all-to-all-start.4 = ((f32[16,8,256]{2,1,0:T(8,128)}), f32[16,8,256]{2,1,0:T(8,128)S(1)}, u32[]{:S(2)}, u32[]{:S(2)}) async-start(f32[16,8,256]{2,1,0:T(8,128)} %get-tuple-element.12), calls=%async_computation.4 | async-start | bytes 262144 | tf_op jit(solution)/shard_map/all_to_all | solution.py:40
  181.0 9.4 %all-to-all-done.4 = f32[16,8,256]{2,1,0:T(8,128)S(1)} async-done(((f32[16,8,256]{2,1,0:T(8,128)}), f32[16,8,256]{2,1,0:T(8,128)S(1)}, u32[]{:S(2)}, u32[]{:S(2)}) %all-to-all-start.4) | async-done | bytes 131104 | tf_op jit(solution)/shard_map/all_to_all | solution.py:40
  (61 shorter events, 33.7 us)
Async XLA Ops:
  2.6 40.9 %all-to-all-start = ((bf16[4,296,256]{2,1,0:T(8,128)(2,1)}), bf16[4,296,256]{2,1,0:T(8,128)(2,1)S(1)}, u32[]{:S(2)}, u32[]{:S(2)}) async-start(bf16[4,296,256]{2,1,0:T(8,128)(2,1)} %get-tuple-element.8), calls=%async_computation | async-start | bytes 1212416 | tf_op jit(solution)/shard_map/all_to_all | solution.py:40
  10.2 17.0 %collective-permute-start = (bf16[144,512]{1,0:T(8,128)(2,1)}, bf16[144,512]{1,0:T(8,128)(2,1)S(1)}, u32[]{:S(2)}, u32[]{:S(2)}) collective-permute-start(bf16[144,512]{1,0:T(8,128)(2,1)} %get-tuple-element.10), channel_id=1, source_target_pairs={{0,16},{16,0},{1,17},{17,1},{2,18},{18,2},{3,19},{19,3},{4,20},{20... | collective-permute-start | bytes 442376 | tf_op jit(solution)/shard_map/ppermute | solution.py:201
  28.1 4.6 %collective-permute-start.1 = (bf16[2,144,512]{2,1,0:T(8,128)(2,1)S(1)}, bf16[2,144,512]{2,1,0:T(8,128)(2,1)S(1)}, u32[]{:S(2)}, u32[]{:S(2)}) collective-permute-start(bf16[2,144,512]{2,1,0:T(8,128)(2,1)S(1)} %get-tuple-element.17), channel_id=1, source_target_pairs={{0,1},{1,0},{2,3},{3,2},{4,5},{5,4},{6,7},{7,6},{8,9},{9,8},{10,11... | collective-permute-start | bytes 884744 | tf_op jit(solution)/shard_map/ppermute | solution.py:23
  32.8 23.8 %collective-permute-start.3 = (bf16[2,2,144,512]{3,2,1,0:T(8,128)(2,1)S(1)}, bf16[2,2,144,512]{3,2,1,0:T(8,128)(2,1)}, u32[]{:S(2)}, u32[]{:S(2)}) collective-permute-start(bf16[2,2,144,512]{3,2,1,0:T(8,128)(2,1)S(1)} %pad_maximum_fusion.refs_0_), channel_id=1, source_target_pairs={{0,4},{1,13},{2,6},{3,15},{4,8},{5,1},{6,10},{7,3},{8,12},{9,5},{1... | collective-permute-start | bytes 1769480 | tf_op jit(solution)/shard_map/ppermute | solution.py:29
  45.1 32.7 %all-to-all-start.1 = ((bf16[4,4,296,256]{3,2,1,0:T(8,128)(2,1)}), bf16[4,4,296,256]{3,2,1,0:T(8,128)(2,1)S(1)}, u32[]{:S(2)}, u32[]{:S(2)}) async-start(bf16[4,4,296,256]{3,2,1,0:T(8,128)(2,1)} %broadcast_in_dim.7), calls=%async_computation.1 | async-start | bytes 4849664 | tf_op jit(solution)/shard_map/all_to_all | solution.py:40
  49.2 19.0 %collective-permute-start.2 = (bf16[2,2,144,512]{3,2,1,0:T(8,128)(2,1)S(1)}, bf16[2,2,144,512]{3,2,1,0:T(8,128)(2,1)}, u32[]{:S(2)}, u32[]{:S(2)}) collective-permute-start(bf16[2,2,144,512]{3,2,1,0:T(8,128)(2,1)S(1)} %pad_maximum_fusion.refs_0_), channel_id=1, source_target_pairs={{0,2},{1,15},{2,4},{3,1},{4,6},{5,3},{6,8},{7,5},{8,10},{9,7},{10,... | collective-permute-start | bytes 1769480 | tf_op jit(solution)/shard_map/ppermute | solution.py:29
  56.6 14.1 %collective-permute-start.4 = (bf16[2,2,144,512]{3,2,1,0:T(8,128)(2,1)}, bf16[2,2,144,512]{3,2,1,0:T(8,128)(2,1)}, u32[]{:S(2)}, u32[]{:S(2)}) collective-permute-start(bf16[2,2,144,512]{3,2,1,0:T(8,128)(2,1)} %collective-permute-done.3.refs_2_), channel_id=1, source_target_pairs={{0,2},{1,15},{2,4},{3,1},{4,6},{5,3},{6,8},{7,5},{8,10},{9,7},{10,... | collective-permute-start | bytes 1769480 | tf_op jit(solution)/shard_map/ppermute | solution.py:29
  61.5 14.1 %collective-permute-start.5 = (bf16[2,144,512]{2,1,0:T(8,128)(2,1)}, bf16[2,144,512]{2,1,0:T(8,128)(2,1)}, u32[]{:S(2)}, u32[]{:S(2)}) collective-permute-start(bf16[2,144,512]{2,1,0:T(8,128)(2,1)} %slice_bitcast_fusion), channel_id=1, source_target_pairs={{0,4},{1,13},{2,6},{3,15},{4,8},{5,1},{6,10},{7,3},{8,12},{9,5},{1... | collective-permute-start | bytes 884744 | tf_op jit(solution)/shard_map/ppermute | solution.py:29
  66.3 12.5 %collective-permute-start.7 = (bf16[2,2,144,512]{3,2,1,0:T(8,128)(2,1)}, bf16[2,2,144,512]{3,2,1,0:T(8,128)(2,1)}, u32[]{:S(2)}, u32[]{:S(2)}) collective-permute-start(bf16[2,2,144,512]{3,2,1,0:T(8,128)(2,1)} %collective-permute-done.3.refs_2_), channel_id=1, source_target_pairs={{0,1},{1,0},{2,3},{3,2},{4,5},{5,4},{6,7},{7,6},{8,9},{9,8},{10,11... | collective-permute-start | bytes 1769480 | tf_op jit(solution)/shard_map/ppermute | solution.py:34
  68.3 10.5 %collective-permute-start.6 = (bf16[2,2,144,512]{3,2,1,0:T(8,128)(2,1)}, bf16[2,2,144,512]{3,2,1,0:T(8,128)(2,1)}, u32[]{:S(2)}, u32[]{:S(2)}) collective-permute-start(bf16[2,2,144,512]{3,2,1,0:T(8,128)(2,1)} %collective-permute-done.2.refs_1_), channel_id=1, source_target_pairs={{0,1},{1,0},{2,3},{3,2},{4,5},{5,4},{6,7},{7,6},{8,9},{9,8},{10,11... | collective-permute-start | bytes 1769480 | tf_op jit(solution)/shard_map/ppermute | solution.py:34
  70.7 8.8 %collective-permute-start.8 = (bf16[2,2,144,512]{3,2,1,0:T(8,128)(2,1)}, bf16[2,2,144,512]{3,2,1,0:T(8,128)(2,1)}, u32[]{:S(2)}, u32[]{:S(2)}) collective-permute-start(bf16[2,2,144,512]{3,2,1,0:T(8,128)(2,1)} %collective-permute-done.4.refs_3_), channel_id=1, source_target_pairs={{0,1},{1,0},{2,3},{3,2},{4,5},{5,4},{6,7},{7,6},{8,9},{9,8},{10,11... | collective-permute-start | bytes 1769480 | tf_op jit(solution)/shard_map/ppermute | solution.py:35
  75.6 3.8 %collective-permute-start.9 = (bf16[2,144,512]{2,1,0:T(8,128)(2,1)}, bf16[2,144,512]{2,1,0:T(8,128)(2,1)}, u32[]{:S(2)}, u32[]{:S(2)}) collective-permute-start(bf16[2,144,512]{2,1,0:T(8,128)(2,1)} %collective-permute-done.5.refs_4_), channel_id=1, source_target_pairs={{0,1},{1,0},{2,3},{3,2},{4,5},{5,4},{6,7},{7,6},{8,9},{9,8},{10,11... | collective-permute-start | bytes 884744 | tf_op jit(solution)/shard_map/ppermute | solution.py:35
  107.9 58.9 %all-to-all-start.3 = ((bf16[4,4,256,256]{3,2,1,0:T(8,128)(2,1)}), bf16[4,4,256,256]{3,2,1,0:T(8,128)(2,1)}, u32[]{:S(2)}, u32[]{:S(2)}) async-start(bf16[4,4,256,256]{3,2,1,0:T(8,128)(2,1)} %broadcast_in_dim.8), calls=%async_computation.3 | async-start | bytes 4194304 | tf_op jit(solution)/shard_map/all_to_all | solution.py:40
  112.5 9.0 %collective-permute-start.11 = (bf16[144,256]{1,0:T(8,128)(2,1)S(1)}, bf16[144,256]{1,0:T(8,128)(2,1)S(1)}, u32[]{:S(2)}, u32[]{:S(2)}) collective-permute-start(bf16[144,256]{1,0:T(8,128)(2,1)S(1)} %bitcast.37), channel_id=1, source_target_pairs={{0,16},{1,17},{2,48},{3,49},{4,80},{5,81},{6,112},{7,113},{8,144},... | collective-permute-start | bytes 221192 | tf_op jit(solution)/shard_map/ppermute | solution.py:225
  114.4 7.1 %collective-permute-start.10 = (bf16[144,256]{1,0:T(8,128)(2,1)S(1)}, bf16[144,256]{1,0:T(8,128)(2,1)S(1)}, u32[]{:S(2)}, u32[]{:S(2)}) collective-permute-start(bf16[144,256]{1,0:T(8,128)(2,1)S(1)} %bitcast.38), channel_id=1, source_target_pairs={{0,0},{1,1},{2,32},{3,33},{4,64},{5,65},{6,96},{7,97},{8,128},{9,1... | collective-permute-start | bytes 221192 | tf_op jit(solution)/shard_map/ppermute | solution.py:225
  121.5 5.8 %collective-permute-start.12 = (bf16[2,144,256]{2,1,0:T(8,128)(2,1)S(1)}, bf16[2,144,256]{2,1,0:T(8,128)(2,1)S(1)}, u32[]{:S(2)}, u32[]{:S(2)}) collective-permute-start(bf16[2,144,256]{2,1,0:T(8,128)(2,1)S(1)} %get-tuple-element.19), channel_id=1, source_target_pairs={{0,1},{1,0},{2,3},{3,2},{4,5},{5,4},{6,7},{7,6},{8,9},{9,8},{10,11... | collective-permute-start | bytes 442376 | tf_op jit(solution)/shard_map/ppermute | solution.py:23
  127.3 21.0 %collective-permute-start.14 = (bf16[2,2,144,256]{3,2,1,0:T(8,128)(2,1)S(1)}, bf16[2,2,144,256]{3,2,1,0:T(8,128)(2,1)S(1)}, u32[]{:S(2)}, u32[]{:S(2)}) collective-permute-start(bf16[2,2,144,256]{3,2,1,0:T(8,128)(2,1)S(1)} %pad_maximum_fusion.2.refs_0_), channel_id=1, source_target_pairs={{0,4},{1,13},{2,6},{3,15},{4,8},{5,1},{6,10},{7,3},{8,12},{9,5},{1... | collective-permute-start | bytes 884744 | tf_op jit(solution)/shard_map/ppermute | solution.py:29
  141.5 14.8 %collective-permute-start.13 = (bf16[2,2,144,256]{3,2,1,0:T(8,128)(2,1)S(1)}, bf16[2,2,144,256]{3,2,1,0:T(8,128)(2,1)S(1)}, u32[]{:S(2)}, u32[]{:S(2)}) collective-permute-start(bf16[2,2,144,256]{3,2,1,0:T(8,128)(2,1)S(1)} %pad_maximum_fusion.2.refs_0_), channel_id=1, source_target_pairs={{0,2},{1,15},{2,4},{3,1},{4,6},{5,3},{6,8},{7,5},{8,10},{9,7},{10,... | collective-permute-start | bytes 884744 | tf_op jit(solution)/shard_map/ppermute | solution.py:29
  148.4 12.3 %collective-permute-start.15 = (bf16[2,2,144,256]{3,2,1,0:T(8,128)(2,1)S(1)}, bf16[2,2,144,256]{3,2,1,0:T(8,128)(2,1)S(1)}, u32[]{:S(2)}, u32[]{:S(2)}) collective-permute-start(bf16[2,2,144,256]{3,2,1,0:T(8,128)(2,1)S(1)} %collective-permute-done.14.refs_2_), channel_id=1, source_target_pairs={{0,2},{1,15},{2,4},{3,1},{4,6},{5,3},{6,8},{7,5},{8,10},{9,7},{10,... | collective-permute-start | bytes 884744 | tf_op jit(solution)/shard_map/ppermute | solution.py:29
  150.9 11.7 %collective-permute-start.16 = (bf16[2,144,256]{2,1,0:T(8,128)(2,1)S(1)}, bf16[2,144,256]{2,1,0:T(8,128)(2,1)S(1)}, u32[]{:S(2)}, u32[]{:S(2)}) collective-permute-start(bf16[2,144,256]{2,1,0:T(8,128)(2,1)S(1)} %slice_bitcast_fusion.1), channel_id=1, source_target_pairs={{0,4},{1,13},{2,6},{3,15},{4,8},{5,1},{6,10},{7,3},{8,12},{9,5},{1... | collective-permute-start | bytes 442376 | tf_op jit(solution)/shard_map/ppermute | solution.py:29
  156.3 8.8 %collective-permute-start.17 = (bf16[2,2,144,256]{3,2,1,0:T(8,128)(2,1)S(1)}, bf16[2,2,144,256]{3,2,1,0:T(8,128)(2,1)S(1)}, u32[]{:S(2)}, u32[]{:S(2)}) collective-permute-start(bf16[2,2,144,256]{3,2,1,0:T(8,128)(2,1)S(1)} %collective-permute-done.13.refs_1_), channel_id=1, source_target_pairs={{0,1},{1,0},{2,3},{3,2},{4,5},{5,4},{6,7},{7,6},{8,9},{9,8},{10,11... | collective-permute-start | bytes 884744 | tf_op jit(solution)/shard_map/ppermute | solution.py:34
  158.2 6.9 %collective-permute-start.18 = (bf16[2,2,144,256]{3,2,1,0:T(8,128)(2,1)S(1)}, bf16[2,2,144,256]{3,2,1,0:T(8,128)(2,1)S(1)}, u32[]{:S(2)}, u32[]{:S(2)}) collective-permute-start(bf16[2,2,144,256]{3,2,1,0:T(8,128)(2,1)S(1)} %collective-permute-done.14.refs_2_), channel_id=1, source_target_pairs={{0,1},{1,0},{2,3},{3,2},{4,5},{5,4},{6,7},{7,6},{8,9},{9,8},{10,11... | collective-permute-start | bytes 884744 | tf_op jit(solution)/shard_map/ppermute | solution.py:34
  160.7 5.3 %collective-permute-start.19 = (bf16[2,2,144,256]{3,2,1,0:T(8,128)(2,1)S(1)}, bf16[2,2,144,256]{3,2,1,0:T(8,128)(2,1)S(1)}, u32[]{:S(2)}, u32[]{:S(2)}) collective-permute-start(bf16[2,2,144,256]{3,2,1,0:T(8,128)(2,1)S(1)} %collective-permute-done.15.refs_3_), channel_id=1, source_target_pairs={{0,1},{1,0},{2,3},{3,2},{4,5},{5,4},{6,7},{7,6},{8,9},{9,8},{10,11... | collective-permute-start | bytes 884744 | tf_op jit(solution)/shard_map/ppermute | solution.py:35
  169.9 20.5 %all-to-all-start.4 = ((f32[16,8,256]{2,1,0:T(8,128)}), f32[16,8,256]{2,1,0:T(8,128)S(1)}, u32[]{:S(2)}, u32[]{:S(2)}) async-start(f32[16,8,256]{2,1,0:T(8,128)} %get-tuple-element.12), calls=%async_computation.4 | async-start | bytes 262144 | tf_op jit(solution)/shard_map/all_to_all | solution.py:40
  (6 other events, 113.6 us)

commit v6 on v5

--- a/solution.py
+++ b/solution.py
@@ -155,9 +155,25 @@
     branch = total * gain[...]
     wide = x[...].astype(F32)
     parts = [jnp.sum(u, axis=0, keepdims=True) for u in (total * total, wide * branch, branch * branch)]
-    stacked = jnp.concatenate(parts + [jnp.zeros((5, 256), F32)], axis=0)
+    halves = [p[:, k : k + 128] for p in parts for k in (0, 128)]
+    stacked = jnp.concatenate(halves + [jnp.zeros((2, 128), F32)], axis=0)
     for i in range(16):
         sums[i] = stacked
+
+
+def finish_kernel(sums, mixed, x, first, after, feed, residual, out):
+    part = sums[0]
+    for i in range(1, 16):
+        part = part + sums[i]
+    after_sq, cross_sum, branch_sq = [
+        jnp.concatenate([part[2 * k : 2 * k + 1], part[2 * k + 1 : 2 * k + 2]], axis=1) for k in range(3)
+    ]
+    scale = lax.rsqrt(after_sq / D + epsilon)
+    low = (x[...].astype(F32) + mixed[...] * scale * after[...]).astype(BF)
+    residual[...] = low
+    feed_sq = first[0:1] + 2.0 * scale * cross_sum + scale * scale * branch_sq
+    feed_scale = lax.rsqrt(feed_sq / D + epsilon)
+    out[...] = (low.astype(F32) * feed_scale * feed[...]).astype(BF)
 
 
 ANY = pl.BlockSpec(memory_space=pl.ANY)
@@ -266,7 +282,7 @@
         output_kernel,
         out_shape=(
             jax.ShapeDtypeStruct((288, rows), F32),
-            jax.ShapeDtypeStruct((16, 8, rows), F32),
+            jax.ShapeDtypeStruct((16, 8, 128), F32),
         ),
         in_specs=[VMEM] * 4,
         out_specs=(VMEM, VMEM),
@@ -274,15 +290,15 @@
         name="project_out",
     )(x_t, after_col, gathered, wo_rows)
 
-    sums = exchanged(sums, hid).sum(axis=0)
-    after_sq, cross_sum, branch_sq = sums[0:1], sums[1:2], sums[2:3]
-    first_sq = first[0:1]
-    after_scale = lax.rsqrt(after_sq / D + epsilon)
-    wide = x_t.astype(F32)
-    residual = (wide + mixed * after_scale * after_col).astype(BF)
-    feed_sq = first_sq + 2.0 * after_scale * cross_sum + after_scale * after_scale * branch_sq
-    feed_scale = lax.rsqrt(feed_sq / D + epsilon)
-    feed_input = (residual.astype(F32) * feed_scale * feed_col).astype(BF)
+    sums = exchanged(sums, hid)
+    residual, feed_input = pl.pallas_call(
+        finish_kernel,
+        out_shape=(jax.ShapeDtypeStruct((288, rows), BF), jax.ShapeDtypeStruct((288, rows), BF)),
+        in_specs=[VMEM] * 6,
+        out_specs=(VMEM, VMEM),
+        compiler_params=params(8),
+        name="finish",
+    )(sums, mixed, x_t, first, after_col, feed_col)
     return (residual.T, feed_input.T)
 
 

time: 192 us -> 192 us (level)
  no operation moved by 1% of the time
where the time goes in v6:
time: 192 us; the launch traced here: 191 us
  starting transfers between devices  103 us (54%)
  waiting for transfers between devices  45.8 us (24%)
  blocking collectives  21.8 us (11%)
  Pallas kernels  12.7 us (7%)
  local copies, waits for them, and re-layouts  5.08 us (3%)
    ppermute x8, starting transfers between devices, send(): lax.ppermute(x, ('z', 'c'), [(2 * a + b, 2 * d + e) for (a, b), (d, e) in...  44.8 us
    all_to_all x4, starting transfers between devices, exchanged(): return lax.all_to_all(x, axis, split_axis=0, concat_axis=0, tiled=True)  27.4 us
    all_to_all x1, blocking collectives, exchanged(): return lax.all_to_all(x, axis, split_axis=0, concat_axis=0, tiled=True)  21.8 us
    ppermute x1, waiting for transfers between devices, per_device(): w_pair = lax.ppermute(w, 'yl', ring(2, 1))  14.7 us
    ppermute x8, waiting for transfers between devices, send(): lax.ppermute(x, ('z', 'c'), [(2 * a + b, 2 * d + e) for (a, b), (d, e) in...  12.2 us
    all_to_all x4, waiting for transfers between devices, exchanged(): return lax.all_to_all(x, axis, split_axis=0, concat_axis=0, tiled=True)  8.83 us
    ppermute x4, starting transfers between devices, z_pieces(): near = [lax.ppermute(p, 'c', ring(2, 1)) for p in (one, two)]  8.66 us
    ppermute x4, starting transfers between devices, z_pieces(): far = [lax.ppermute(p, 'c', ring(2, 1)) for p in (three, four)]  8.49 us
  transfers between devices with their start and end apart: 25, of which 10 were waited for; matrix products, arithmetic and copies ran while one was open for 3% of the time, Pallas kernels for 1%

profile of v6, /device:TPU:1, one launch (start us, length us, event | category | flops | bytes accessed | tf_op | source)
XLA Modules:
  0.0 190.7 jit_solution(13553522526937762969)
XLA Ops:
  2.6 7.6 %all-to-all-start = ((bf16[4,296,256]{2,1,0:T(8,128)(2,1)}), bf16[4,296,256]{2,1,0:T(8,128)(2,1)S(1)}, u32[]{:S(2)}, u32[]{:S(2)}) async-start(bf16[4,296,256]{2,1,0:T(8,128)(2,1)} %get-tuple-element.10), calls=%async_computation | async-start | bytes 1212416 | tf_op jit(solution)/shard_map/all_to_all | solution.py:40
  10.2 2.3 %collective-permute-start = (bf16[144,512]{1,0:T(8,128)(2,1)}, bf16[144,512]{1,0:T(8,128)(2,1)S(1)}, u32[]{:S(2)}, u32[]{:S(2)}) collective-permute-start(bf16[144,512]{1,0:T(8,128)(2,1)} %get-tuple-element.12), channel_id=1, source_target_pairs={{0,16},{16,0},{1,17},{17,1},{2,18},{18,2},{3,19},{19,3},{4,20},{20... | collective-permute-start | bytes 442376 | tf_op jit(solution)/shard_map/ppermute | solution.py:217
  12.5 14.7 %collective-permute-done = bf16[144,512]{1,0:T(8,128)(2,1)S(1)} collective-permute-done((bf16[144,512]{1,0:T(8,128)(2,1)}, bf16[144,512]{1,0:T(8,128)(2,1)S(1)}, u32[]{:S(2)}, u32[]{:S(2)}) %collective-permute-start) | collective-permute-done | bytes 147488 | tf_op jit(solution)/shard_map/ppermute | solution.py:217
  28.1 3.4 %collective-permute-start.1 = (bf16[2,144,512]{2,1,0:T(8,128)(2,1)S(1)}, bf16[2,144,512]{2,1,0:T(8,128)(2,1)S(1)}, u32[]{:S(2)}, u32[]{:S(2)}) collective-permute-start(bf16[2,144,512]{2,1,0:T(8,128)(2,1)S(1)} %get-tuple-element.19), channel_id=1, source_target_pairs={{0,1},{1,0},{2,3},{3,2},{4,5},{5,4},{6,7},{7,6},{8,9},{9,8},{10,11... | collective-permute-start | bytes 884744 | tf_op jit(solution)/shard_map/ppermute | solution.py:23
  32.8 10.7 %collective-permute-start.3 = (bf16[2,2,144,512]{3,2,1,0:T(8,128)(2,1)S(1)}, bf16[2,2,144,512]{3,2,1,0:T(8,128)(2,1)}, u32[]{:S(2)}, u32[]{:S(2)}) collective-permute-start(bf16[2,2,144,512]{3,2,1,0:T(8,128)(2,1)S(1)} %pad_maximum_fusion.refs_0_), channel_id=1, source_target_pairs={{0,4},{1,13},{2,6},{3,15},{4,8},{5,1},{6,10},{7,3},{8,12},{9,5},{1... | collective-permute-start | bytes 1769480 | tf_op jit(solution)/shard_map/ppermute | solution.py:29
  45.1 4.1 %all-to-all-start.1 = ((bf16[4,4,296,256]{3,2,1,0:T(8,128)(2,1)}), bf16[4,4,296,256]{3,2,1,0:T(8,128)(2,1)S(1)}, u32[]{:S(2)}, u32[]{:S(2)}) async-start(bf16[4,4,296,256]{3,2,1,0:T(8,128)(2,1)} %broadcast_in_dim.24), calls=%async_computation.1 | async-start | bytes 4849664 | tf_op jit(solution)/shard_map/all_to_all | solution.py:40
  51.4 5.2 %collective-permute-done.3.refs_2_ = bf16[2,2,144,512]{3,2,1,0:T(8,128)(2,1)} collective-permute-done((bf16[2,2,144,512]{3,2,1,0:T(8,128)(2,1)S(1)}, bf16[2,2,144,512]{3,2,1,0:T(8,128)(2,1)}, u32[]{:S(2)}, u32[]{:S(2)}) %collective-permute-start.3) | collective-permute-done | bytes 589856 | tf_op jit(solution)/shard_map/ppermute | solution.py:29
  56.6 3.2 %collective-permute-start.4 = (bf16[2,2,144,512]{3,2,1,0:T(8,128)(2,1)}, bf16[2,2,144,512]{3,2,1,0:T(8,128)(2,1)}, u32[]{:S(2)}, u32[]{:S(2)}) collective-permute-start(bf16[2,2,144,512]{3,2,1,0:T(8,128)(2,1)} %collective-permute-done.3.refs_2_), channel_id=1, source_target_pairs={{0,2},{1,15},{2,4},{3,1},{4,6},{5,3},{6,8},{7,5},{8,10},{9,7},{10,... | collective-permute-start | bytes 1769480 | tf_op jit(solution)/shard_map/ppermute | solution.py:29
  61.5 4.8 %collective-permute-start.5 = (bf16[2,144,512]{2,1,0:T(8,128)(2,1)}, bf16[2,144,512]{2,1,0:T(8,128)(2,1)}, u32[]{:S(2)}, u32[]{:S(2)}) collective-permute-start(bf16[2,144,512]{2,1,0:T(8,128)(2,1)} %slice_bitcast_fusion), channel_id=1, source_target_pairs={{0,4},{1,13},{2,6},{3,15},{4,8},{5,1},{6,10},{7,3},{8,12},{9,5},{1... | collective-permute-start | bytes 884744 | tf_op jit(solution)/shard_map/ppermute | solution.py:29
  68.3 2.4 %collective-permute-start.6 = (bf16[2,2,144,512]{3,2,1,0:T(8,128)(2,1)}, bf16[2,2,144,512]{3,2,1,0:T(8,128)(2,1)}, u32[]{:S(2)}, u32[]{:S(2)}) collective-permute-start(bf16[2,2,144,512]{3,2,1,0:T(8,128)(2,1)} %collective-permute-done.2.refs_1_), channel_id=1, source_target_pairs={{0,1},{1,0},{2,3},{3,2},{4,5},{5,4},{6,7},{7,6},{8,9},{9,8},{10,11... | collective-permute-start | bytes 1769480 | tf_op jit(solution)/shard_map/ppermute | solution.py:34
  79.4 5.1 %attend.1 = bf16[4,256,256]{2,1,0:T(8,128)(2,1)S(1)} custom-call(s32[3]{0:T(128)S(1)} %pad_add_fusion.pos, bf16[256,4608]{1,0:T(8,128)(2,1)S(1)} %get-tuple-element.11.normed, f32[256,64]{1,0:T(8,128)S(1)} %get-tuple-element.23.cos, f32[256,64]{1,0:T(8,128)S(1)} %get-tuple-element.22.sin, f32[256,256]{1,0:T(8,128)S(1)} %fusion.1.mask, ...), custom_call_target="tpu_custom_call" | custom-call | tf_op jit(solution)/shard_map/attend/pallas_call | solution.py:254
  84.5 21.8 %all_to_all.25 = bf16[4,256,256]{2,1,0:T(8,128)(2,1)S(1)} all-to-all(bf16[4,256,256]{2,1,0:T(8,128)(2,1)S(1)} %attend.1), channel_id=1, replica_groups=mesh['hx'=4,'hy'=4,'yl'=2,'z'=8,'c'=2] {'hx'}, dimensions={0} | all-to-all | bytes 1048576 | tf_op jit(solution)/shard_map/all_to_all | solution.py:40
  107.9 4.6 %all-to-all-start.3 = ((bf16[4,4,256,256]{3,2,1,0:T(8,128)(2,1)}), bf16[4,4,256,256]{3,2,1,0:T(8,128)(2,1)}, u32[]{:S(2)}, u32[]{:S(2)}) async-start(bf16[4,4,256,256]{3,2,1,0:T(8,128)(2,1)} %broadcast_in_dim.25), calls=%async_computation.3 | async-start | bytes 4194304 | tf_op jit(solution)/shard_map/all_to_all | solution.py:40
  115.1 6.4 %collective-permute-done.11 = bf16[144,256]{1,0:T(8,128)(2,1)S(1)} collective-permute-done((bf16[144,256]{1,0:T(8,128)(2,1)S(1)}, bf16[144,256]{1,0:T(8,128)(2,1)S(1)}, u32[]{:S(2)}, u32[]{:S(2)}) %collective-permute-start.11) | collective-permute-done | bytes 73760 | tf_op jit(solution)/shard_map/ppermute | solution.py:241
  121.5 4.8 %collective-permute-start.12 = (bf16[2,144,256]{2,1,0:T(8,128)(2,1)S(1)}, bf16[2,144,256]{2,1,0:T(8,128)(2,1)S(1)}, u32[]{:S(2)}, u32[]{:S(2)}) collective-permute-start(bf16[2,144,256]{2,1,0:T(8,128)(2,1)S(1)} %get-tuple-element.21), channel_id=1, source_target_pairs={{0,1},{1,0},{2,3},{3,2},{4,5},{5,4},{6,7},{7,6},{8,9},{9,8},{10,11... | collective-permute-start | bytes 442376 | tf_op jit(solution)/shard_map/ppermute | solution.py:23
  127.4 14.2 %collective-permute-start.14 = (bf16[2,2,144,256]{3,2,1,0:T(8,128)(2,1)S(1)}, bf16[2,2,144,256]{3,2,1,0:T(8,128)(2,1)S(1)}, u32[]{:S(2)}, u32[]{:S(2)}) collective-permute-start(bf16[2,2,144,256]{3,2,1,0:T(8,128)(2,1)S(1)} %pad_maximum_fusion.2.refs_0_), channel_id=1, source_target_pairs={{0,4},{1,13},{2,6},{3,15},{4,8},{5,1},{6,10},{7,3},{8,12},{9,5},{1... | collective-permute-start | bytes 884744 | tf_op jit(solution)/shard_map/ppermute | solution.py:29
  143.5 4.9 %collective-permute-done.14.refs_2_ = bf16[2,2,144,256]{3,2,1,0:T(8,128)(2,1)S(1)} collective-permute-done((bf16[2,2,144,256]{3,2,1,0:T(8,128)(2,1)S(1)}, bf16[2,2,144,256]{3,2,1,0:T(8,128)(2,1)S(1)}, u32[]{:S(2)}, u32[]{:S(2)}) %collective-permute-start.14) | collective-permute-done | bytes 294944 | tf_op jit(solution)/shard_map/ppermute | solution.py:29
  148.4 2.5 %collective-permute-start.15 = (bf16[2,2,144,256]{3,2,1,0:T(8,128)(2,1)S(1)}, bf16[2,2,144,256]{3,2,1,0:T(8,128)(2,1)S(1)}, u32[]{:S(2)}, u32[]{:S(2)}) collective-permute-start(bf16[2,2,144,256]{3,2,1,0:T(8,128)(2,1)S(1)} %collective-permute-done.14.refs_2_), channel_id=1, source_target_pairs={{0,2},{1,15},{2,4},{3,1},{4,6},{5,3},{6,8},{7,5},{8,10},{9,7},{10,... | collective-permute-start | bytes 884744 | tf_op jit(solution)/shard_map/ppermute | solution.py:29
  150.9 5.4 %collective-permute-start.16 = (bf16[2,144,256]{2,1,0:T(8,128)(2,1)S(1)}, bf16[2,144,256]{2,1,0:T(8,128)(2,1)S(1)}, u32[]{:S(2)}, u32[]{:S(2)}) collective-permute-start(bf16[2,144,256]{2,1,0:T(8,128)(2,1)S(1)} %slice_bitcast_fusion.1), channel_id=1, source_target_pairs={{0,4},{1,13},{2,6},{3,15},{4,8},{5,1},{6,10},{7,3},{8,12},{9,5},{1... | collective-permute-start | bytes 442376 | tf_op jit(solution)/shard_map/ppermute | solution.py:29
  158.2 2.4 %collective-permute-start.18 = (bf16[2,2,144,256]{3,2,1,0:T(8,128)(2,1)S(1)}, bf16[2,2,144,256]{3,2,1,0:T(8,128)(2,1)S(1)}, u32[]{:S(2)}, u32[]{:S(2)}) collective-permute-start(bf16[2,2,144,256]{3,2,1,0:T(8,128)(2,1)S(1)} %collective-permute-done.14.refs_2_), channel_id=1, source_target_pairs={{0,1},{1,0},{2,3},{3,2},{4,5},{5,4},{6,7},{7,6},{8,9},{9,8},{10,11... | collective-permute-start | bytes 884744 | tf_op jit(solution)/shard_map/ppermute | solution.py:34
  162.6 2.4 %collective-permute-start.20 = (bf16[2,144,256]{2,1,0:T(8,128)(2,1)S(1)}, bf16[2,144,256]{2,1,0:T(8,128)(2,1)S(1)}, u32[]{:S(2)}, u32[]{:S(2)}) collective-permute-start(bf16[2,144,256]{2,1,0:T(8,128)(2,1)S(1)} %collective-permute-done.16.refs_4_), channel_id=1, source_target_pairs={{0,1},{1,0},{2,3},{3,2},{4,5},{5,4},{6,7},{7,6},{8,9},{9,8},{10,11... | collective-permute-start | bytes 442376 | tf_op jit(solution)/shard_map/ppermute | solution.py:35
  166.8 3.1 %project_out.1 = (f32[288,256]{1,0:T(8,128)S(1)}, f32[16,8,128]{2,1,0:T(8,128)}) custom-call(bf16[288,256]{1,0:T(8,128)(2,1)S(1)} %bitcast.22, f32[288,1]{1,0:T(8,128)S(1)} %reshape.24.gain.after, bf16[4,4,256,256]{3,2,1,0:T(8,128)(2,1)} %all-to-all-done.3.att, bf16[16,2,144,256]{3,2,1,0:T(8,128)(2,1)S(1)} %place.1.rows), custom_call_target="tpu_custom_call" | custom-call | tf_op jit(solution)/shard_map/project_out/pallas_call | solution.py:281
  169.9 11.1 %all-to-all-start.4 = ((f32[16,8,128]{2,1,0:T(8,128)}), f32[16,8,128]{2,1,0:T(8,128)S(1)}, u32[]{:S(2)}, u32[]{:S(2)}) async-start(f32[16,8,128]{2,1,0:T(8,128)} %get-tuple-element.13), calls=%async_computation.4 | async-start | bytes 131072 | tf_op jit(solution)/shard_map/all_to_all | solution.py:40
  181.1 8.8 %all-to-all-done.4.sums = f32[16,8,128]{2,1,0:T(8,128)S(1)} async-done(((f32[16,8,128]{2,1,0:T(8,128)}), f32[16,8,128]{2,1,0:T(8,128)S(1)}, u32[]{:S(2)}, u32[]{:S(2)}) %all-to-all-start.4) | async-done | bytes 65568 | tf_op jit(solution)/shard_map/all_to_all | solution.py:40
  (58 shorter events, 33.8 us)
Async XLA Ops:
  2.6 40.9 %all-to-all-start = ((bf16[4,296,256]{2,1,0:T(8,128)(2,1)}), bf16[4,296,256]{2,1,0:T(8,128)(2,1)S(1)}, u32[]{:S(2)}, u32[]{:S(2)}) async-start(bf16[4,296,256]{2,1,0:T(8,128)(2,1)} %get-tuple-element.10), calls=%async_computation | async-start | bytes 1212416 | tf_op jit(solution)/shard_map/all_to_all | solution.py:40
  10.2 17.0 %collective-permute-start = (bf16[144,512]{1,0:T(8,128)(2,1)}, bf16[144,512]{1,0:T(8,128)(2,1)S(1)}, u32[]{:S(2)}, u32[]{:S(2)}) collective-permute-start(bf16[144,512]{1,0:T(8,128)(2,1)} %get-tuple-element.12), channel_id=1, source_target_pairs={{0,16},{16,0},{1,17},{17,1},{2,18},{18,2},{3,19},{19,3},{4,20},{20... | collective-permute-start | bytes 442376 | tf_op jit(solution)/shard_map/ppermute | solution.py:217
  28.1 4.6 %collective-permute-start.1 = (bf16[2,144,512]{2,1,0:T(8,128)(2,1)S(1)}, bf16[2,144,512]{2,1,0:T(8,128)(2,1)S(1)}, u32[]{:S(2)}, u32[]{:S(2)}) collective-permute-start(bf16[2,144,512]{2,1,0:T(8,128)(2,1)S(1)} %get-tuple-element.19), channel_id=1, source_target_pairs={{0,1},{1,0},{2,3},{3,2},{4,5},{5,4},{6,7},{7,6},{8,9},{9,8},{10,11... | collective-permute-start | bytes 884744 | tf_op jit(solution)/shard_map/ppermute | solution.py:23
  32.8 23.8 %collective-permute-start.3 = (bf16[2,2,144,512]{3,2,1,0:T(8,128)(2,1)S(1)}, bf16[2,2,144,512]{3,2,1,0:T(8,128)(2,1)}, u32[]{:S(2)}, u32[]{:S(2)}) collective-permute-start(bf16[2,2,144,512]{3,2,1,0:T(8,128)(2,1)S(1)} %pad_maximum_fusion.refs_0_), channel_id=1, source_target_pairs={{0,4},{1,13},{2,6},{3,15},{4,8},{5,1},{6,10},{7,3},{8,12},{9,5},{1... | collective-permute-start | bytes 1769480 | tf_op jit(solution)/shard_map/ppermute | solution.py:29
  45.1 32.7 %all-to-all-start.1 = ((bf16[4,4,296,256]{3,2,1,0:T(8,128)(2,1)}), bf16[4,4,296,256]{3,2,1,0:T(8,128)(2,1)S(1)}, u32[]{:S(2)}, u32[]{:S(2)}) async-start(bf16[4,4,296,256]{3,2,1,0:T(8,128)(2,1)} %broadcast_in_dim.24), calls=%async_computation.1 | async-start | bytes 4849664 | tf_op jit(solution)/shard_map/all_to_all | solution.py:40
  49.2 19.1 %collective-permute-start.2 = (bf16[2,2,144,512]{3,2,1,0:T(8,128)(2,1)S(1)}, bf16[2,2,144,512]{3,2,1,0:T(8,128)(2,1)}, u32[]{:S(2)}, u32[]{:S(2)}) collective-permute-start(bf16[2,2,144,512]{3,2,1,0:T(8,128)(2,1)S(1)} %pad_maximum_fusion.refs_0_), channel_id=1, source_target_pairs={{0,2},{1,15},{2,4},{3,1},{4,6},{5,3},{6,8},{7,5},{8,10},{9,7},{10,... | collective-permute-start | bytes 1769480 | tf_op jit(solution)/shard_map/ppermute | solution.py:29
  56.6 14.1 %collective-permute-start.4 = (bf16[2,2,144,512]{3,2,1,0:T(8,128)(2,1)}, bf16[2,2,144,512]{3,2,1,0:T(8,128)(2,1)}, u32[]{:S(2)}, u32[]{:S(2)}) collective-permute-start(bf16[2,2,144,512]{3,2,1,0:T(8,128)(2,1)} %collective-permute-done.3.refs_2_), channel_id=1, source_target_pairs={{0,2},{1,15},{2,4},{3,1},{4,6},{5,3},{6,8},{7,5},{8,10},{9,7},{10,... | collective-permute-start | bytes 1769480 | tf_op jit(solution)/shard_map/ppermute | solution.py:29
  61.5 14.1 %collective-permute-start.5 = (bf16[2,144,512]{2,1,0:T(8,128)(2,1)}, bf16[2,144,512]{2,1,0:T(8,128)(2,1)}, u32[]{:S(2)}, u32[]{:S(2)}) collective-permute-start(bf16[2,144,512]{2,1,0:T(8,128)(2,1)} %slice_bitcast_fusion), channel_id=1, source_target_pairs={{0,4},{1,13},{2,6},{3,15},{4,8},{5,1},{6,10},{7,3},{8,12},{9,5},{1... | collective-permute-start | bytes 884744 | tf_op jit(solution)/shard_map/ppermute | solution.py:29
  66.3 12.5 %collective-permute-start.7 = (bf16[2,2,144,512]{3,2,1,0:T(8,128)(2,1)}, bf16[2,2,144,512]{3,2,1,0:T(8,128)(2,1)}, u32[]{:S(2)}, u32[]{:S(2)}) collective-permute-start(bf16[2,2,144,512]{3,2,1,0:T(8,128)(2,1)} %collective-permute-done.3.refs_2_), channel_id=1, source_target_pairs={{0,1},{1,0},{2,3},{3,2},{4,5},{5,4},{6,7},{7,6},{8,9},{9,8},{10,11... | collective-permute-start | bytes 1769480 | tf_op jit(solution)/shard_map/ppermute | solution.py:34
  68.3 10.5 %collective-permute-start.6 = (bf16[2,2,144,512]{3,2,1,0:T(8,128)(2,1)}, bf16[2,2,144,512]{3,2,1,0:T(8,128)(2,1)}, u32[]{:S(2)}, u32[]{:S(2)}) collective-permute-start(bf16[2,2,144,512]{3,2,1,0:T(8,128)(2,1)} %collective-permute-done.2.refs_1_), channel_id=1, source_target_pairs={{0,1},{1,0},{2,3},{3,2},{4,5},{5,4},{6,7},{7,6},{8,9},{9,8},{10,11... | collective-permute-start | bytes 1769480 | tf_op jit(solution)/shard_map/ppermute | solution.py:34
  70.7 8.7 %collective-permute-start.8 = (bf16[2,2,144,512]{3,2,1,0:T(8,128)(2,1)}, bf16[2,2,144,512]{3,2,1,0:T(8,128)(2,1)}, u32[]{:S(2)}, u32[]{:S(2)}) collective-permute-start(bf16[2,2,144,512]{3,2,1,0:T(8,128)(2,1)} %collective-permute-done.4.refs_3_), channel_id=1, source_target_pairs={{0,1},{1,0},{2,3},{3,2},{4,5},{5,4},{6,7},{7,6},{8,9},{9,8},{10,11... | collective-permute-start | bytes 1769480 | tf_op jit(solution)/shard_map/ppermute | solution.py:35
  75.6 3.8 %collective-permute-start.9 = (bf16[2,144,512]{2,1,0:T(8,128)(2,1)}, bf16[2,144,512]{2,1,0:T(8,128)(2,1)}, u32[]{:S(2)}, u32[]{:S(2)}) collective-permute-start(bf16[2,144,512]{2,1,0:T(8,128)(2,1)} %collective-permute-done.5.refs_4_), channel_id=1, source_target_pairs={{0,1},{1,0},{2,3},{3,2},{4,5},{5,4},{6,7},{7,6},{8,9},{9,8},{10,11... | collective-permute-start | bytes 884744 | tf_op jit(solution)/shard_map/ppermute | solution.py:35
  107.9 58.9 %all-to-all-start.3 = ((bf16[4,4,256,256]{3,2,1,0:T(8,128)(2,1)}), bf16[4,4,256,256]{3,2,1,0:T(8,128)(2,1)}, u32[]{:S(2)}, u32[]{:S(2)}) async-start(bf16[4,4,256,256]{3,2,1,0:T(8,128)(2,1)} %broadcast_in_dim.25), calls=%async_computation.3 | async-start | bytes 4194304 | tf_op jit(solution)/shard_map/all_to_all | solution.py:40
  112.5 9.0 %collective-permute-start.11 = (bf16[144,256]{1,0:T(8,128)(2,1)S(1)}, bf16[144,256]{1,0:T(8,128)(2,1)S(1)}, u32[]{:S(2)}, u32[]{:S(2)}) collective-permute-start(bf16[144,256]{1,0:T(8,128)(2,1)S(1)} %bitcast.32), channel_id=1, source_target_pairs={{0,16},{1,17},{2,48},{3,49},{4,80},{5,81},{6,112},{7,113},{8,144},... | collective-permute-start | bytes 221192 | tf_op jit(solution)/shard_map/ppermute | solution.py:241
  114.4 7.1 %collective-permute-start.10 = (bf16[144,256]{1,0:T(8,128)(2,1)S(1)}, bf16[144,256]{1,0:T(8,128)(2,1)S(1)}, u32[]{:S(2)}, u32[]{:S(2)}) collective-permute-start(bf16[144,256]{1,0:T(8,128)(2,1)S(1)} %bitcast.33), channel_id=1, source_target_pairs={{0,0},{1,1},{2,32},{3,33},{4,64},{5,65},{6,96},{7,97},{8,128},{9,1... | collective-permute-start | bytes 221192 | tf_op jit(solution)/shard_map/ppermute | solution.py:241
  121.5 5.8 %collective-permute-start.12 = (bf16[2,144,256]{2,1,0:T(8,128)(2,1)S(1)}, bf16[2,144,256]{2,1,0:T(8,128)(2,1)S(1)}, u32[]{:S(2)}, u32[]{:S(2)}) collective-permute-start(bf16[2,144,256]{2,1,0:T(8,128)(2,1)S(1)} %get-tuple-element.21), channel_id=1, source_target_pairs={{0,1},{1,0},{2,3},{3,2},{4,5},{5,4},{6,7},{7,6},{8,9},{9,8},{10,11... | collective-permute-start | bytes 442376 | tf_op jit(solution)/shard_map/ppermute | solution.py:23
  127.4 21.0 %collective-permute-start.14 = (bf16[2,2,144,256]{3,2,1,0:T(8,128)(2,1)S(1)}, bf16[2,2,144,256]{3,2,1,0:T(8,128)(2,1)S(1)}, u32[]{:S(2)}, u32[]{:S(2)}) collective-permute-start(bf16[2,2,144,256]{3,2,1,0:T(8,128)(2,1)S(1)} %pad_maximum_fusion.2.refs_0_), channel_id=1, source_target_pairs={{0,4},{1,13},{2,6},{3,15},{4,8},{5,1},{6,10},{7,3},{8,12},{9,5},{1... | collective-permute-start | bytes 884744 | tf_op jit(solution)/shard_map/ppermute | solution.py:29
  141.5 14.8 %collective-permute-start.13 = (bf16[2,2,144,256]{3,2,1,0:T(8,128)(2,1)S(1)}, bf16[2,2,144,256]{3,2,1,0:T(8,128)(2,1)S(1)}, u32[]{:S(2)}, u32[]{:S(2)}) collective-permute-start(bf16[2,2,144,256]{3,2,1,0:T(8,128)(2,1)S(1)} %pad_maximum_fusion.2.refs_0_), channel_id=1, source_target_pairs={{0,2},{1,15},{2,4},{3,1},{4,6},{5,3},{6,8},{7,5},{8,10},{9,7},{10,... | collective-permute-start | bytes 884744 | tf_op jit(solution)/shard_map/ppermute | solution.py:29
  148.4 12.3 %collective-permute-start.15 = (bf16[2,2,144,256]{3,2,1,0:T(8,128)(2,1)S(1)}, bf16[2,2,144,256]{3,2,1,0:T(8,128)(2,1)S(1)}, u32[]{:S(2)}, u32[]{:S(2)}) collective-permute-start(bf16[2,2,144,256]{3,2,1,0:T(8,128)(2,1)S(1)} %collective-permute-done.14.refs_2_), channel_id=1, source_target_pairs={{0,2},{1,15},{2,4},{3,1},{4,6},{5,3},{6,8},{7,5},{8,10},{9,7},{10,... | collective-permute-start | bytes 884744 | tf_op jit(solution)/shard_map/ppermute | solution.py:29
  150.9 11.7 %collective-permute-start.16 = (bf16[2,144,256]{2,1,0:T(8,128)(2,1)S(1)}, bf16[2,144,256]{2,1,0:T(8,128)(2,1)S(1)}, u32[]{:S(2)}, u32[]{:S(2)}) collective-permute-start(bf16[2,144,256]{2,1,0:T(8,128)(2,1)S(1)} %slice_bitcast_fusion.1), channel_id=1, source_target_pairs={{0,4},{1,13},{2,6},{3,15},{4,8},{5,1},{6,10},{7,3},{8,12},{9,5},{1... | collective-permute-start | bytes 442376 | tf_op jit(solution)/shard_map/ppermute | solution.py:29
  156.3 8.8 %collective-permute-start.17 = (bf16[2,2,144,256]{3,2,1,0:T(8,128)(2,1)S(1)}, bf16[2,2,144,256]{3,2,1,0:T(8,128)(2,1)S(1)}, u32[]{:S(2)}, u32[]{:S(2)}) collective-permute-start(bf16[2,2,144,256]{3,2,1,0:T(8,128)(2,1)S(1)} %collective-permute-done.13.refs_1_), channel_id=1, source_target_pairs={{0,1},{1,0},{2,3},{3,2},{4,5},{5,4},{6,7},{7,6},{8,9},{9,8},{10,11... | collective-permute-start | bytes 884744 | tf_op jit(solution)/shard_map/ppermute | solution.py:34
  158.2 6.9 %collective-permute-start.18 = (bf16[2,2,144,256]{3,2,1,0:T(8,128)(2,1)S(1)}, bf16[2,2,144,256]{3,2,1,0:T(8,128)(2,1)S(1)}, u32[]{:S(2)}, u32[]{:S(2)}) collective-permute-start(bf16[2,2,144,256]{3,2,1,0:T(8,128)(2,1)S(1)} %collective-permute-done.14.refs_2_), channel_id=1, source_target_pairs={{0,1},{1,0},{2,3},{3,2},{4,5},{5,4},{6,7},{7,6},{8,9},{9,8},{10,11... | collective-permute-start | bytes 884744 | tf_op jit(solution)/shard_map/ppermute | solution.py:34
  160.7 5.3 %collective-permute-start.19 = (bf16[2,2,144,256]{3,2,1,0:T(8,128)(2,1)S(1)}, bf16[2,2,144,256]{3,2,1,0:T(8,128)(2,1)S(1)}, u32[]{:S(2)}, u32[]{:S(2)}) collective-permute-start(bf16[2,2,144,256]{3,2,1,0:T(8,128)(2,1)S(1)} %collective-permute-done.15.refs_3_), channel_id=1, source_target_pairs={{0,1},{1,0},{2,3},{3,2},{4,5},{5,4},{6,7},{7,6},{8,9},{9,8},{10,11... | collective-permute-start | bytes 884744 | tf_op jit(solution)/shard_map/ppermute | solution.py:35
  169.9 20.0 %all-to-all-start.4 = ((f32[16,8,128]{2,1,0:T(8,128)}), f32[16,8,128]{2,1,0:T(8,128)S(1)}, u32[]{:S(2)}, u32[]{:S(2)}) async-start(f32[16,8,128]{2,1,0:T(8,128)} %get-tuple-element.13), calls=%async_computation.4 | async-start | bytes 131072 | tf_op jit(solution)/shard_map/all_to_all | solution.py:40
  (6 other events, 113.6 us)
